TPU v7x, 32 devices: a whole 2x2x4 slice. The times are simulated.
32 devices in a mesh: seq: 16 (over z, y, x), rep: 2 (over core).
Axes of the slice: x: 2, y: 2, z: 4, core: 2. Of those that a mesh axis runs over, the one named last changes fastest.
Arguments:
- queries: bfloat16 [4096, 4096], P(('rep', 'seq')), parts along dimension 0, may hold values from -160 to 160
- keys_values: bfloat16 [2, 4096, 1024], P(None, ('rep', 'seq')), parts along dimension 1, may hold values from -6 to 6
- segment_ids: int32 [4096], P(('rep', 'seq')), parts along dimension 0, may hold values from 0 to 31, never falling along the last dimension, each value on 1 to 1024 neighbouring positions
Outputs:
- attended: bfloat16 [4096, 4096], P(('rep', 'seq')), parts along dimension 0
There are 2 independent parts, one for each index of `rep`. A program takes and returns all parts, laid end to end along the dimension named above; each array names one. Nothing has to cross between parts.
Inputs may be any that keep to these rules, and one draw needn't show every extreme that they name: `segment_ids`: ids never fall along the tokens; every document holds 1 to 1024 consecutive tokens, one exactly 1024.
All inputs are finite; a program needn't handle non-finite values.
Results may differ from a plain program's by a relative error of at most 0.004.
Values may be sent and summed in bfloat16 or wider, within the bound.
No kernel may reach another device: no remote copies, remote signals or barrier semaphores. Data moves between devices by JAX's collectives and lax.ppermute only.
A program may use at most 192 MiB of HBM per device.

v0:
```python
import functools
import jax
import jax.numpy as jnp
from jax import lax
from jax.experimental import pallas as pl
from jax.experimental.pallas import tpu as pltpu
from jax.sharding import PartitionSpec as P

HQ = 32
HK = 8
DH = 128
WINDOW = 2048

GROUP = HQ // HK
NEG_BIG = -1e30
LOG2E = 1.4426950408889634
ID_ROWS = 16


def pack_kv(place, kv, ids, *outs, size, chunks):
    rows = kv.shape[1]
    tag = jnp.broadcast_to(ids[...].astype(jnp.float32), (ID_ROWS, rows)).astype(jnp.bfloat16)
    for k in range(size):
        for c in range(chunks):
            start = pl.multiple_of(((place[0] ^ k) * chunks + c) * DH, DH)
            for part in range(2):
                first = (2 * c + part) * rows
                outs[k][first : first + rows, :] = kv[part, :, pl.ds(start, DH)]
        outs[k][2 * chunks * rows :, :] = tag


def pack_q(place, q, *outs, size):
    width = outs[0].shape[1]
    for k in range(size):
        start = pl.multiple_of((place[0] ^ k) * width, width)
        outs[k][...] = q[:, pl.ds(start, width)]


def join(*refs, count, chunks, rows):
    outs = refs[count:]
    for n in range(count):
        for c in range(chunks):
            outs[c][2 * n * rows : 2 * (n + 1) * rows, :] = refs[n][2 * c * rows : 2 * (c + 1) * rows, :]
        outs[0][2 * count * rows + n * ID_ROWS : 2 * count * rows + (n + 1) * ID_ROWS, :] = refs[n][
            2 * chunks * rows :, :
        ]


def unpack(place, *refs, size, chunks):
    out = refs[-1]
    width = refs[0].shape[1]
    for c in range(chunks):
        for k in range(size):
            start = pl.multiple_of(((place[0] ^ k) * chunks + c) * width, width)
            out[:, pl.ds(start, width)] = refs[c * size + k][...]


def attend(place, *refs, chunk, size, chunks, rows, steps, first, last):
    q_refs, near, refs = refs[:size], refs[size : 2 * size], refs[2 * size :]
    far = {}
    for d in steps:
        if d:
            count = 3 if chunk else 2
            own, rest, tags = refs[0], refs[1], refs[count - 1]
            far[d] = (own, rest, tags)
            refs = refs[count:]
    if not first:
        old_top_ref, old_sum_ref, old_acc_ref = refs[:3]
        refs = refs[3:]
    if last:
        outs, refs = refs[:size], refs[size:]
    else:
        top_ref, sum_ref, acc_ref = refs[:3]
        refs = refs[3:]
    k_buf, v_buf, bias, s_buf = refs
    keys = k_buf.shape[0]
    wide = GROUP * rows
    tile = min(256, keys)
    member, block = place[0], place[1]
    tag_at = 2 * chunks * rows
    tag_rows = []
    for x, d in enumerate(steps):
        for k in range(size):
            n = x * size + k
            if d == 0 or k == 0:
                ref = near[k] if d == 0 else far[d][0]
                start, tag_ref, tag_row = 2 * chunk * rows, ref, tag_at
            else:
                ref, tag_ref = far[d][1], far[d][2]
                start, tag_row = 2 * (k - 1) * rows, 2 * (size - 1) * rows + (k - 1) * ID_ROWS
            k_buf[n * rows : (n + 1) * rows, :] = ref[start : start + rows, :]
            v_buf[n * rows : (n + 1) * rows, :] = ref[start + rows : start + 2 * rows, :]
            tag = tag_ref[tag_row : tag_row + 1, :].astype(jnp.float32)
            tag_rows.append(tag if d == 0 else jnp.where(block >= d, tag, -1.0))
    ahead = lax.broadcasted_iota(jnp.int32, (rows, rows), 0) - lax.broadcasted_iota(jnp.int32, (rows, rows), 1)
    scale = DH**-0.5 * LOG2E
    for i in range(size):
        tag_row = near[i][tag_at : tag_at + 1, :].astype(jnp.float32)
        q_tag = jnp.broadcast_to(tag_row, (rows, rows)).T
        for n, k_tag in enumerate(tag_rows):
            d = steps[n // size]
            distance = ahead + (d * size + (member ^ i) - (member ^ (n % size))) * rows
            allowed = q_tag == jnp.broadcast_to(k_tag, (rows, rows))
            if d == 0:
                allowed = allowed & (distance >= 0)
            if (d * size + size) * rows > WINDOW:
                allowed = allowed & (distance < WINDOW)
            bias[i % 2, :, n * rows : (n + 1) * rows] = jnp.where(allowed, 0.0, NEG_BIG)
        at = chunk * GROUP * DH
        q4 = jnp.concatenate([q_refs[i][:, at + h * DH : at + (h + 1) * DH] for h in range(GROUP)], axis=0)
        top = None
        for t in range(0, keys, tile):
            s = lax.dot_general(
                q4, k_buf[t : t + tile, :], (((1,), (1,)), ((), ())), preferred_element_type=jnp.float32
            )
            b = bias[i % 2, :, t : t + tile]
            s = s + jnp.concatenate([b] * GROUP, axis=0)
            s_buf[i % 2, :, t : t + tile] = s
            for u in range(0, tile, DH):
                part = s[:, u : u + DH]
                top = part if top is None else jnp.maximum(top, part)
        top = jnp.broadcast_to(jnp.max(top, axis=1, keepdims=True), (wide, DH))
        if not first:
            old_top = old_top_ref[i]
            top = jnp.maximum(top, old_top)
        total = acc = None
        for t in range(0, keys, tile):
            w = []
            for u in range(t, t + tile, DH):
                part = jnp.exp2((s_buf[i % 2, :, u : u + DH] - top) * scale)
                total = part if total is None else total + part
                w.append(part.astype(jnp.bfloat16))
            add = lax.dot_general(
                jnp.concatenate(w, axis=1),
                v_buf[t : t + tile, :],
                (((1,), (0,)), ((), ())),
                preferred_element_type=jnp.float32,
            )
            acc = add if acc is None else acc + add
        total = jnp.broadcast_to(jnp.sum(total, axis=1, keepdims=True), (wide, DH))
        if not first:
            rescale = jnp.exp2((old_top - top) * scale)
            total = total + old_sum_ref[i] * rescale
            acc = acc + old_acc_ref[i] * rescale
        if last:
            result = (acc / total).astype(jnp.bfloat16)
            for h in range(GROUP):
                outs[i][:, h * DH : (h + 1) * DH] = result[h * rows : (h + 1) * rows, :]
        else:
            top_ref[i] = top
            sum_ref[i] = total
            acc_ref[i] = acc


def layout_of(shards, rows):
    size = 1
    while (2 * size) ** 2 <= shards and 2 * size <= HK:
        size *= 2
    reach = min(WINDOW, rows * shards // 2)
    back = min(-(-(reach - 1) // (size * rows)), shards // size - 1)
    return size, HK // size, back


def local(queries, keys_values, segment_ids, shards):
    rows = queries.shape[0]
    size, chunks, back = layout_of(shards, rows)
    width = GROUP * DH
    me = lax.axis_index("seq")
    place = jnp.stack([me & (size - 1), me >> (size.bit_length() - 1)]).astype(jnp.int32)
    smem = pl.BlockSpec(memory_space=pltpu.SMEM)
    vmem = pl.BlockSpec(memory_space=pltpu.VMEM)
    params = pltpu.CompilerParams(vmem_limit_bytes=48 * 1024 * 1024)
    bf16 = functools.partial(jax.ShapeDtypeStruct, dtype=jnp.bfloat16)
    f32 = functools.partial(jax.ShapeDtypeStruct, dtype=jnp.float32)

    def call(body, shapes, args, scratch=()):
        return pl.pallas_call(
            body,
            in_specs=[smem if a is place else vmem for a in args],
            out_specs=[vmem] * len(shapes),
            out_shape=shapes,
            scratch_shapes=scratch,
            compiler_params=params,
        )(*args)

    def swap(x, k):
        return lax.ppermute(x, "seq", [(i, i ^ k) for i in range(shards)]) if k else x

    def onward(x):
        return lax.ppermute(x, "seq", [(i, i + size) for i in range(shards - size)])

    sent = call(
        functools.partial(pack_kv, size=size, chunks=chunks),
        [bf16((2 * chunks * rows + ID_ROWS, DH))] * size,
        [place, keys_values, segment_ids.reshape(1, rows)],
    )
    near = [swap(sent[k], k) for k in range(size)]
    q_sent = call(functools.partial(pack_q, size=size), [bf16((rows, chunks * width))] * size, [place, queries])
    q_parts = [swap(q_sent[k], k) for k in range(size)]
    count = size - 1
    rest_shapes = [bf16((count * (2 * rows + (0 if c else ID_ROWS)), DH)) for c in range(chunks)]
    far_own, far_rest = [sent[0]], []
    if back:
        far_rest.append(call(functools.partial(join, count=count, chunks=chunks, rows=rows), rest_shapes, near[1:]))
    for d in range(1, back + 1):
        far_own.append(onward(far_own[d - 1]))
        far_rest.append([onward(far_rest[d - 1][c]) for c in range(chunks)])

    def stage(c, steps, state, first, last):
        keys = len(steps) * size * rows
        args = [place] + q_parts + near
        for d in steps:
            if d:
                args += [far_own[d], far_rest[d][c]] + ([far_rest[d][0]] if c else [])
        args += list(state)
        shapes = [bf16((rows, width))] * size if last else [f32((size, GROUP * rows, DH))] * 3
        scratch = [
            pltpu.VMEM((keys, DH), jnp.bfloat16),
            pltpu.VMEM((keys, DH), jnp.bfloat16),
            pltpu.VMEM((2, rows, keys), jnp.float32),
            pltpu.VMEM((2, GROUP * rows, keys), jnp.float32),
        ]
        body = functools.partial(
            attend, chunk=c, size=size, chunks=chunks, rows=rows, steps=steps, first=first, last=last
        )
        return call(body, shapes, args, scratch)

    states = [()] * chunks
    if back:
        states = [stage(c, tuple(range(back)), (), True, False) for c in range(chunks)]
    done = []
    for c in range(chunks):
        result = stage(c, (back,), states[c], not back, True)
        done += [swap(result[k], k) for k in range(size)]
    return call(functools.partial(unpack, size=size, chunks=chunks), [bf16(queries.shape)], [place] + done)[0]


def solution(mesh):
    shards = mesh.shape["seq"]

    def body(queries, keys_values, segment_ids):
        return local(queries, keys_values, segment_ids, shards)

    return jax.shard_map(
        body,
        mesh=mesh,
        in_specs=(P(("rep", "seq"), None), P(None, ("rep", "seq"), None), P(("rep", "seq"))),
        out_specs=P(("rep", "seq"), None),
        check_vma=False,
    )
```

profile of v0, /device:TPU:0, one launch (start us, length us, event | category | flops | bytes accessed | tf_op | source)
XLA Modules:
  0.0 65.8 jit_solution(3973546023471424148)
XLA Ops:
  0.0 0.1 pad_add_fusion.place
  0.1 0.7 copy-done.2
  0.7 1.0 %copy-done.1 = bf16[2,128,1024]{2,1,0:T(8,128)(2,1)S(1)} copy-done((bf16[2,128,1024]{2,1,0:T(8,128)(2,1)S(1)}, bf16[2,128,1024]{2,1,0:T(8,128)(2,1)}, u32[]{:S(2)}) %copy-start.1) | copy-done | bytes 524312
  1.8 0.7 %shard_map.38 = (bf16[528,128]{1,0:T(8,128)(2,1)S(1)}, bf16[528,128]{1,0:T(8,128)(2,1)S(1)}, bf16[528,128]{1,0:T(8,128)(2,1)S(1)}, bf16[528,128]{1,0:T(8,128)(2,1)S(1)}) custom-call(s32[2]{0:T(128)S(1)} %pad_add_fusion.place, bf16[2,128,1024]{2,1,0:T(8,128)(2,1)S(1)} %copy-done.1, s32[1,128]{1,0:T(1,128)S(1)} %bitcast.3), custom_call_target="tpu_custom_call" | custom-call | tf_op jit(solution)/shard_map/pallas_call | solution.py:177
  2.5 3.0 %collective-permute-start.3 = (bf16[528,128]{1,0:T(8,128)(2,1)S(1)}, bf16[528,128]{1,0:T(8,128)(2,1)S(1)}, u32[]{:S(2)}, u32[]{:S(2)}) collective-permute-start(bf16[528,128]{1,0:T(8,128)(2,1)S(1)} %get-tuple-element.34), channel_id=1, source_target_pairs={{0,2},{2,0},{4,6},{6,4},{8,10},{10,8},{12,14},{14,12},{16,18},{18,... | collective-permute-start | bytes 405512 | tf_op jit(solution)/shard_map/ppermute | solution.py:187
  5.5 1.5 %collective-permute-start.4 = (bf16[528,128]{1,0:T(8,128)(2,1)S(1)}, bf16[528,128]{1,0:T(8,128)(2,1)S(1)}, u32[]{:S(2)}, u32[]{:S(2)}) collective-permute-start(bf16[528,128]{1,0:T(8,128)(2,1)S(1)} %get-tuple-element.35), channel_id=1, source_target_pairs={{0,4},{2,6},{4,0},{6,2},{8,12},{10,14},{12,8},{14,10},{16,20},{18,... | collective-permute-start | bytes 405512 | tf_op jit(solution)/shard_map/ppermute | solution.py:187
  7.0 0.0 collective-permute-start.5
  7.0 2.4 %collective-permute-done.3.refs_0_.refs_5_ = bf16[528,128]{1,0:T(8,128)(2,1)S(1)} collective-permute-done((bf16[528,128]{1,0:T(8,128)(2,1)S(1)}, bf16[528,128]{1,0:T(8,128)(2,1)S(1)}, u32[]{:S(2)}, u32[]{:S(2)}) %collective-permute-start.3) | collective-permute-done | bytes 135200 | tf_op jit(solution)/shard_map/ppermute | solution.py:187
  9.5 4.0 %collective-permute-done.4.refs_1_.refs_6_ = bf16[528,128]{1,0:T(8,128)(2,1)S(1)} collective-permute-done((bf16[528,128]{1,0:T(8,128)(2,1)S(1)}, bf16[528,128]{1,0:T(8,128)(2,1)S(1)}, u32[]{:S(2)}, u32[]{:S(2)}) %collective-permute-start.4) | collective-permute-done | bytes 135200 | tf_op jit(solution)/shard_map/ppermute | solution.py:187
  13.4 0.0 collective-permute-done.5.refs_2_.refs_7_
  13.5 3.5 %collective-permute-start.8 = (bf16[816,128]{1,0:T(8,128)(2,1)S(1)}, bf16[816,128]{1,0:T(8,128)(2,1)S(1)}, u32[]{:S(2)}, u32[]{:S(2)}) collective-permute-start(bf16[816,128]{1,0:T(8,128)(2,1)S(1)} %get-tuple-element.37), channel_id=1, source_target_pairs={{0,8},{2,10},{4,12},{6,14},{8,16},{10,18},{12,20},{14,22},{16,24},... | collective-permute-start | bytes 626696 | tf_op jit(solution)/shard_map/ppermute | solution.py:190
  17.0 3.5 %collective-permute-start.6 = (bf16[528,128]{1,0:T(8,128)(2,1)S(1)}, bf16[528,128]{1,0:T(8,128)(2,1)S(1)}, u32[]{:S(2)}, u32[]{:S(2)}) collective-permute-start(bf16[528,128]{1,0:T(8,128)(2,1)S(1)} %get-tuple-element.33.refs_4_), channel_id=1, source_target_pairs={{0,8},{2,10},{4,12},{6,14},{8,16},{10,18},{12,20},{14,22},{16,24},... | collective-permute-start | bytes 405512 | tf_op jit(solution)/shard_map/ppermute | solution.py:190
  20.5 0.0 copy-start
  20.5 1.2 %copy-done = bf16[128,4096]{1,0:T(8,128)(2,1)S(1)} copy-done((bf16[128,4096]{1,0:T(8,128)(2,1)S(1)}, bf16[128,4096]{1,0:T(8,128)(2,1)}, u32[]{:S(2)}) %copy-start) | copy-done | bytes 1048600
  21.7 0.6 shard_map.37
  22.3 1.3 %collective-permute-start = (bf16[128,1024]{1,0:T(8,128)(2,1)S(1)}, bf16[128,1024]{1,0:T(8,128)(2,1)S(1)}, u32[]{:S(2)}, u32[]{:S(2)}) collective-permute-start(bf16[128,1024]{1,0:T(8,128)(2,1)S(1)} %get-tuple-element.30), channel_id=1, source_target_pairs={{0,2},{2,0},{4,6},{6,4},{8,10},{10,8},{12,14},{14,12},{16,18},{18,... | collective-permute-start | bytes 786440 | tf_op jit(solution)/shard_map/ppermute | solution.py:187
  23.6 3.5 %collective-permute-start.13 = (bf16[768,128]{1,0:T(8,128)(2,1)S(1)}, bf16[768,128]{1,0:T(8,128)(2,1)S(1)}, u32[]{:S(2)}, u32[]{:S(2)}) collective-permute-start(bf16[768,128]{1,0:T(8,128)(2,1)S(1)} %get-tuple-element.45), channel_id=1, source_target_pairs={{0,8},{2,10},{4,12},{6,14},{8,16},{10,18},{12,20},{14,22},{16,24},... | collective-permute-start | bytes 589832 | tf_op jit(solution)/shard_map/ppermute | solution.py:190
  27.1 0.9 %collective-permute-start.1 = (bf16[128,1024]{1,0:T(8,128)(2,1)S(1)}, bf16[128,1024]{1,0:T(8,128)(2,1)S(1)}, u32[]{:S(2)}, u32[]{:S(2)}) collective-permute-start(bf16[128,1024]{1,0:T(8,128)(2,1)S(1)} %get-tuple-element.31), channel_id=1, source_target_pairs={{0,4},{2,6},{4,0},{6,2},{8,12},{10,14},{12,8},{14,10},{16,20},{18,... | collective-permute-start | bytes 786440 | tf_op jit(solution)/shard_map/ppermute | solution.py:187
  28.0 0.0 collective-permute-done.6.refs_8_
  28.0 1.4 %collective-permute-start.2 = (bf16[128,1024]{1,0:T(8,128)(2,1)S(1)}, bf16[128,1024]{1,0:T(8,128)(2,1)S(1)}, u32[]{:S(2)}, u32[]{:S(2)}) collective-permute-start(bf16[128,1024]{1,0:T(8,128)(2,1)S(1)} %get-tuple-element.32), channel_id=1, source_target_pairs={{0,6},{2,4},{4,2},{6,0},{8,14},{10,12},{12,10},{14,8},{16,22},{18,... | collective-permute-start | bytes 786440 | tf_op jit(solution)/shard_map/ppermute | solution.py:187
  29.4 0.0 collective-permute-done.8.refs_9_.refs_10_
  29.4 1.9 %collective-permute-start.9 = (bf16[816,128]{1,0:T(8,128)(2,1)S(1)}, bf16[816,128]{1,0:T(8,128)(2,1)S(1)}, u32[]{:S(2)}, u32[]{:S(2)}) collective-permute-start(bf16[816,128]{1,0:T(8,128)(2,1)S(1)} %collective-permute-done.8.refs_9_.refs_10_), channel_id=1, source_target_pairs={{0,8},{2,10},{4,12},{6,14},{8,16},{10,18},{12,20},{14,22},{16,24},... | collective-permute-start | bytes 626696 | tf_op jit(solution)/shard_map/ppermute | solution.py:190
  31.3 0.4 collective-permute-done.13.refs_9_
  31.8 4.4 %collective-permute-start.14 = (bf16[768,128]{1,0:T(8,128)(2,1)S(1)}, bf16[768,128]{1,0:T(8,128)(2,1)S(1)}, u32[]{:S(2)}, u32[]{:S(2)}) collective-permute-start(bf16[768,128]{1,0:T(8,128)(2,1)S(1)} %collective-permute-done.13.refs_9_), channel_id=1, source_target_pairs={{0,8},{2,10},{4,12},{6,14},{8,16},{10,18},{12,20},{14,22},{16,24},... | collective-permute-start | bytes 589832 | tf_op jit(solution)/shard_map/ppermute | solution.py:190
  36.2 0.0 collective-permute-done.refs_1_
  36.2 1.9 %collective-permute-start.7 = (bf16[528,128]{1,0:T(8,128)(2,1)S(1)}, bf16[528,128]{1,0:T(8,128)(2,1)S(1)}, u32[]{:S(2)}, u32[]{:S(2)}) collective-permute-start(bf16[528,128]{1,0:T(8,128)(2,1)S(1)} %collective-permute-done.6.refs_8_), channel_id=1, source_target_pairs={{0,8},{2,10},{4,12},{6,14},{8,16},{10,18},{12,20},{14,22},{16,24},... | collective-permute-start | bytes 405512 | tf_op jit(solution)/shard_map/ppermute | solution.py:190
  38.1 0.7 %collective-permute-done.1.refs_2_ = bf16[128,1024]{1,0:T(8,128)(2,1)S(1)} collective-permute-done((bf16[128,1024]{1,0:T(8,128)(2,1)S(1)}, bf16[128,1024]{1,0:T(8,128)(2,1)S(1)}, u32[]{:S(2)}, u32[]{:S(2)}) %collective-permute-start.1) | collective-permute-done | bytes 262176 | tf_op jit(solution)/shard_map/ppermute | solution.py:187
  38.8 0.0 collective-permute-done.2.refs_3_
  38.8 4.2 %shard_map.42 = (f32[4,512,128]{2,1,0:T(8,128)S(1)}, f32[4,512,128]{2,1,0:T(8,128)S(1)}, f32[4,512,128]{2,1,0:T(8,128)S(1)}) custom-call(s32[2]{0:T(128)S(1)} %pad_add_fusion.place, bf16[128,1024]{1,0:T(8,128)(2,1)S(1)} %get-tuple-element.29.refs_0_, bf16[128,1024]{1,0:T(8,128)(2,1)S(1)} %collective-permute-done.refs_1_, ...), custom_call_target="tpu_custom_call" | custom-call | tf_op jit(solution)/shard_map/pallas_call | solution.py:177
  43.1 0.0 collective-permute-done.7.refs_8_
  43.1 0.0 collective-permute-done.14.refs_9_
  43.1 0.0 collective-permute-done.9.refs_9_.refs_10_
  43.1 2.7 %shard_map.43 = (bf16[128,512]{1,0:T(8,128)(2,1)S(1)}, bf16[128,512]{1,0:T(8,128)(2,1)S(1)}, bf16[128,512]{1,0:T(8,128)(2,1)S(1)}, bf16[128,512]{1,0:T(8,128)(2,1)S(1)}) custom-call(s32[2]{0:T(128)S(1)} %pad_add_fusion.place, bf16[128,1024]{1,0:T(8,128)(2,1)S(1)} %get-tuple-element.29.refs_0_, bf16[128,1024]{1,0:T(8,128)(2,1)S(1)} %collective-permute-done.refs_1_, ...), custom_call_target="tpu_custom_call" | custom-call | tf_op jit(solution)/shard_map/pallas_call | solution.py:177
  45.8 0.6 collective-permute-start.15
  46.4 4.2 %shard_map.40 = (f32[4,512,128]{2,1,0:T(8,128)S(1)}, f32[4,512,128]{2,1,0:T(8,128)S(1)}, f32[4,512,128]{2,1,0:T(8,128)S(1)}) custom-call(s32[2]{0:T(128)S(1)} %pad_add_fusion.place, bf16[128,1024]{1,0:T(8,128)(2,1)S(1)} %get-tuple-element.29.refs_0_, bf16[128,1024]{1,0:T(8,128)(2,1)S(1)} %collective-permute-done.refs_1_, ...), custom_call_target="tpu_custom_call" | custom-call | tf_op jit(solution)/shard_map/pallas_call | solution.py:177
  50.7 1.4 %collective-permute-start.16 = (bf16[128,512]{1,0:T(8,128)(2,1)S(1)}, bf16[128,512]{1,0:T(8,128)(2,1)S(1)}, u32[]{:S(2)}, u32[]{:S(2)}) collective-permute-start(bf16[128,512]{1,0:T(8,128)(2,1)S(1)} %get-tuple-element.51), channel_id=1, source_target_pairs={{0,4},{2,6},{4,0},{6,2},{8,12},{10,14},{12,8},{14,10},{16,20},{18,... | collective-permute-start | bytes 393224 | tf_op jit(solution)/shard_map/ppermute | solution.py:187
  52.1 1.6 %collective-permute-start.17 = (bf16[128,512]{1,0:T(8,128)(2,1)S(1)}, bf16[128,512]{1,0:T(8,128)(2,1)S(1)}, u32[]{:S(2)}, u32[]{:S(2)}) collective-permute-start(bf16[128,512]{1,0:T(8,128)(2,1)S(1)} %get-tuple-element.52), channel_id=1, source_target_pairs={{0,6},{2,4},{4,2},{6,0},{8,14},{10,12},{12,10},{14,8},{16,22},{18,... | collective-permute-start | bytes 393224 | tf_op jit(solution)/shard_map/ppermute | solution.py:187
  53.7 2.7 %shard_map.41 = (bf16[128,512]{1,0:T(8,128)(2,1)S(1)}, bf16[128,512]{1,0:T(8,128)(2,1)S(1)}, bf16[128,512]{1,0:T(8,128)(2,1)S(1)}, bf16[128,512]{1,0:T(8,128)(2,1)S(1)}) custom-call(s32[2]{0:T(128)S(1)} %pad_add_fusion.place, bf16[128,1024]{1,0:T(8,128)(2,1)S(1)} %get-tuple-element.29.refs_0_, bf16[128,1024]{1,0:T(8,128)(2,1)S(1)} %collective-permute-done.refs_1_, ...), custom_call_target="tpu_custom_call" | custom-call | tf_op jit(solution)/shard_map/pallas_call | solution.py:177
  56.4 0.6 collective-permute-start.10
  57.0 1.4 %collective-permute-start.11 = (bf16[128,512]{1,0:T(8,128)(2,1)S(1)}, bf16[128,512]{1,0:T(8,128)(2,1)S(1)}, u32[]{:S(2)}, u32[]{:S(2)}) collective-permute-start(bf16[128,512]{1,0:T(8,128)(2,1)S(1)} %get-tuple-element.43), channel_id=1, source_target_pairs={{0,4},{2,6},{4,0},{6,2},{8,12},{10,14},{12,8},{14,10},{16,20},{18,... | collective-permute-start | bytes 393224 | tf_op jit(solution)/shard_map/ppermute | solution.py:187
  58.3 0.0 collective-permute-done.15.refs_5_
  58.3 1.6 %collective-permute-start.12 = (bf16[128,512]{1,0:T(8,128)(2,1)S(1)}, bf16[128,512]{1,0:T(8,128)(2,1)S(1)}, u32[]{:S(2)}, u32[]{:S(2)}) collective-permute-start(bf16[128,512]{1,0:T(8,128)(2,1)S(1)} %get-tuple-element.44), channel_id=1, source_target_pairs={{0,6},{2,4},{4,2},{6,0},{8,14},{10,12},{12,10},{14,8},{16,22},{18,... | collective-permute-start | bytes 393224 | tf_op jit(solution)/shard_map/ppermute | solution.py:187
  59.9 0.0 collective-permute-done.16.refs_6_
  59.9 0.0 collective-permute-done.17.refs_7_
  60.0 1.5 %collective-permute-done.10.refs_1_ = bf16[128,512]{1,0:T(8,128)(2,1)S(1)} collective-permute-done((bf16[128,512]{1,0:T(8,128)(2,1)S(1)}, bf16[128,512]{1,0:T(8,128)(2,1)S(1)}, u32[]{:S(2)}, u32[]{:S(2)}) %collective-permute-start.10) | collective-permute-done | bytes 131104 | tf_op jit(solution)/shard_map/ppermute | solution.py:187
  61.4 0.6 collective-permute-done.11.refs_2_
  62.0 2.2 %collective-permute-done.12.refs_3_ = bf16[128,512]{1,0:T(8,128)(2,1)S(1)} collective-permute-done((bf16[128,512]{1,0:T(8,128)(2,1)S(1)}, bf16[128,512]{1,0:T(8,128)(2,1)S(1)}, u32[]{:S(2)}, u32[]{:S(2)}) %collective-permute-start.12) | collective-permute-done | bytes 131104 | tf_op jit(solution)/shard_map/ppermute | solution.py:187
  64.2 1.6 %shard_map.44 = bf16[128,4096]{1,0:T(8,128)(2,1)} custom-call(s32[2]{0:T(128)S(1)} %pad_add_fusion.place, bf16[128,512]{1,0:T(8,128)(2,1)S(1)} %get-tuple-element.41.refs_0_, bf16[128,512]{1,0:T(8,128)(2,1)S(1)} %collective-permute-done.10.refs_1_, bf16[128,512]{1,0:T(8,128)(2,1)S(1)} %collective-permute-done.11.refs_2_, ...), custom_call_target="tpu_custom_call" | custom-call | tf_op jit(solution)/shard_map/pallas_call | solution.py:177
  (3 shorter events, 0.0 us)
Async XLA Ops:
  0.1 0.7 copy-start.2
  0.7 1.0 %copy-start.1 = (bf16[2,128,1024]{2,1,0:T(8,128)(2,1)S(1)}, bf16[2,128,1024]{2,1,0:T(8,128)(2,1)}, u32[]{:S(2)}) copy-start(bf16[2,128,1024]{2,1,0:T(8,128)(2,1)} %kv.1) | copy-start | bytes 1572868
  2.5 7.0 %collective-permute-start.3 = (bf16[528,128]{1,0:T(8,128)(2,1)S(1)}, bf16[528,128]{1,0:T(8,128)(2,1)S(1)}, u32[]{:S(2)}, u32[]{:S(2)}) collective-permute-start(bf16[528,128]{1,0:T(8,128)(2,1)S(1)} %get-tuple-element.34), channel_id=1, source_target_pairs={{0,2},{2,0},{4,6},{6,4},{8,10},{10,8},{12,14},{14,12},{16,18},{18,... | collective-permute-start | bytes 405512 | tf_op jit(solution)/shard_map/ppermute | solution.py:187
  5.5 7.9 %collective-permute-start.4 = (bf16[528,128]{1,0:T(8,128)(2,1)S(1)}, bf16[528,128]{1,0:T(8,128)(2,1)S(1)}, u32[]{:S(2)}, u32[]{:S(2)}) collective-permute-start(bf16[528,128]{1,0:T(8,128)(2,1)S(1)} %get-tuple-element.35), channel_id=1, source_target_pairs={{0,4},{2,6},{4,0},{6,2},{8,12},{10,14},{12,8},{14,10},{16,20},{18,... | collective-permute-start | bytes 405512 | tf_op jit(solution)/shard_map/ppermute | solution.py:187
  7.0 6.4 %collective-permute-start.5 = (bf16[528,128]{1,0:T(8,128)(2,1)S(1)}, bf16[528,128]{1,0:T(8,128)(2,1)S(1)}, u32[]{:S(2)}, u32[]{:S(2)}) collective-permute-start(bf16[528,128]{1,0:T(8,128)(2,1)S(1)} %get-tuple-element.36), channel_id=1, source_target_pairs={{0,6},{2,4},{4,2},{6,0},{8,14},{10,12},{12,10},{14,8},{16,22},{18,... | collective-permute-start | bytes 405512 | tf_op jit(solution)/shard_map/ppermute | solution.py:187
  13.5 15.9 %collective-permute-start.8 = (bf16[816,128]{1,0:T(8,128)(2,1)S(1)}, bf16[816,128]{1,0:T(8,128)(2,1)S(1)}, u32[]{:S(2)}, u32[]{:S(2)}) collective-permute-start(bf16[816,128]{1,0:T(8,128)(2,1)S(1)} %get-tuple-element.37), channel_id=1, source_target_pairs={{0,8},{2,10},{4,12},{6,14},{8,16},{10,18},{12,20},{14,22},{16,24},... | collective-permute-start | bytes 626696 | tf_op jit(solution)/shard_map/ppermute | solution.py:190
  17.0 11.0 %collective-permute-start.6 = (bf16[528,128]{1,0:T(8,128)(2,1)S(1)}, bf16[528,128]{1,0:T(8,128)(2,1)S(1)}, u32[]{:S(2)}, u32[]{:S(2)}) collective-permute-start(bf16[528,128]{1,0:T(8,128)(2,1)S(1)} %get-tuple-element.33.refs_4_), channel_id=1, source_target_pairs={{0,8},{2,10},{4,12},{6,14},{8,16},{10,18},{12,20},{14,22},{16,24},... | collective-permute-start | bytes 405512 | tf_op jit(solution)/shard_map/ppermute | solution.py:190
  20.5 1.2 %copy-start = (bf16[128,4096]{1,0:T(8,128)(2,1)S(1)}, bf16[128,4096]{1,0:T(8,128)(2,1)}, u32[]{:S(2)}) copy-start(bf16[128,4096]{1,0:T(8,128)(2,1)} %q.1) | copy-start | bytes 3145732
  22.3 13.9 %collective-permute-start = (bf16[128,1024]{1,0:T(8,128)(2,1)S(1)}, bf16[128,1024]{1,0:T(8,128)(2,1)S(1)}, u32[]{:S(2)}, u32[]{:S(2)}) collective-permute-start(bf16[128,1024]{1,0:T(8,128)(2,1)S(1)} %get-tuple-element.30), channel_id=1, source_target_pairs={{0,2},{2,0},{4,6},{6,4},{8,10},{10,8},{12,14},{14,12},{16,18},{18,... | collective-permute-start | bytes 786440 | tf_op jit(solution)/shard_map/ppermute | solution.py:187
  23.6 8.2 %collective-permute-start.13 = (bf16[768,128]{1,0:T(8,128)(2,1)S(1)}, bf16[768,128]{1,0:T(8,128)(2,1)S(1)}, u32[]{:S(2)}, u32[]{:S(2)}) collective-permute-start(bf16[768,128]{1,0:T(8,128)(2,1)S(1)} %get-tuple-element.45), channel_id=1, source_target_pairs={{0,8},{2,10},{4,12},{6,14},{8,16},{10,18},{12,20},{14,22},{16,24},... | collective-permute-start | bytes 589832 | tf_op jit(solution)/shard_map/ppermute | solution.py:190
  27.1 11.8 %collective-permute-start.1 = (bf16[128,1024]{1,0:T(8,128)(2,1)S(1)}, bf16[128,1024]{1,0:T(8,128)(2,1)S(1)}, u32[]{:S(2)}, u32[]{:S(2)}) collective-permute-start(bf16[128,1024]{1,0:T(8,128)(2,1)S(1)} %get-tuple-element.31), channel_id=1, source_target_pairs={{0,4},{2,6},{4,0},{6,2},{8,12},{10,14},{12,8},{14,10},{16,20},{18,... | collective-permute-start | bytes 786440 | tf_op jit(solution)/shard_map/ppermute | solution.py:187
  28.0 10.9 %collective-permute-start.2 = (bf16[128,1024]{1,0:T(8,128)(2,1)S(1)}, bf16[128,1024]{1,0:T(8,128)(2,1)S(1)}, u32[]{:S(2)}, u32[]{:S(2)}) collective-permute-start(bf16[128,1024]{1,0:T(8,128)(2,1)S(1)} %get-tuple-element.32), channel_id=1, source_target_pairs={{0,6},{2,4},{4,2},{6,0},{8,14},{10,12},{12,10},{14,8},{16,22},{18,... | collective-permute-start | bytes 786440 | tf_op jit(solution)/shard_map/ppermute | solution.py:187
  29.4 13.7 %collective-permute-start.9 = (bf16[816,128]{1,0:T(8,128)(2,1)S(1)}, bf16[816,128]{1,0:T(8,128)(2,1)S(1)}, u32[]{:S(2)}, u32[]{:S(2)}) collective-permute-start(bf16[816,128]{1,0:T(8,128)(2,1)S(1)} %collective-permute-done.8.refs_9_.refs_10_), channel_id=1, source_target_pairs={{0,8},{2,10},{4,12},{6,14},{8,16},{10,18},{12,20},{14,22},{16,24},... | collective-permute-start | bytes 626696 | tf_op jit(solution)/shard_map/ppermute | solution.py:190
  31.8 11.3 %collective-permute-start.14 = (bf16[768,128]{1,0:T(8,128)(2,1)S(1)}, bf16[768,128]{1,0:T(8,128)(2,1)S(1)}, u32[]{:S(2)}, u32[]{:S(2)}) collective-permute-start(bf16[768,128]{1,0:T(8,128)(2,1)S(1)} %collective-permute-done.13.refs_9_), channel_id=1, source_target_pairs={{0,8},{2,10},{4,12},{6,14},{8,16},{10,18},{12,20},{14,22},{16,24},... | collective-permute-start | bytes 589832 | tf_op jit(solution)/shard_map/ppermute | solution.py:190
  36.2 6.9 %collective-permute-start.7 = (bf16[528,128]{1,0:T(8,128)(2,1)S(1)}, bf16[528,128]{1,0:T(8,128)(2,1)S(1)}, u32[]{:S(2)}, u32[]{:S(2)}) collective-permute-start(bf16[528,128]{1,0:T(8,128)(2,1)S(1)} %collective-permute-done.6.refs_8_), channel_id=1, source_target_pairs={{0,8},{2,10},{4,12},{6,14},{8,16},{10,18},{12,20},{14,22},{16,24},... | collective-permute-start | bytes 405512 | tf_op jit(solution)/shard_map/ppermute | solution.py:190
  45.8 12.5 %collective-permute-start.15 = (bf16[128,512]{1,0:T(8,128)(2,1)S(1)}, bf16[128,512]{1,0:T(8,128)(2,1)S(1)}, u32[]{:S(2)}, u32[]{:S(2)}) collective-permute-start(bf16[128,512]{1,0:T(8,128)(2,1)S(1)} %get-tuple-element.50), channel_id=1, source_target_pairs={{0,2},{2,0},{4,6},{6,4},{8,10},{10,8},{12,14},{14,12},{16,18},{18,... | collective-permute-start | bytes 393224 | tf_op jit(solution)/shard_map/ppermute | solution.py:187
  50.7 9.3 %collective-permute-start.16 = (bf16[128,512]{1,0:T(8,128)(2,1)S(1)}, bf16[128,512]{1,0:T(8,128)(2,1)S(1)}, u32[]{:S(2)}, u32[]{:S(2)}) collective-permute-start(bf16[128,512]{1,0:T(8,128)(2,1)S(1)} %get-tuple-element.51), channel_id=1, source_target_pairs={{0,4},{2,6},{4,0},{6,2},{8,12},{10,14},{12,8},{14,10},{16,20},{18,... | collective-permute-start | bytes 393224 | tf_op jit(solution)/shard_map/ppermute | solution.py:187
  52.1 7.9 %collective-permute-start.17 = (bf16[128,512]{1,0:T(8,128)(2,1)S(1)}, bf16[128,512]{1,0:T(8,128)(2,1)S(1)}, u32[]{:S(2)}, u32[]{:S(2)}) collective-permute-start(bf16[128,512]{1,0:T(8,128)(2,1)S(1)} %get-tuple-element.52), channel_id=1, source_target_pairs={{0,6},{2,4},{4,2},{6,0},{8,14},{10,12},{12,10},{14,8},{16,22},{18,... | collective-permute-start | bytes 393224 | tf_op jit(solution)/shard_map/ppermute | solution.py:187
  56.4 5.0 %collective-permute-start.10 = (bf16[128,512]{1,0:T(8,128)(2,1)S(1)}, bf16[128,512]{1,0:T(8,128)(2,1)S(1)}, u32[]{:S(2)}, u32[]{:S(2)}) collective-permute-start(bf16[128,512]{1,0:T(8,128)(2,1)S(1)} %get-tuple-element.42), channel_id=1, source_target_pairs={{0,2},{2,0},{4,6},{6,4},{8,10},{10,8},{12,14},{14,12},{16,18},{18,... | collective-permute-start | bytes 393224 | tf_op jit(solution)/shard_map/ppermute | solution.py:187
  57.0 5.0 %collective-permute-start.11 = (bf16[128,512]{1,0:T(8,128)(2,1)S(1)}, bf16[128,512]{1,0:T(8,128)(2,1)S(1)}, u32[]{:S(2)}, u32[]{:S(2)}) collective-permute-start(bf16[128,512]{1,0:T(8,128)(2,1)S(1)} %get-tuple-element.43), channel_id=1, source_target_pairs={{0,4},{2,6},{4,0},{6,2},{8,12},{10,14},{12,8},{14,10},{16,20},{18,... | collective-permute-start | bytes 393224 | tf_op jit(solution)/shard_map/ppermute | solution.py:187
  58.3 5.9 %collective-permute-start.12 = (bf16[128,512]{1,0:T(8,128)(2,1)S(1)}, bf16[128,512]{1,0:T(8,128)(2,1)S(1)}, u32[]{:S(2)}, u32[]{:S(2)}) collective-permute-start(bf16[128,512]{1,0:T(8,128)(2,1)S(1)} %get-tuple-element.44), channel_id=1, source_target_pairs={{0,6},{2,4},{4,2},{6,0},{8,14},{10,12},{12,10},{14,8},{16,22},{18,... | collective-permute-start | bytes 393224 | tf_op jit(solution)/shard_map/ppermute | solution.py:187
where the time goes:
time: 66.1 us; the launch traced here: 65.8 us
  starting transfers between devices  34 us (51%)
  Pallas kernels  16.8 us (25%)
  waiting for transfers between devices  11.9 us (18%)
  local copies, waits for them, and re-layouts  2.92 us (4%)
    ppermute x6, starting transfers between devices, onward(): return lax.ppermute(x, 'seq', [(i, i + size) for i in range(shards - size)])  18.7 us
    pallas_call x8, Pallas kernels, call(): pl.pallas_call(body, in_specs=[smem if a is place else vmem for a in args...  16.8 us
    ppermute x12, starting transfers between devices, swap(): lax.ppermute(x, 'seq', [(i, i ^ k) for i in range(shards)])  15.4 us
    ppermute x12, waiting for transfers between devices, swap(): lax.ppermute(x, 'seq', [(i, i ^ k) for i in range(shards)])  11.4 us
    unnamed x6, local copies, waits for them, and re-layouts  2.92 us
  transfers between devices with their start and end apart: 18, of which 7 were waited for; matrix products, arithmetic and copies ran while one was open for 0% of the time, Pallas kernels for 18%

commit v1 on v0

v1 whole, which is shorter than its diff:
```python
import functools
import jax
import jax.numpy as jnp
from jax import lax
from jax.experimental import pallas as pl
from jax.experimental.pallas import tpu as pltpu
from jax.sharding import PartitionSpec as P

HQ = 32
HK = 8
DH = 128
WINDOW = 2048

GROUP = HQ // HK
NEG_BIG = -1e30
LOG2E = 1.4426950408889634
ID_ROWS = 16
IDS = 32


def pack(place, kv, ids, q, *refs, size, chunks):
    kv_outs, q_outs, (ids_buf, sems) = refs[:size], refs[size : 2 * size], refs[2 * size :]
    rows = kv.shape[1]
    width = q_outs[0].shape[1]
    moves = [(ids, ids_buf)]
    for k in range(size):
        for c in range(chunks):
            start = pl.multiple_of(((place[0] ^ k) * chunks + c) * DH, DH)
            for part in range(2):
                first = (2 * c + part) * rows
                moves.append((kv.at[part, :, pl.ds(start, DH)], kv_outs[k].at[pl.ds(first, rows), :]))
    for k in range(size):
        moves.append((q.at[:, pl.ds(pl.multiple_of((place[0] ^ k) * width, width), width)], q_outs[k]))
    copies = [pltpu.make_async_copy(a, b, sems.at[n]) for n, (a, b) in enumerate(moves)]
    for copy in copies:
        copy.start()
    copies[0].wait()
    tag = jnp.broadcast_to(ids_buf[...].astype(jnp.float32), (ID_ROWS, rows)).astype(jnp.bfloat16)
    for k in range(size):
        kv_outs[k][2 * chunks * rows :, :] = tag
    for copy in copies[1:]:
        copy.wait()


def join(*refs, count, chunks, rows):
    outs = refs[count:]
    for n in range(count):
        for c in range(chunks):
            outs[c][2 * n * rows : 2 * (n + 1) * rows, :] = refs[n][2 * c * rows : 2 * (c + 1) * rows, :]
        outs[0][2 * count * rows + n * ID_ROWS : 2 * count * rows + (n + 1) * ID_ROWS, :] = refs[n][
            2 * chunks * rows :, :
        ]


def unpack(place, *refs, size, chunks):
    out, sems = refs[-2:]
    width = refs[0].shape[1]
    copies = []
    for c in range(chunks):
        for k in range(size):
            start = pl.multiple_of(((place[0] ^ k) * chunks + c) * width, width)
            n = c * size + k
            copies.append(pltpu.make_async_copy(refs[n], out.at[:, pl.ds(start, width)], sems.at[n]))
    for copy in copies:
        copy.start()
    for copy in copies:
        copy.wait()


def attend(place, *refs, chunk, size, chunks, rows, steps, first, last):
    q_refs, near, refs = refs[:size], refs[size : 2 * size], refs[2 * size :]
    far = {}
    for d in steps:
        if d:
            count = 3 if chunk else 2
            far[d] = (refs[0], refs[1], refs[count - 1])
            refs = refs[count:]
    if not first:
        old_top_ref, old_sum_ref, old_acc_ref = refs[:3]
        refs = refs[3:]
    if last:
        outs, refs = refs[:size], refs[size:]
    else:
        top_ref, sum_ref, acc_ref = refs[:3]
        refs = refs[3:]
    q_buf, k_buf, v_buf, s_buf, w_buf = refs
    keys = k_buf.shape[0]
    tile = min(256, keys)
    member, block = place[0], place[1]
    tag_at = 2 * chunks * rows
    lane = lax.broadcasted_iota(jnp.int32, (rows, DH), 1)
    lane_tag = lane.astype(jnp.float32)
    after = lane > lax.broadcasted_iota(jnp.int32, (rows, DH), 0)
    scale = DH**-0.5 * LOG2E

    def column(tag_row):
        return jnp.broadcast_to(tag_row.astype(jnp.float32), (rows, DH)).T

    for x, d in enumerate(steps):
        for k in range(size):
            n = x * size + k
            if d == 0 or k == 0:
                ref = near[k] if d == 0 else far[d][0]
                start, tag_ref, tag_row = 2 * chunk * rows, ref, tag_at
            else:
                ref, tag_ref = far[d][1], far[d][2]
                start, tag_row = 2 * (k - 1) * rows, 2 * (size - 1) * rows + (k - 1) * ID_ROWS
            at = slice(n * rows, (n + 1) * rows)
            k_buf[at, :DH] = ref[start : start + rows, :]
            v_buf[at, :] = ref[start + rows : start + 2 * rows, :]
            other = column(tag_ref[tag_row : tag_row + 1, :]) != lane_tag
            if d:
                blocked = (other & (lane < IDS)) | (block < d)
            else:
                blocked = (other & (lane < IDS)) | (lane == IDS + (member ^ k))
            k_buf[at, DH:] = jnp.where(blocked, NEG_BIG, 0.0).astype(jnp.bfloat16)

    def scores(i):
        own = column(near[i][tag_at : tag_at + 1, :]) == lane_tag
        later = (lane > IDS + (member ^ i)) & (lane < IDS + size)
        mark = jnp.where(own | later, 1.0, 0.0).astype(jnp.bfloat16)
        at = chunk * GROUP * DH
        for h in range(GROUP):
            q_buf[i % 2, h * rows : (h + 1) * rows, :DH] = q_refs[i][:, at + h * DH : at + (h + 1) * DH]
            q_buf[i % 2, h * rows : (h + 1) * rows, DH:] = mark
        for t in range(0, keys, tile):
            s_buf[i % 2, :, t : t + tile] = lax.dot_general(
                q_buf[i % 2],
                k_buf[t : t + tile, :],
                (((1,), (1,)), ((), ())),
                preferred_element_type=jnp.float32,
            )

    def softmax(i):
        kept = []
        for h in range(GROUP):
            at = slice(h * rows, (h + 1) * rows)
            top = None
            for t in range(0, keys, DH):
                part = s_buf[i % 2, at, t : t + DH]
                if steps[0] == 0 and t == i * rows and rows == DH:
                    part = jnp.where(after, NEG_BIG, part)
                    s_buf[i % 2, at, t : t + DH] = part
                top = part if top is None else jnp.maximum(top, part)
            top = jnp.broadcast_to(jnp.max(top, axis=1, keepdims=True), (rows, DH))
            if not first:
                top = jnp.maximum(top, old_top_ref[i, at, :])
            total = None
            for t in range(0, keys, DH):
                part = jnp.exp2((s_buf[i % 2, at, t : t + DH] - top) * scale)
                total = part if total is None else total + part
                w_buf[i % 2, at, t : t + DH] = part.astype(jnp.bfloat16)
            total = jnp.broadcast_to(jnp.sum(total, axis=1, keepdims=True), (rows, DH))
            if not first:
                rescale = jnp.exp2((old_top_ref[i, at, :] - top) * scale)
                total = total + old_sum_ref[i, at, :] * rescale
            else:
                rescale = None
            if not last:
                top_ref[i, at, :] = top
                sum_ref[i, at, :] = total
            kept.append((total, rescale))
        return kept

    def context(i, kept):
        acc = jnp.dot(w_buf[i % 2], v_buf[...], preferred_element_type=jnp.float32)
        for h, (total, rescale) in enumerate(kept):
            at = slice(h * rows, (h + 1) * rows)
            part = acc[at, :]
            if rescale is not None:
                part = part + old_acc_ref[i, at, :] * rescale
            if last:
                outs[i][:, h * DH : (h + 1) * DH] = (part / total).astype(jnp.bfloat16)
            else:
                acc_ref[i, at, :] = part

    scores(0)
    for i in range(size):
        if i + 1 < size:
            scores(i + 1)
        context(i, softmax(i))


def layout_of(shards, rows):
    size = 1
    while (2 * size) ** 2 <= shards and 2 * size <= HK:
        size *= 2
    reach = min(WINDOW, rows * shards // 2)
    back = min(-(-(reach - 1) // (size * rows)), shards // size - 1)
    return size, HK // size, back


def local(queries, keys_values, segment_ids, shards):
    rows = queries.shape[0]
    size, chunks, back = layout_of(shards, rows)
    width = GROUP * DH
    me = lax.axis_index("seq")
    place = jnp.stack([me & (size - 1), me >> (size.bit_length() - 1)]).astype(jnp.int32)
    smem = pl.BlockSpec(memory_space=pltpu.SMEM)
    vmem = pl.BlockSpec(memory_space=pltpu.VMEM)
    hbm = pl.BlockSpec(memory_space=pltpu.HBM)
    params = pltpu.CompilerParams(vmem_limit_bytes=48 * 1024 * 1024)
    bf16 = functools.partial(jax.ShapeDtypeStruct, dtype=jnp.bfloat16)
    f32 = functools.partial(jax.ShapeDtypeStruct, dtype=jnp.float32)

    def call(body, shapes, args, scratch=(), far_in=(), far_out=False):
        return pl.pallas_call(
            body,
            in_specs=[smem if a is place else hbm if n in far_in else vmem for n, a in enumerate(args)],
            out_specs=[hbm if far_out else vmem] * len(shapes),
            out_shape=shapes,
            scratch_shapes=scratch,
            compiler_params=params,
        )(*args)

    def swap(x, k):
        return lax.ppermute(x, "seq", [(i, i ^ k) for i in range(shards)]) if k else x

    def onward(x):
        return lax.ppermute(x, "seq", [(i, i + size) for i in range(shards - size)])

    packed = call(
        functools.partial(pack, size=size, chunks=chunks),
        [bf16((2 * chunks * rows + ID_ROWS, DH))] * size + [bf16((rows, chunks * width))] * size,
        [place, keys_values, segment_ids.reshape(1, rows), queries],
        [pltpu.VMEM((1, rows), jnp.int32), pltpu.SemaphoreType.DMA((1 + 2 * HK + size,))],
        far_in=(1, 2, 3),
    )
    sent, q_sent = packed[:size], packed[size:]
    near = [swap(sent[k], k) for k in range(size)]
    q_parts = [swap(q_sent[k], k) for k in range(size)]
    count = size - 1
    rest_shapes = [bf16((count * (2 * rows + (0 if c else ID_ROWS)), DH)) for c in range(chunks)]
    far_own, far_rest = [sent[0]], []
    if back:
        far_rest.append(call(functools.partial(join, count=count, chunks=chunks, rows=rows), rest_shapes, near[1:]))
    for d in range(1, back + 1):
        far_own.append(onward(far_own[d - 1]))
        far_rest.append([onward(far_rest[d - 1][c]) for c in range(chunks)])

    def stage(c, steps, state, first, last):
        keys = len(steps) * size * rows
        args = [place] + q_parts + near
        for d in steps:
            if d:
                args += [far_own[d], far_rest[d][c]] + ([far_rest[d][0]] if c else [])
        args += list(state)
        shapes = [bf16((rows, width))] * size if last else [f32((size, GROUP * rows, DH))] * 3
        scratch = [
            pltpu.VMEM((2, GROUP * rows, 2 * DH), jnp.bfloat16),
            pltpu.VMEM((keys, 2 * DH), jnp.bfloat16),
            pltpu.VMEM((keys, DH), jnp.bfloat16),
            pltpu.VMEM((2, GROUP * rows, keys), jnp.float32),
            pltpu.VMEM((2, GROUP * rows, keys), jnp.bfloat16),
        ]
        body = functools.partial(
            attend, chunk=c, size=size, chunks=chunks, rows=rows, steps=steps, first=first, last=last
        )
        return call(body, shapes, args, scratch)

    states = [()] * chunks
    if back:
        states = [stage(c, tuple(range(back)), (), True, False) for c in range(chunks)]
    done = []
    for c in range(chunks):
        result = stage(c, (back,), states[c], not back, True)
        done += [swap(result[k], k) for k in range(size)]
    return call(
        functools.partial(unpack, size=size, chunks=chunks),
        [bf16(queries.shape)],
        [place] + done,
        [pltpu.SemaphoreType.DMA((len(done),))],
        far_out=True,
    )[0]


def solution(mesh):
    shards = mesh.shape["seq"]

    def body(queries, keys_values, segment_ids):
        return local(queries, keys_values, segment_ids, shards)

    return jax.shard_map(
        body,
        mesh=mesh,
        in_specs=(P(("rep", "seq"), None), P(None, ("rep", "seq"), None), P(("rep", "seq"))),
        out_specs=P(("rep", "seq"), None),
        check_vma=False,
    )
```

time: 66.1 us -> 67.6 us (1.023)
  starting transfers between devices: 34 us -> 36.3 us
  waiting for transfers between devices: 11.9 us -> 10.9 us
    ppermute x6, starting transfers between devices: 18.7 us -> 20.9 us  [onward(): return lax.ppermute(x, 'seq', [(i, i + size) for i in range(shards - size)])]
    pallas_call x8 -> x7, Pallas kernels: 16.8 us -> 17 us  [call(): pl.pallas_call(body, in_specs=[smem if a is place else hbm if n in far_in...]
  transfers between devices with their start and end apart: 18 -> 18, of which waited for: 7 -> 5; matrix products, arithmetic and copies ran while one was open for 0% -> 0% of each run, Pallas kernels for 18% -> 17%
where the time goes in v1:
time: 67.6 us; the launch traced here: 67.3 us
  starting transfers between devices  36.3 us (54%)
  Pallas kernels  17 us (25%)
  waiting for transfers between devices  10.9 us (16%)
  local copies, waits for them, and re-layouts  2.92 us (4%)
    ppermute x6, starting transfers between devices, onward(): return lax.ppermute(x, 'seq', [(i, i + size) for i in range(shards - size)])  20.9 us
    pallas_call x7, Pallas kernels, call(): pl.pallas_call(body, in_specs=[smem if a is place else hbm if n in far_in...  17 us
    ppermute x12, starting transfers between devices, swap(): lax.ppermute(x, 'seq', [(i, i ^ k) for i in range(shards)])  15.4 us
    ppermute x12, waiting for transfers between devices, swap(): lax.ppermute(x, 'seq', [(i, i ^ k) for i in range(shards)])  10.8 us
    unnamed x6, local copies, waits for them, and re-layouts  2.92 us
  transfers between devices with their start and end apart: 18, of which 5 were waited for; matrix products, arithmetic and copies ran while one was open for 0% of the time, Pallas kernels for 17%

profile of v1, /device:TPU:0, one launch (start us, length us, event | category | flops | bytes accessed | tf_op | source)
XLA Modules:
  0.0 67.3 jit_solution(13505637534162276922)
XLA Ops:
  0.0 0.1 pad_add_fusion.place
  0.1 0.0 copy-start.2
  0.1 0.7 copy-done.2
  0.7 0.0 copy-start
  0.7 1.2 %copy-done = bf16[128,4096]{1,0:T(8,128)(2,1)S(1)} copy-done((bf16[128,4096]{1,0:T(8,128)(2,1)S(1)}, bf16[128,4096]{1,0:T(8,128)(2,1)}, u32[]{:S(2)}) %copy-start) | copy-done | bytes 1048600
  2.0 1.0 %copy-done.1 = bf16[2,128,1024]{2,1,0:T(8,128)(2,1)S(1)} copy-done((bf16[2,128,1024]{2,1,0:T(8,128)(2,1)S(1)}, bf16[2,128,1024]{2,1,0:T(8,128)(2,1)}, u32[]{:S(2)}) %copy-start.1) | copy-done | bytes 524312
  3.0 1.0 %shard_map.37 = (bf16[528,128]{1,0:T(8,128)(2,1)S(1)}, bf16[528,128]{1,0:T(8,128)(2,1)S(1)}, bf16[528,128]{1,0:T(8,128)(2,1)S(1)}, bf16[528,128]{1,0:T(8,128)(2,...) custom-call(s32[2]{0:T(128)S(1)} %pad_add_fusion.place, ...), custom_call_target="tpu_custom_call" | custom-call | tf_op jit(solution)/shard_map/pallas_call | solution.py:207
  4.0 3.0 %collective-permute-start.3 = (bf16[528,128]{1,0:T(8,128)(2,1)S(1)}, bf16[528,128]{1,0:T(8,128)(2,1)S(1)}, u32[]{:S(2)}, u32[]{:S(2)}) collective-permute-start(bf16[528,128]{1,0:T(8,128)(2,1)S(1)} %get-tuple-element.34), channel_id=1, source_target_pairs={{0,2},{2,0},{4,6},{6,4},{8,10},{10,8},{12,14},{14,12},{16,18},{18,... | collective-permute-start | bytes 405512 | tf_op jit(solution)/shard_map/ppermute | solution.py:217
  7.0 1.5 %collective-permute-start.4 = (bf16[528,128]{1,0:T(8,128)(2,1)S(1)}, bf16[528,128]{1,0:T(8,128)(2,1)S(1)}, u32[]{:S(2)}, u32[]{:S(2)}) collective-permute-start(bf16[528,128]{1,0:T(8,128)(2,1)S(1)} %get-tuple-element.35), channel_id=1, source_target_pairs={{0,4},{2,6},{4,0},{6,2},{8,12},{10,14},{12,8},{14,10},{16,20},{18,... | collective-permute-start | bytes 405512 | tf_op jit(solution)/shard_map/ppermute | solution.py:217
  8.6 0.0 collective-permute-start.5
  8.6 2.4 %collective-permute-done.3.refs_0_.refs_5_ = bf16[528,128]{1,0:T(8,128)(2,1)S(1)} collective-permute-done((bf16[528,128]{1,0:T(8,128)(2,1)S(1)}, bf16[528,128]{1,0:T(8,128)(2,1)S(1)}, u32[]{:S(2)}, u32[]{:S(2)}) %collective-permute-start.3) | collective-permute-done | bytes 135200 | tf_op jit(solution)/shard_map/ppermute | solution.py:217
  11.0 4.0 %collective-permute-done.4.refs_1_.refs_6_ = bf16[528,128]{1,0:T(8,128)(2,1)S(1)} collective-permute-done((bf16[528,128]{1,0:T(8,128)(2,1)S(1)}, bf16[528,128]{1,0:T(8,128)(2,1)S(1)}, u32[]{:S(2)}, u32[]{:S(2)}) %collective-permute-start.4) | collective-permute-done | bytes 135200 | tf_op jit(solution)/shard_map/ppermute | solution.py:217
  15.0 0.0 collective-permute-done.5.refs_2_.refs_7_
  15.0 3.5 %collective-permute-start.8 = (bf16[816,128]{1,0:T(8,128)(2,1)S(1)}, bf16[816,128]{1,0:T(8,128)(2,1)S(1)}, u32[]{:S(2)}, u32[]{:S(2)}) collective-permute-start(bf16[816,128]{1,0:T(8,128)(2,1)S(1)} %get-tuple-element.37), channel_id=1, source_target_pairs={{0,8},{2,10},{4,12},{6,14},{8,16},{10,18},{12,20},{14,22},{16,24},... | collective-permute-start | bytes 626696 | tf_op jit(solution)/shard_map/ppermute | solution.py:220
  18.5 3.5 %collective-permute-start.6 = (bf16[528,128]{1,0:T(8,128)(2,1)S(1)}, bf16[528,128]{1,0:T(8,128)(2,1)S(1)}, u32[]{:S(2)}, u32[]{:S(2)}) collective-permute-start(bf16[528,128]{1,0:T(8,128)(2,1)S(1)} %get-tuple-element.33.refs_4_), channel_id=1, source_target_pairs={{0,8},{2,10},{4,12},{6,14},{8,16},{10,18},{12,20},{14,22},{16,24},... | collective-permute-start | bytes 405512 | tf_op jit(solution)/shard_map/ppermute | solution.py:220
  22.0 1.3 %collective-permute-start = (bf16[128,1024]{1,0:T(8,128)(2,1)S(1)}, bf16[128,1024]{1,0:T(8,128)(2,1)S(1)}, u32[]{:S(2)}, u32[]{:S(2)}) collective-permute-start(bf16[128,1024]{1,0:T(8,128)(2,1)S(1)} %get-tuple-element.30), channel_id=1, source_target_pairs={{0,2},{2,0},{4,6},{6,4},{8,10},{10,8},{12,14},{14,12},{16,18},{18,... | collective-permute-start | bytes 786440 | tf_op jit(solution)/shard_map/ppermute | solution.py:217
  23.3 3.5 %collective-permute-start.13 = (bf16[768,128]{1,0:T(8,128)(2,1)S(1)}, bf16[768,128]{1,0:T(8,128)(2,1)S(1)}, u32[]{:S(2)}, u32[]{:S(2)}) collective-permute-start(bf16[768,128]{1,0:T(8,128)(2,1)S(1)} %get-tuple-element.45), channel_id=1, source_target_pairs={{0,8},{2,10},{4,12},{6,14},{8,16},{10,18},{12,20},{14,22},{16,24},... | collective-permute-start | bytes 589832 | tf_op jit(solution)/shard_map/ppermute | solution.py:220
  26.8 0.9 %collective-permute-start.1 = (bf16[128,1024]{1,0:T(8,128)(2,1)S(1)}, bf16[128,1024]{1,0:T(8,128)(2,1)S(1)}, u32[]{:S(2)}, u32[]{:S(2)}) collective-permute-start(bf16[128,1024]{1,0:T(8,128)(2,1)S(1)} %get-tuple-element.31), channel_id=1, source_target_pairs={{0,4},{2,6},{4,0},{6,2},{8,12},{10,14},{12,8},{14,10},{16,20},{18,... | collective-permute-start | bytes 786440 | tf_op jit(solution)/shard_map/ppermute | solution.py:217
  27.7 0.0 collective-permute-done.6.refs_8_
  27.7 1.4 %collective-permute-start.2 = (bf16[128,1024]{1,0:T(8,128)(2,1)S(1)}, bf16[128,1024]{1,0:T(8,128)(2,1)S(1)}, u32[]{:S(2)}, u32[]{:S(2)}) collective-permute-start(bf16[128,1024]{1,0:T(8,128)(2,1)S(1)} %get-tuple-element.32), channel_id=1, source_target_pairs={{0,6},{2,4},{4,2},{6,0},{8,14},{10,12},{12,10},{14,8},{16,22},{18,... | collective-permute-start | bytes 786440 | tf_op jit(solution)/shard_map/ppermute | solution.py:217
  29.1 0.0 collective-permute-done.8.refs_9_.refs_10_
  29.1 2.2 %collective-permute-start.9 = (bf16[816,128]{1,0:T(8,128)(2,1)S(1)}, bf16[816,128]{1,0:T(8,128)(2,1)S(1)}, u32[]{:S(2)}, u32[]{:S(2)}) collective-permute-start(bf16[816,128]{1,0:T(8,128)(2,1)S(1)} %collective-permute-done.8.refs_9_.refs_10_), channel_id=1, source_target_pairs={{0,8},{2,10},{4,12},{6,14},{8,16},{10,18},{12,20},{14,22},{16,24},... | collective-permute-start | bytes 626696 | tf_op jit(solution)/shard_map/ppermute | solution.py:220
  31.3 0.0 collective-permute-done.13.refs_9_
  31.3 4.1 %collective-permute-start.14 = (bf16[768,128]{1,0:T(8,128)(2,1)S(1)}, bf16[768,128]{1,0:T(8,128)(2,1)S(1)}, u32[]{:S(2)}, u32[]{:S(2)}) collective-permute-start(bf16[768,128]{1,0:T(8,128)(2,1)S(1)} %collective-permute-done.13.refs_9_), channel_id=1, source_target_pairs={{0,8},{2,10},{4,12},{6,14},{8,16},{10,18},{12,20},{14,22},{16,24},... | collective-permute-start | bytes 589832 | tf_op jit(solution)/shard_map/ppermute | solution.py:220
  35.4 0.0 collective-permute-done.refs_1_
  35.4 4.2 %collective-permute-start.7 = (bf16[528,128]{1,0:T(8,128)(2,1)S(1)}, bf16[528,128]{1,0:T(8,128)(2,1)S(1)}, u32[]{:S(2)}, u32[]{:S(2)}) collective-permute-start(bf16[528,128]{1,0:T(8,128)(2,1)S(1)} %collective-permute-done.6.refs_8_), channel_id=1, source_target_pairs={{0,8},{2,10},{4,12},{6,14},{8,16},{10,18},{12,20},{14,22},{16,24},... | collective-permute-start | bytes 405512 | tf_op jit(solution)/shard_map/ppermute | solution.py:220
  39.6 0.0 collective-permute-done.1.refs_2_
  39.7 0.0 collective-permute-done.2.refs_3_
  39.7 4.4 %shard_map.41 = (f32[4,512,128]{2,1,0:T(8,128)S(1)}, f32[4,512,128]{2,1,0:T(8,128)S(1)}, f32[4,512,128]{2,1,0:T(8,128)S(1)}) custom-call(s32[2]{0:T(128)S(1)} %pad_add_fusion.place, bf16[128,1024]{1,0:T(8,128)(2,1)S(1)} %get-tuple-element.29.refs_0_, bf16[128,1024]{1,0:T(8,128)(2,1)S(1)} %collective-permute-done.refs_1_, ...), custom_call_target="tpu_custom_call" | custom-call | tf_op jit(solution)/shard_map/pallas_call | solution.py:207
  44.1 0.0 collective-permute-done.7.refs_8_
  44.1 0.0 collective-permute-done.14.refs_9_
  44.1 0.0 collective-permute-done.9.refs_9_.refs_10_
  44.1 2.8 %shard_map.42 = (bf16[128,512]{1,0:T(8,128)(2,1)S(1)}, bf16[128,512]{1,0:T(8,128)(2,1)S(1)}, bf16[128,512]{1,0:T(8,128)(2,1)S(1)}, bf16[128,512]{1,0:T(8,128)(2,1)S(1)}) custom-call(s32[2]{0:T(128)S(1)} %pad_add_fusion.place, bf16[128,1024]{1,0:T(8,128)(2,1)S(1)} %get-tuple-element.29.refs_0_, bf16[128,1024]{1,0:T(8,128)(2,1)S(1)} %collective-permute-done.refs_1_, ...), custom_call_target="tpu_custom_call" | custom-call | tf_op jit(solution)/shard_map/pallas_call | solution.py:207
  46.9 0.6 collective-permute-start.15
  47.5 4.4 %shard_map.39 = (f32[4,512,128]{2,1,0:T(8,128)S(1)}, f32[4,512,128]{2,1,0:T(8,128)S(1)}, f32[4,512,128]{2,1,0:T(8,128)S(1)}) custom-call(s32[2]{0:T(128)S(1)} %pad_add_fusion.place, bf16[128,1024]{1,0:T(8,128)(2,1)S(1)} %get-tuple-element.29.refs_0_, bf16[128,1024]{1,0:T(8,128)(2,1)S(1)} %collective-permute-done.refs_1_, ...), custom_call_target="tpu_custom_call" | custom-call | tf_op jit(solution)/shard_map/pallas_call | solution.py:207
  51.9 1.6 %collective-permute-start.16 = (bf16[128,512]{1,0:T(8,128)(2,1)S(1)}, bf16[128,512]{1,0:T(8,128)(2,1)S(1)}, u32[]{:S(2)}, u32[]{:S(2)}) collective-permute-start(bf16[128,512]{1,0:T(8,128)(2,1)S(1)} %get-tuple-element.51), channel_id=1, source_target_pairs={{0,4},{2,6},{4,0},{6,2},{8,12},{10,14},{12,8},{14,10},{16,20},{18,... | collective-permute-start | bytes 393224 | tf_op jit(solution)/shard_map/ppermute | solution.py:217
  53.5 1.4 %collective-permute-start.17 = (bf16[128,512]{1,0:T(8,128)(2,1)S(1)}, bf16[128,512]{1,0:T(8,128)(2,1)S(1)}, u32[]{:S(2)}, u32[]{:S(2)}) collective-permute-start(bf16[128,512]{1,0:T(8,128)(2,1)S(1)} %get-tuple-element.52), channel_id=1, source_target_pairs={{0,6},{2,4},{4,2},{6,0},{8,14},{10,12},{12,10},{14,8},{16,22},{18,... | collective-permute-start | bytes 393224 | tf_op jit(solution)/shard_map/ppermute | solution.py:217
  55.0 2.8 %shard_map.40 = (bf16[128,512]{1,0:T(8,128)(2,1)S(1)}, bf16[128,512]{1,0:T(8,128)(2,1)S(1)}, bf16[128,512]{1,0:T(8,128)(2,1)S(1)}, bf16[128,512]{1,0:T(8,128)(2,1)S(1)}) custom-call(s32[2]{0:T(128)S(1)} %pad_add_fusion.place, bf16[128,1024]{1,0:T(8,128)(2,1)S(1)} %get-tuple-element.29.refs_0_, bf16[128,1024]{1,0:T(8,128)(2,1)S(1)} %collective-permute-done.refs_1_, ...), custom_call_target="tpu_custom_call" | custom-call | tf_op jit(solution)/shard_map/pallas_call | solution.py:207
  57.8 0.6 collective-permute-start.10
  58.4 1.5 %collective-permute-start.11 = (bf16[128,512]{1,0:T(8,128)(2,1)S(1)}, bf16[128,512]{1,0:T(8,128)(2,1)S(1)}, u32[]{:S(2)}, u32[]{:S(2)}) collective-permute-start(bf16[128,512]{1,0:T(8,128)(2,1)S(1)} %get-tuple-element.43), channel_id=1, source_target_pairs={{0,4},{2,6},{4,0},{6,2},{8,12},{10,14},{12,8},{14,10},{16,20},{18,... | collective-permute-start | bytes 393224 | tf_op jit(solution)/shard_map/ppermute | solution.py:217
  59.9 0.0 collective-permute-done.15.refs_5_
  59.9 1.4 %collective-permute-start.12 = (bf16[128,512]{1,0:T(8,128)(2,1)S(1)}, bf16[128,512]{1,0:T(8,128)(2,1)S(1)}, u32[]{:S(2)}, u32[]{:S(2)}) collective-permute-start(bf16[128,512]{1,0:T(8,128)(2,1)S(1)} %get-tuple-element.44), channel_id=1, source_target_pairs={{0,6},{2,4},{4,2},{6,0},{8,14},{10,12},{12,10},{14,8},{16,22},{18,... | collective-permute-start | bytes 393224 | tf_op jit(solution)/shard_map/ppermute | solution.py:217
  61.3 0.0 collective-permute-done.16.refs_6_
  61.3 0.0 collective-permute-done.17.refs_7_
  61.3 1.5 %collective-permute-done.10.refs_1_ = bf16[128,512]{1,0:T(8,128)(2,1)S(1)} collective-permute-done((bf16[128,512]{1,0:T(8,128)(2,1)S(1)}, bf16[128,512]{1,0:T(8,128)(2,1)S(1)}, u32[]{:S(2)}, u32[]{:S(2)}) %collective-permute-start.10) | collective-permute-done | bytes 131104 | tf_op jit(solution)/shard_map/ppermute | solution.py:217
  62.8 0.5 collective-permute-done.11.refs_2_
  63.3 2.4 %collective-permute-done.12.refs_3_ = bf16[128,512]{1,0:T(8,128)(2,1)S(1)} collective-permute-done((bf16[128,512]{1,0:T(8,128)(2,1)S(1)}, bf16[128,512]{1,0:T(8,128)(2,1)S(1)}, u32[]{:S(2)}, u32[]{:S(2)}) %collective-permute-start.12) | collective-permute-done | bytes 131104 | tf_op jit(solution)/shard_map/ppermute | solution.py:217
  65.7 1.6 %shard_map.43 = bf16[128,4096]{1,0:T(8,128)(2,1)} custom-call(s32[2]{0:T(128)S(1)} %pad_add_fusion.place, bf16[128,512]{1,0:T(8,128)(2,1)S(1)} %get-tuple-element.41.refs_0_, bf16[128,512]{1,0:T(8,128)(2,1)S(1)} %collective-permute-done.10.refs_1_, bf16[128,512]{1,0:T(8,128)(2,1)S(1)} %collective-permute-done.11.refs_2_, ...), custom_call_target="tpu_custom_call" | custom-call | tf_op jit(solution)/shard_map/pallas_call | solution.py:207
  (2 shorter events, 0.0 us)
Async XLA Ops:
  0.1 0.7 copy-start.2
  0.7 1.2 %copy-start = (bf16[128,4096]{1,0:T(8,128)(2,1)S(1)}, bf16[128,4096]{1,0:T(8,128)(2,1)}, u32[]{:S(2)}) copy-start(bf16[128,4096]{1,0:T(8,128)(2,1)} %q.1) | copy-start | bytes 3145732
  2.0 1.0 %copy-start.1 = (bf16[2,128,1024]{2,1,0:T(8,128)(2,1)S(1)}, bf16[2,128,1024]{2,1,0:T(8,128)(2,1)}, u32[]{:S(2)}) copy-start(bf16[2,128,1024]{2,1,0:T(8,128)(2,1)} %kv.1) | copy-start | bytes 1572868
  4.0 7.0 %collective-permute-start.3 = (bf16[528,128]{1,0:T(8,128)(2,1)S(1)}, bf16[528,128]{1,0:T(8,128)(2,1)S(1)}, u32[]{:S(2)}, u32[]{:S(2)}) collective-permute-start(bf16[528,128]{1,0:T(8,128)(2,1)S(1)} %get-tuple-element.34), channel_id=1, source_target_pairs={{0,2},{2,0},{4,6},{6,4},{8,10},{10,8},{12,14},{14,12},{16,18},{18,... | collective-permute-start | bytes 405512 | tf_op jit(solution)/shard_map/ppermute | solution.py:217
  7.0 7.9 %collective-permute-start.4 = (bf16[528,128]{1,0:T(8,128)(2,1)S(1)}, bf16[528,128]{1,0:T(8,128)(2,1)S(1)}, u32[]{:S(2)}, u32[]{:S(2)}) collective-permute-start(bf16[528,128]{1,0:T(8,128)(2,1)S(1)} %get-tuple-element.35), channel_id=1, source_target_pairs={{0,4},{2,6},{4,0},{6,2},{8,12},{10,14},{12,8},{14,10},{16,20},{18,... | collective-permute-start | bytes 405512 | tf_op jit(solution)/shard_map/ppermute | solution.py:217
  8.6 6.4 %collective-permute-start.5 = (bf16[528,128]{1,0:T(8,128)(2,1)S(1)}, bf16[528,128]{1,0:T(8,128)(2,1)S(1)}, u32[]{:S(2)}, u32[]{:S(2)}) collective-permute-start(bf16[528,128]{1,0:T(8,128)(2,1)S(1)} %get-tuple-element.36), channel_id=1, source_target_pairs={{0,6},{2,4},{4,2},{6,0},{8,14},{10,12},{12,10},{14,8},{16,22},{18,... | collective-permute-start | bytes 405512 | tf_op jit(solution)/shard_map/ppermute | solution.py:217
  15.0 14.1 %collective-permute-start.8 = (bf16[816,128]{1,0:T(8,128)(2,1)S(1)}, bf16[816,128]{1,0:T(8,128)(2,1)S(1)}, u32[]{:S(2)}, u32[]{:S(2)}) collective-permute-start(bf16[816,128]{1,0:T(8,128)(2,1)S(1)} %get-tuple-element.37), channel_id=1, source_target_pairs={{0,8},{2,10},{4,12},{6,14},{8,16},{10,18},{12,20},{14,22},{16,24},... | collective-permute-start | bytes 626696 | tf_op jit(solution)/shard_map/ppermute | solution.py:220
  18.5 9.2 %collective-permute-start.6 = (bf16[528,128]{1,0:T(8,128)(2,1)S(1)}, bf16[528,128]{1,0:T(8,128)(2,1)S(1)}, u32[]{:S(2)}, u32[]{:S(2)}) collective-permute-start(bf16[528,128]{1,0:T(8,128)(2,1)S(1)} %get-tuple-element.33.refs_4_), channel_id=1, source_target_pairs={{0,8},{2,10},{4,12},{6,14},{8,16},{10,18},{12,20},{14,22},{16,24},... | collective-permute-start | bytes 405512 | tf_op jit(solution)/shard_map/ppermute | solution.py:220
  22.0 13.4 %collective-permute-start = (bf16[128,1024]{1,0:T(8,128)(2,1)S(1)}, bf16[128,1024]{1,0:T(8,128)(2,1)S(1)}, u32[]{:S(2)}, u32[]{:S(2)}) collective-permute-start(bf16[128,1024]{1,0:T(8,128)(2,1)S(1)} %get-tuple-element.30), channel_id=1, source_target_pairs={{0,2},{2,0},{4,6},{6,4},{8,10},{10,8},{12,14},{14,12},{16,18},{18,... | collective-permute-start | bytes 786440 | tf_op jit(solution)/shard_map/ppermute | solution.py:217
  23.3 8.0 %collective-permute-start.13 = (bf16[768,128]{1,0:T(8,128)(2,1)S(1)}, bf16[768,128]{1,0:T(8,128)(2,1)S(1)}, u32[]{:S(2)}, u32[]{:S(2)}) collective-permute-start(bf16[768,128]{1,0:T(8,128)(2,1)S(1)} %get-tuple-element.45), channel_id=1, source_target_pairs={{0,8},{2,10},{4,12},{6,14},{8,16},{10,18},{12,20},{14,22},{16,24},... | collective-permute-start | bytes 589832 | tf_op jit(solution)/shard_map/ppermute | solution.py:220
  26.8 12.8 %collective-permute-start.1 = (bf16[128,1024]{1,0:T(8,128)(2,1)S(1)}, bf16[128,1024]{1,0:T(8,128)(2,1)S(1)}, u32[]{:S(2)}, u32[]{:S(2)}) collective-permute-start(bf16[128,1024]{1,0:T(8,128)(2,1)S(1)} %get-tuple-element.31), channel_id=1, source_target_pairs={{0,4},{2,6},{4,0},{6,2},{8,12},{10,14},{12,8},{14,10},{16,20},{18,... | collective-permute-start | bytes 786440 | tf_op jit(solution)/shard_map/ppermute | solution.py:217
  27.7 12.0 %collective-permute-start.2 = (bf16[128,1024]{1,0:T(8,128)(2,1)S(1)}, bf16[128,1024]{1,0:T(8,128)(2,1)S(1)}, u32[]{:S(2)}, u32[]{:S(2)}) collective-permute-start(bf16[128,1024]{1,0:T(8,128)(2,1)S(1)} %get-tuple-element.32), channel_id=1, source_target_pairs={{0,6},{2,4},{4,2},{6,0},{8,14},{10,12},{12,10},{14,8},{16,22},{18,... | collective-permute-start | bytes 786440 | tf_op jit(solution)/shard_map/ppermute | solution.py:217
  29.1 15.0 %collective-permute-start.9 = (bf16[816,128]{1,0:T(8,128)(2,1)S(1)}, bf16[816,128]{1,0:T(8,128)(2,1)S(1)}, u32[]{:S(2)}, u32[]{:S(2)}) collective-permute-start(bf16[816,128]{1,0:T(8,128)(2,1)S(1)} %collective-permute-done.8.refs_9_.refs_10_), channel_id=1, source_target_pairs={{0,8},{2,10},{4,12},{6,14},{8,16},{10,18},{12,20},{14,22},{16,24},... | collective-permute-start | bytes 626696 | tf_op jit(solution)/shard_map/ppermute | solution.py:220
  31.3 12.8 %collective-permute-start.14 = (bf16[768,128]{1,0:T(8,128)(2,1)S(1)}, bf16[768,128]{1,0:T(8,128)(2,1)S(1)}, u32[]{:S(2)}, u32[]{:S(2)}) collective-permute-start(bf16[768,128]{1,0:T(8,128)(2,1)S(1)} %collective-permute-done.13.refs_9_), channel_id=1, source_target_pairs={{0,8},{2,10},{4,12},{6,14},{8,16},{10,18},{12,20},{14,22},{16,24},... | collective-permute-start | bytes 589832 | tf_op jit(solution)/shard_map/ppermute | solution.py:220
  35.4 8.7 %collective-permute-start.7 = (bf16[528,128]{1,0:T(8,128)(2,1)S(1)}, bf16[528,128]{1,0:T(8,128)(2,1)S(1)}, u32[]{:S(2)}, u32[]{:S(2)}) collective-permute-start(bf16[528,128]{1,0:T(8,128)(2,1)S(1)} %collective-permute-done.6.refs_8_), channel_id=1, source_target_pairs={{0,8},{2,10},{4,12},{6,14},{8,16},{10,18},{12,20},{14,22},{16,24},... | collective-permute-start | bytes 405512 | tf_op jit(solution)/shard_map/ppermute | solution.py:220
  46.9 12.9 %collective-permute-start.15 = (bf16[128,512]{1,0:T(8,128)(2,1)S(1)}, bf16[128,512]{1,0:T(8,128)(2,1)S(1)}, u32[]{:S(2)}, u32[]{:S(2)}) collective-permute-start(bf16[128,512]{1,0:T(8,128)(2,1)S(1)} %get-tuple-element.50), channel_id=1, source_target_pairs={{0,2},{2,0},{4,6},{6,4},{8,10},{10,8},{12,14},{14,12},{16,18},{18,... | collective-permute-start | bytes 393224 | tf_op jit(solution)/shard_map/ppermute | solution.py:217
  51.9 9.4 %collective-permute-start.16 = (bf16[128,512]{1,0:T(8,128)(2,1)S(1)}, bf16[128,512]{1,0:T(8,128)(2,1)S(1)}, u32[]{:S(2)}, u32[]{:S(2)}) collective-permute-start(bf16[128,512]{1,0:T(8,128)(2,1)S(1)} %get-tuple-element.51), channel_id=1, source_target_pairs={{0,4},{2,6},{4,0},{6,2},{8,12},{10,14},{12,8},{14,10},{16,20},{18,... | collective-permute-start | bytes 393224 | tf_op jit(solution)/shard_map/ppermute | solution.py:217
  53.5 7.8 %collective-permute-start.17 = (bf16[128,512]{1,0:T(8,128)(2,1)S(1)}, bf16[128,512]{1,0:T(8,128)(2,1)S(1)}, u32[]{:S(2)}, u32[]{:S(2)}) collective-permute-start(bf16[128,512]{1,0:T(8,128)(2,1)S(1)} %get-tuple-element.52), channel_id=1, source_target_pairs={{0,6},{2,4},{4,2},{6,0},{8,14},{10,12},{12,10},{14,8},{16,22},{18,... | collective-permute-start | bytes 393224 | tf_op jit(solution)/shard_map/ppermute | solution.py:217
  57.8 5.0 %collective-permute-start.10 = (bf16[128,512]{1,0:T(8,128)(2,1)S(1)}, bf16[128,512]{1,0:T(8,128)(2,1)S(1)}, u32[]{:S(2)}, u32[]{:S(2)}) collective-permute-start(bf16[128,512]{1,0:T(8,128)(2,1)S(1)} %get-tuple-element.42), channel_id=1, source_target_pairs={{0,2},{2,0},{4,6},{6,4},{8,10},{10,8},{12,14},{14,12},{16,18},{18,... | collective-permute-start | bytes 393224 | tf_op jit(solution)/shard_map/ppermute | solution.py:217
  58.4 5.0 %collective-permute-start.11 = (bf16[128,512]{1,0:T(8,128)(2,1)S(1)}, bf16[128,512]{1,0:T(8,128)(2,1)S(1)}, u32[]{:S(2)}, u32[]{:S(2)}) collective-permute-start(bf16[128,512]{1,0:T(8,128)(2,1)S(1)} %get-tuple-element.43), channel_id=1, source_target_pairs={{0,4},{2,6},{4,0},{6,2},{8,12},{10,14},{12,8},{14,10},{16,20},{18,... | collective-permute-start | bytes 393224 | tf_op jit(solution)/shard_map/ppermute | solution.py:217
  59.9 5.9 %collective-permute-start.12 = (bf16[128,512]{1,0:T(8,128)(2,1)S(1)}, bf16[128,512]{1,0:T(8,128)(2,1)S(1)}, u32[]{:S(2)}, u32[]{:S(2)}) collective-permute-start(bf16[128,512]{1,0:T(8,128)(2,1)S(1)} %get-tuple-element.44), channel_id=1, source_target_pairs={{0,6},{2,4},{4,2},{6,0},{8,14},{10,12},{12,10},{14,8},{16,22},{18,... | collective-permute-start | bytes 393224 | tf_op jit(solution)/shard_map/ppermute | solution.py:217

commit v2 on v1

v2 whole, which is shorter than its diff:
```python
import functools
import jax
import jax.numpy as jnp
from jax import lax
from jax.experimental import pallas as pl
from jax.experimental.pallas import tpu as pltpu
from jax.sharding import PartitionSpec as P

HQ = 32
HK = 8
DH = 128
WINDOW = 2048

GROUP = HQ // HK
NEG_BIG = -1e30
LOG2E = 1.4426950408889634
ID_ROWS = 16


def pack(place, kv, ids, q, *refs, size, chunks):
    kv_outs, q_outs, (ids_buf, sems) = refs[:size], refs[size : 2 * size], refs[2 * size :]
    rows = kv.shape[1]
    width = q_outs[0].shape[1]
    moves = [(ids, ids_buf)]
    for k in range(size):
        for c in range(chunks):
            start = pl.multiple_of(((place[0] ^ k) * chunks + c) * DH, DH)
            for part in range(2):
                first = (2 * c + part) * rows
                moves.append((kv.at[part, :, pl.ds(start, DH)], kv_outs[k].at[pl.ds(first, rows), :]))
    for k in range(size):
        moves.append((q.at[:, pl.ds(pl.multiple_of((place[0] ^ k) * width, width), width)], q_outs[k]))
    copies = [pltpu.make_async_copy(a, b, sems.at[n]) for n, (a, b) in enumerate(moves)]
    for copy in copies:
        copy.start()
    copies[0].wait()
    tag = jnp.broadcast_to(ids_buf[...].astype(jnp.float32), (ID_ROWS, rows)).astype(jnp.bfloat16)
    for k in range(size):
        kv_outs[k][2 * chunks * rows :, :] = tag
    for copy in copies[1:]:
        copy.wait()


def join(*refs, count, chunks, rows):
    outs = refs[count:]
    for n in range(count):
        for c in range(chunks):
            outs[c][2 * n * rows : 2 * (n + 1) * rows, :] = refs[n][2 * c * rows : 2 * (c + 1) * rows, :]
        outs[0][2 * count * rows + n * ID_ROWS : 2 * count * rows + (n + 1) * ID_ROWS, :] = refs[n][
            2 * chunks * rows :, :
        ]


def unpack(place, *refs, size, chunks):
    out, sems = refs[-2:]
    width = refs[0].shape[1]
    copies = []
    for c in range(chunks):
        for k in range(size):
            start = pl.multiple_of(((place[0] ^ k) * chunks + c) * width, width)
            n = c * size + k
            copies.append(pltpu.make_async_copy(refs[n], out.at[:, pl.ds(start, width)], sems.at[n]))
    for copy in copies:
        copy.start()
    for copy in copies:
        copy.wait()


def attend(place, *refs, chunk, size, chunks, rows, reach, steps, first, last):
    q_refs, near, refs = refs[:size], refs[size : 2 * size], refs[2 * size :]
    far = {}
    for d in steps:
        if d:
            count = 3 if chunk else 2
            far[d] = (refs[0], refs[1], refs[count - 1])
            refs = refs[count:]
    if not first:
        old_top_ref, old_sum_ref, old_acc_ref = refs[:3]
        refs = refs[3:]
    if last:
        outs, refs = refs[:size], refs[size:]
    else:
        top_ref, sum_ref, acc_ref = refs[:3]
        refs = refs[3:]
    q_buf, k_buf, v_buf, tag_buf, bias, s_buf, o_buf = refs
    wide = GROUP * rows
    member, block = place[0], place[1]
    tag_at = 2 * chunks * rows
    blocks = sorted(set(steps) | {0}, reverse=True)
    for k in range(size):
        spot = member ^ k
        for d in blocks:
            if d == 0 or k == 0:
                ref = near[k] if d == 0 else far[d][0]
                start, tag_ref, tag_row = 2 * chunk * rows, ref, tag_at
            else:
                ref, tag_ref = far[d][1], far[d][2]
                start, tag_row = 2 * (k - 1) * rows, 2 * (size - 1) * rows + (k - 1) * ID_ROWS
            at = pl.ds(pl.multiple_of((blocks.index(d) * size + spot) * rows, rows), rows)
            if d in steps:
                k_buf[at, :] = ref[start : start + rows, :]
                v_buf[at, :] = ref[start + rows : start + 2 * rows, :]
            tag = tag_ref[tag_row : tag_row + 1, :].astype(jnp.float32)
            if d:
                tag = jnp.where(block >= d, tag, -1.0)
            at = pl.ds(pl.multiple_of((blocks.index(d) * size + spot) * 8, 8), 8)
            tag_buf[at, :] = jnp.broadcast_to(tag, (8, rows))
        for h in range(GROUP):
            at = pl.ds(pl.multiple_of(spot * wide + h * rows, rows), rows)
            col = (chunk * GROUP + h) * DH
            q_buf[at, :] = q_refs[k][:, col : col + DH]
    ahead = lax.broadcasted_iota(jnp.int32, (rows, rows), 0) - lax.broadcasted_iota(jnp.int32, (rows, rows), 1)
    scale = DH**-0.5 * LOG2E
    for j in range(size):
        seen = []
        for d in steps:
            for n in range(size):
                apart = d * size + j - n
                if apart >= 0 and apart * rows - (rows - 1) < reach:
                    seen.append((blocks.index(d) * size + n, apart))
        seen.sort()
        low, high = seen[0][0] * rows, (seen[-1][0] + 1) * rows
        turn = j % 2
        spot = blocks.index(0) * size + j
        q_tag = jnp.broadcast_to(tag_buf[spot * 8 : spot * 8 + 1, :], (rows, rows)).T
        for spot, apart in seen:
            allowed = q_tag == jnp.broadcast_to(tag_buf[spot * 8 : spot * 8 + 1, :], (rows, rows))
            if apart == 0:
                allowed = allowed & (ahead >= 0)
            if apart * rows + rows > WINDOW:
                allowed = allowed & (ahead + apart * rows < WINDOW)
            bias[turn, :, spot * rows : (spot + 1) * rows] = jnp.where(allowed, 0.0, NEG_BIG)
        q4 = q_buf[j * wide : (j + 1) * wide, :]
        tiles = [(t, min(256, high - t)) for t in range(low, high, 256)]
        top = None
        for t, w in tiles:
            s = lax.dot_general(
                q4, k_buf[t : t + w, :], (((1,), (1,)), ((), ())), preferred_element_type=jnp.float32
            )
            s = s + jnp.concatenate([bias[turn, :, t : t + w]] * GROUP, axis=0)
            s_buf[turn, :, t : t + w] = s
            for u in range(0, w, DH):
                part = s[:, u : u + DH]
                top = part if top is None else jnp.maximum(top, part)
        top = jnp.broadcast_to(jnp.max(top, axis=1, keepdims=True), (wide, DH))
        if not first:
            old_top = old_top_ref[j]
            top = jnp.maximum(top, old_top)
        total = acc = None
        for t, w in tiles:
            parts = []
            for u in range(t, t + w, DH):
                part = jnp.exp2((s_buf[turn, :, u : u + DH] - top) * scale)
                total = part if total is None else total + part
                parts.append(part.astype(jnp.bfloat16))
            add = jnp.dot(jnp.concatenate(parts, axis=1), v_buf[t : t + w, :], preferred_element_type=jnp.float32)
            acc = add if acc is None else acc + add
        total = jnp.broadcast_to(jnp.sum(total, axis=1, keepdims=True), (wide, DH))
        if not first:
            rescale = jnp.exp2((old_top - top) * scale)
            total = total + old_sum_ref[j] * rescale
            acc = acc + old_acc_ref[j] * rescale
        if last:
            result = (acc / total).astype(jnp.bfloat16)
            for h in range(GROUP):
                o_buf[j * rows : (j + 1) * rows, h * DH : (h + 1) * DH] = result[h * rows : (h + 1) * rows, :]
        else:
            top_ref[j] = top
            sum_ref[j] = total
            acc_ref[j] = acc
    if last:
        for k in range(size):
            outs[k][...] = o_buf[pl.ds(pl.multiple_of((member ^ k) * rows, rows), rows), :]


def scratch_of(size, rows, steps):
    spots = len(set(steps) | {0}) * size
    keys = spots * rows
    return [
        pltpu.VMEM((size * GROUP * rows, DH), jnp.bfloat16),
        pltpu.VMEM((keys, DH), jnp.bfloat16),
        pltpu.VMEM((keys, DH), jnp.bfloat16),
        pltpu.VMEM((spots * 8, rows), jnp.float32),
        pltpu.VMEM((2, rows, keys), jnp.float32),
        pltpu.VMEM((2, GROUP * rows, keys), jnp.float32),
        pltpu.VMEM((size * rows, GROUP * DH), jnp.bfloat16),
    ]


def layout_of(shards, rows):
    size = 1
    while (2 * size) ** 2 <= shards and 2 * size <= HK:
        size *= 2
    reach = min(WINDOW, rows * shards // 2)
    back = min(-(-(reach - 1) // (size * rows)), shards // size - 1)
    return size, HK // size, back, reach


def local(queries, keys_values, segment_ids, shards):
    rows = queries.shape[0]
    size, chunks, back, reach = layout_of(shards, rows)
    width = GROUP * DH
    me = lax.axis_index("seq")
    place = jnp.stack([me & (size - 1), me >> (size.bit_length() - 1)]).astype(jnp.int32)
    smem = pl.BlockSpec(memory_space=pltpu.SMEM)
    vmem = pl.BlockSpec(memory_space=pltpu.VMEM)
    hbm = pl.BlockSpec(memory_space=pltpu.HBM)
    params = pltpu.CompilerParams(vmem_limit_bytes=48 * 1024 * 1024)
    bf16 = functools.partial(jax.ShapeDtypeStruct, dtype=jnp.bfloat16)
    f32 = functools.partial(jax.ShapeDtypeStruct, dtype=jnp.float32)

    def call(body, shapes, args, scratch=(), far_in=(), far_out=False):
        return pl.pallas_call(
            body,
            in_specs=[smem if a is place else hbm if n in far_in else vmem for n, a in enumerate(args)],
            out_specs=[hbm if far_out else vmem] * len(shapes),
            out_shape=shapes,
            scratch_shapes=scratch,
            compiler_params=params,
        )(*[pltpu.with_memory_space_constraint(a, pltpu.HBM) if n in far_in else a for n, a in enumerate(args)])

    def swap(x, k):
        return lax.ppermute(x, "seq", [(i, i ^ k) for i in range(shards)]) if k else x

    def onward(x, d):
        return lax.ppermute(x, "seq", [(i, i + size) for i in range((d - 1) * size, shards - size)])

    packed = call(
        functools.partial(pack, size=size, chunks=chunks),
        [bf16((2 * chunks * rows + ID_ROWS, DH))] * size + [bf16((rows, chunks * width))] * size,
        [place, keys_values, segment_ids.reshape(1, rows), queries],
        [pltpu.VMEM((1, rows), jnp.int32), pltpu.SemaphoreType.DMA((1 + 2 * HK + size,))],
        far_in=(1, 2, 3),
    )
    sent, q_sent = packed[:size], packed[size:]
    near = [swap(sent[k], k) for k in range(size)]
    q_parts = [swap(q_sent[k], k) for k in range(size)]
    count = size - 1
    rest_shapes = [bf16((count * (2 * rows + (0 if c else ID_ROWS)), DH)) for c in range(chunks)]
    far_own, far_rest = [sent[0]], []
    if back:
        far_rest.append(call(functools.partial(join, count=count, chunks=chunks, rows=rows), rest_shapes, near[1:]))
    for d in range(1, back + 1):
        far_own.append(onward(far_own[d - 1], d))
        far_rest.append([onward(far_rest[d - 1][c], d) for c in range(chunks)])

    def stage(c, steps, state, first, last):
        args = [place] + q_parts + near
        for d in steps:
            if d:
                args += [far_own[d], far_rest[d][c]] + ([far_rest[d][0]] if c else [])
        args += list(state)
        shapes = [bf16((rows, width))] * size if last else [f32((size, GROUP * rows, DH))] * 3
        scratch = scratch_of(size, rows, steps)
        body = functools.partial(
            attend, chunk=c, size=size, chunks=chunks, rows=rows, reach=reach, steps=steps, first=first, last=last
        )
        return call(body, shapes, args, scratch)

    states = [()] * chunks
    if back:
        states = [stage(c, tuple(range(back)), (), True, False) for c in range(chunks)]
    done = []
    for c in range(chunks):
        result = stage(c, (back,), states[c], not back, True)
        done += [swap(result[k], k) for k in range(size)]
    return call(
        functools.partial(unpack, size=size, chunks=chunks),
        [bf16(queries.shape)],
        [place] + done,
        [pltpu.SemaphoreType.DMA((len(done),))],
        far_out=True,
    )[0]


def solution(mesh):
    shards = mesh.shape["seq"]

    def body(queries, keys_values, segment_ids):
        return local(queries, keys_values, segment_ids, shards)

    return jax.shard_map(
        body,
        mesh=mesh,
        in_specs=(P(("rep", "seq"), None), P(None, ("rep", "seq"), None), P(("rep", "seq"))),
        out_specs=P(("rep", "seq"), None),
        check_vma=False,
    )
```

time: 67.6 us -> 61.6 us (0.911)
  starting transfers between devices: 36.3 us -> 27.8 us
  waiting for transfers between devices: 10.9 us -> 17.5 us
  local copies, waits for them, and re-layouts: 2.92 us -> 0 us
  Pallas kernels: 17 us -> 15.9 us
    ppermute x6, starting transfers between devices: 20.9 us -> 12.4 us  [onward(): lax.ppermute(x, 'seq', [(i, i + size) for i in range((d - 1) * size, shar...]
    ppermute x12, waiting for transfers between devices: 10.8 us -> 17.3 us  [swap(): lax.ppermute(x, 'seq', [(i, i ^ k) for i in range(shards)])]
    unnamed x6 -> x0, local copies, waits for them, and re-layouts: 2.92 us -> none
    pallas_call x7, Pallas kernels: 17 us -> 15.9 us  [call(): pl.pallas_call(body, in_specs=[smem if a is place else hbm if n in far_in...]
  transfers between devices with their start and end apart: 18 -> 18, of which waited for: 5 -> 7; matrix products, arithmetic and copies ran while one was open for 0% -> 0% of each run, Pallas kernels for 17% -> 16%
where the time goes in v2:
time: 61.6 us; the launch traced here: 61.4 us
  starting transfers between devices  27.8 us (45%)
  waiting for transfers between devices  17.5 us (28%)
  Pallas kernels  15.9 us (26%)
    ppermute x12, waiting for transfers between devices, swap(): lax.ppermute(x, 'seq', [(i, i ^ k) for i in range(shards)])  17.3 us
    pallas_call x7, Pallas kernels, call(): pl.pallas_call(body, in_specs=[smem if a is place else hbm if n in far_in...  15.9 us
    ppermute x12, starting transfers between devices, swap(): lax.ppermute(x, 'seq', [(i, i ^ k) for i in range(shards)])  15.4 us
    ppermute x6, starting transfers between devices, onward(): lax.ppermute(x, 'seq', [(i, i + size) for i in range((d - 1) * size, shar...  12.4 us
  transfers between devices with their start and end apart: 18, of which 7 were waited for; matrix products, arithmetic and copies ran while one was open for 0% of the time, Pallas kernels for 16%

profile of v2, /device:TPU:0, one launch (start us, length us, event | category | flops | bytes accessed | tf_op | source)
XLA Modules:
  0.0 61.4 jit_solution(15228609483416826019)
XLA Ops:
  0.0 0.1 pad_add_fusion.place
  0.1 2.2 %shard_map.37 = (bf16[528,128]{1,0:T(8,128)(2,1)S(1)}, bf16[528,128]{1,0:T(8,128)(2,1)S(1)}, bf16[528,128]{1,0:T(8,128)(2,1)S(1)}, bf16[528,128]{1,0:T(8,128)(2,...) custom-call(s32[2]{0:T(128)S(1)} %pad_add_fusion.place, ...), custom_call_target="tpu_custom_call" | custom-call | tf_op jit(solution)/shard_map/pallas_call | solution.py:213
  2.3 3.0 %collective-permute-start.3 = (bf16[528,128]{1,0:T(8,128)(2,1)S(1)}, bf16[528,128]{1,0:T(8,128)(2,1)S(1)}, u32[]{:S(2)}, u32[]{:S(2)}) collective-permute-start(bf16[528,128]{1,0:T(8,128)(2,1)S(1)} %get-tuple-element.34), channel_id=1, source_target_pairs={{0,2},{2,0},{4,6},{6,4},{8,10},{10,8},{12,14},{14,12},{16,18},{18,... | collective-permute-start | bytes 405512 | tf_op jit(solution)/shard_map/ppermute | solution.py:223
  5.3 1.5 %collective-permute-start.4 = (bf16[528,128]{1,0:T(8,128)(2,1)S(1)}, bf16[528,128]{1,0:T(8,128)(2,1)S(1)}, u32[]{:S(2)}, u32[]{:S(2)}) collective-permute-start(bf16[528,128]{1,0:T(8,128)(2,1)S(1)} %get-tuple-element.35), channel_id=1, source_target_pairs={{0,4},{2,6},{4,0},{6,2},{8,12},{10,14},{12,8},{14,10},{16,20},{18,... | collective-permute-start | bytes 405512 | tf_op jit(solution)/shard_map/ppermute | solution.py:223
  6.9 0.0 collective-permute-start.5
  6.9 2.4 %collective-permute-done.3.refs_0_.refs_5_ = bf16[528,128]{1,0:T(8,128)(2,1)S(1)} collective-permute-done((bf16[528,128]{1,0:T(8,128)(2,1)S(1)}, bf16[528,128]{1,0:T(8,128)(2,1)S(1)}, u32[]{:S(2)}, u32[]{:S(2)}) %collective-permute-start.3) | collective-permute-done | bytes 135200 | tf_op jit(solution)/shard_map/ppermute | solution.py:223
  9.3 4.0 %collective-permute-done.4.refs_1_.refs_6_ = bf16[528,128]{1,0:T(8,128)(2,1)S(1)} collective-permute-done((bf16[528,128]{1,0:T(8,128)(2,1)S(1)}, bf16[528,128]{1,0:T(8,128)(2,1)S(1)}, u32[]{:S(2)}, u32[]{:S(2)}) %collective-permute-start.4) | collective-permute-done | bytes 135200 | tf_op jit(solution)/shard_map/ppermute | solution.py:223
  13.3 0.0 collective-permute-done.5.refs_2_.refs_7_
  13.3 3.5 %collective-permute-start.8 = (bf16[816,128]{1,0:T(8,128)(2,1)S(1)}, bf16[816,128]{1,0:T(8,128)(2,1)S(1)}, u32[]{:S(2)}, u32[]{:S(2)}) collective-permute-start(bf16[816,128]{1,0:T(8,128)(2,1)S(1)} %get-tuple-element.37), channel_id=1, source_target_pairs={{0,8},{2,10},{4,12},{6,14},{8,16},{10,18},{12,20},{14,22},{16,24},... | collective-permute-start | bytes 626696 | tf_op jit(solution)/shard_map/ppermute | solution.py:226
  16.8 3.5 %collective-permute-start.6 = (bf16[528,128]{1,0:T(8,128)(2,1)S(1)}, bf16[528,128]{1,0:T(8,128)(2,1)S(1)}, u32[]{:S(2)}, u32[]{:S(2)}) collective-permute-start(bf16[528,128]{1,0:T(8,128)(2,1)S(1)} %get-tuple-element.33.refs_4_), channel_id=1, source_target_pairs={{0,8},{2,10},{4,12},{6,14},{8,16},{10,18},{12,20},{14,22},{16,24},... | collective-permute-start | bytes 405512 | tf_op jit(solution)/shard_map/ppermute | solution.py:226
  20.3 1.3 %collective-permute-start = (bf16[128,1024]{1,0:T(8,128)(2,1)S(1)}, bf16[128,1024]{1,0:T(8,128)(2,1)S(1)}, u32[]{:S(2)}, u32[]{:S(2)}) collective-permute-start(bf16[128,1024]{1,0:T(8,128)(2,1)S(1)} %get-tuple-element.30), channel_id=1, source_target_pairs={{0,2},{2,0},{4,6},{6,4},{8,10},{10,8},{12,14},{14,12},{16,18},{18,... | collective-permute-start | bytes 786440 | tf_op jit(solution)/shard_map/ppermute | solution.py:223
  21.6 3.5 %collective-permute-start.13 = (bf16[768,128]{1,0:T(8,128)(2,1)S(1)}, bf16[768,128]{1,0:T(8,128)(2,1)S(1)}, u32[]{:S(2)}, u32[]{:S(2)}) collective-permute-start(bf16[768,128]{1,0:T(8,128)(2,1)S(1)} %get-tuple-element.45), channel_id=1, source_target_pairs={{0,8},{2,10},{4,12},{6,14},{8,16},{10,18},{12,20},{14,22},{16,24},... | collective-permute-start | bytes 589832 | tf_op jit(solution)/shard_map/ppermute | solution.py:226
  25.1 0.9 %collective-permute-start.1 = (bf16[128,1024]{1,0:T(8,128)(2,1)S(1)}, bf16[128,1024]{1,0:T(8,128)(2,1)S(1)}, u32[]{:S(2)}, u32[]{:S(2)}) collective-permute-start(bf16[128,1024]{1,0:T(8,128)(2,1)S(1)} %get-tuple-element.31), channel_id=1, source_target_pairs={{0,4},{2,6},{4,0},{6,2},{8,12},{10,14},{12,8},{14,10},{16,20},{18,... | collective-permute-start | bytes 786440 | tf_op jit(solution)/shard_map/ppermute | solution.py:223
  26.0 0.0 collective-permute-done.6.refs_8_
  26.0 1.4 %collective-permute-start.2 = (bf16[128,1024]{1,0:T(8,128)(2,1)S(1)}, bf16[128,1024]{1,0:T(8,128)(2,1)S(1)}, u32[]{:S(2)}, u32[]{:S(2)}) collective-permute-start(bf16[128,1024]{1,0:T(8,128)(2,1)S(1)} %get-tuple-element.32), channel_id=1, source_target_pairs={{0,6},{2,4},{4,2},{6,0},{8,14},{10,12},{12,10},{14,8},{16,22},{18,... | collective-permute-start | bytes 786440 | tf_op jit(solution)/shard_map/ppermute | solution.py:223
  27.4 0.0 collective-permute-done.8.refs_9_.refs_10_
  27.4 0.7 %collective-permute-start.9 = (bf16[816,128]{1,0:T(8,128)(2,1)S(1)}, bf16[816,128]{1,0:T(8,128)(2,1)S(1)}, u32[]{:S(2)}, u32[]{:S(2)}) collective-permute-start(bf16[816,128]{1,0:T(8,128)(2,1)S(1)} %collective-permute-done.8.refs_9_.refs_10_), channel_id=1, source_target_pairs={{8,16},{10,18},{12,20},{14,22},{16,24},{18,26},{20,28},{22,30},{9,... | collective-permute-start | bytes 626696 | tf_op jit(solution)/shard_map/ppermute | solution.py:226
  28.1 0.2 collective-permute-done.13.refs_9_
  28.3 0.7 %collective-permute-start.14 = (bf16[768,128]{1,0:T(8,128)(2,1)S(1)}, bf16[768,128]{1,0:T(8,128)(2,1)S(1)}, u32[]{:S(2)}, u32[]{:S(2)}) collective-permute-start(bf16[768,128]{1,0:T(8,128)(2,1)S(1)} %collective-permute-done.13.refs_9_), channel_id=1, source_target_pairs={{8,16},{10,18},{12,20},{14,22},{16,24},{18,26},{20,28},{22,30},{9,... | collective-permute-start | bytes 589832 | tf_op jit(solution)/shard_map/ppermute | solution.py:226
  28.9 0.0 collective-permute-done.refs_1_
  28.9 0.7 %collective-permute-start.7 = (bf16[528,128]{1,0:T(8,128)(2,1)S(1)}, bf16[528,128]{1,0:T(8,128)(2,1)S(1)}, u32[]{:S(2)}, u32[]{:S(2)}) collective-permute-start(bf16[528,128]{1,0:T(8,128)(2,1)S(1)} %collective-permute-done.6.refs_8_), channel_id=1, source_target_pairs={{8,16},{10,18},{12,20},{14,22},{16,24},{18,26},{20,28},{22,30},{9,... | collective-permute-start | bytes 405512 | tf_op jit(solution)/shard_map/ppermute | solution.py:226
  29.6 7.2 %collective-permute-done.1.refs_2_ = bf16[128,1024]{1,0:T(8,128)(2,1)S(1)} collective-permute-done((bf16[128,1024]{1,0:T(8,128)(2,1)S(1)}, bf16[128,1024]{1,0:T(8,128)(2,1)S(1)}, u32[]{:S(2)}, u32[]{:S(2)}) %collective-permute-start.1) | collective-permute-done | bytes 262176 | tf_op jit(solution)/shard_map/ppermute | solution.py:223
  36.8 0.0 collective-permute-done.2.refs_3_
  36.8 3.9 %shard_map.41 = (f32[4,512,128]{2,1,0:T(8,128)S(1)}, f32[4,512,128]{2,1,0:T(8,128)S(1)}, f32[4,512,128]{2,1,0:T(8,128)S(1)}) custom-call(s32[2]{0:T(128)S(1)} %pad_add_fusion.place, bf16[128,1024]{1,0:T(8,128)(2,1)S(1)} %get-tuple-element.29.refs_0_, bf16[128,1024]{1,0:T(8,128)(2,1)S(1)} %collective-permute-done.refs_1_, ...), custom_call_target="tpu_custom_call" | custom-call | tf_op jit(solution)/shard_map/pallas_call | solution.py:213
  40.7 0.0 collective-permute-done.7.refs_8_
  40.7 0.0 collective-permute-done.14.refs_9_
  40.7 0.0 collective-permute-done.9.refs_9_.refs_10_
  40.7 2.2 %shard_map.42 = (bf16[128,512]{1,0:T(8,128)(2,1)S(1)}, bf16[128,512]{1,0:T(8,128)(2,1)S(1)}, bf16[128,512]{1,0:T(8,128)(2,1)S(1)}, bf16[128,512]{1,0:T(8,128)(2,1)S(1)}) custom-call(s32[2]{0:T(128)S(1)} %pad_add_fusion.place, bf16[128,1024]{1,0:T(8,128)(2,1)S(1)} %get-tuple-element.29.refs_0_, bf16[128,1024]{1,0:T(8,128)(2,1)S(1)} %collective-permute-done.refs_1_, ...), custom_call_target="tpu_custom_call" | custom-call | tf_op jit(solution)/shard_map/pallas_call | solution.py:213
  42.9 0.6 collective-permute-start.15
  43.5 3.9 %shard_map.39 = (f32[4,512,128]{2,1,0:T(8,128)S(1)}, f32[4,512,128]{2,1,0:T(8,128)S(1)}, f32[4,512,128]{2,1,0:T(8,128)S(1)}) custom-call(s32[2]{0:T(128)S(1)} %pad_add_fusion.place, bf16[128,1024]{1,0:T(8,128)(2,1)S(1)} %get-tuple-element.29.refs_0_, bf16[128,1024]{1,0:T(8,128)(2,1)S(1)} %collective-permute-done.refs_1_, ...), custom_call_target="tpu_custom_call" | custom-call | tf_op jit(solution)/shard_map/pallas_call | solution.py:213
  47.4 0.8 %collective-permute-start.16 = (bf16[128,512]{1,0:T(8,128)(2,1)S(1)}, bf16[128,512]{1,0:T(8,128)(2,1)S(1)}, u32[]{:S(2)}, u32[]{:S(2)}) collective-permute-start(bf16[128,512]{1,0:T(8,128)(2,1)S(1)} %get-tuple-element.51), channel_id=1, source_target_pairs={{0,4},{2,6},{4,0},{6,2},{8,12},{10,14},{12,8},{14,10},{16,20},{18,... | collective-permute-start | bytes 393224 | tf_op jit(solution)/shard_map/ppermute | solution.py:223
  48.2 2.2 %collective-permute-start.17 = (bf16[128,512]{1,0:T(8,128)(2,1)S(1)}, bf16[128,512]{1,0:T(8,128)(2,1)S(1)}, u32[]{:S(2)}, u32[]{:S(2)}) collective-permute-start(bf16[128,512]{1,0:T(8,128)(2,1)S(1)} %get-tuple-element.52), channel_id=1, source_target_pairs={{0,6},{2,4},{4,2},{6,0},{8,14},{10,12},{12,10},{14,8},{16,22},{18,... | collective-permute-start | bytes 393224 | tf_op jit(solution)/shard_map/ppermute | solution.py:223
  50.4 2.2 %shard_map.40 = (bf16[128,512]{1,0:T(8,128)(2,1)S(1)}, bf16[128,512]{1,0:T(8,128)(2,1)S(1)}, bf16[128,512]{1,0:T(8,128)(2,1)S(1)}, bf16[128,512]{1,0:T(8,128)(2,1)S(1)}) custom-call(s32[2]{0:T(128)S(1)} %pad_add_fusion.place, bf16[128,1024]{1,0:T(8,128)(2,1)S(1)} %get-tuple-element.29.refs_0_, bf16[128,1024]{1,0:T(8,128)(2,1)S(1)} %collective-permute-done.refs_1_, ...), custom_call_target="tpu_custom_call" | custom-call | tf_op jit(solution)/shard_map/pallas_call | solution.py:213
  52.6 0.6 collective-permute-start.10
  53.2 0.8 %collective-permute-start.11 = (bf16[128,512]{1,0:T(8,128)(2,1)S(1)}, bf16[128,512]{1,0:T(8,128)(2,1)S(1)}, u32[]{:S(2)}, u32[]{:S(2)}) collective-permute-start(bf16[128,512]{1,0:T(8,128)(2,1)S(1)} %get-tuple-element.43), channel_id=1, source_target_pairs={{0,4},{2,6},{4,0},{6,2},{8,12},{10,14},{12,8},{14,10},{16,20},{18,... | collective-permute-start | bytes 393224 | tf_op jit(solution)/shard_map/ppermute | solution.py:223
  53.9 0.0 collective-permute-done.15.refs_5_
  53.9 2.2 %collective-permute-start.12 = (bf16[128,512]{1,0:T(8,128)(2,1)S(1)}, bf16[128,512]{1,0:T(8,128)(2,1)S(1)}, u32[]{:S(2)}, u32[]{:S(2)}) collective-permute-start(bf16[128,512]{1,0:T(8,128)(2,1)S(1)} %get-tuple-element.44), channel_id=1, source_target_pairs={{0,6},{2,4},{4,2},{6,0},{8,14},{10,12},{12,10},{14,8},{16,22},{18,... | collective-permute-start | bytes 393224 | tf_op jit(solution)/shard_map/ppermute | solution.py:223
  56.2 0.0 collective-permute-done.16.refs_6_
  56.2 0.0 collective-permute-done.17.refs_7_
  56.2 1.8 %collective-permute-done.10.refs_1_ = bf16[128,512]{1,0:T(8,128)(2,1)S(1)} collective-permute-done((bf16[128,512]{1,0:T(8,128)(2,1)S(1)}, bf16[128,512]{1,0:T(8,128)(2,1)S(1)}, u32[]{:S(2)}, u32[]{:S(2)}) %collective-permute-start.10) | collective-permute-done | bytes 131104 | tf_op jit(solution)/shard_map/ppermute | solution.py:223
  58.0 0.2 collective-permute-done.11.refs_2_
  58.2 1.6 %collective-permute-done.12.refs_3_ = bf16[128,512]{1,0:T(8,128)(2,1)S(1)} collective-permute-done((bf16[128,512]{1,0:T(8,128)(2,1)S(1)}, bf16[128,512]{1,0:T(8,128)(2,1)S(1)}, u32[]{:S(2)}, u32[]{:S(2)}) %collective-permute-start.12) | collective-permute-done | bytes 131104 | tf_op jit(solution)/shard_map/ppermute | solution.py:223
  59.8 1.6 %shard_map.43 = bf16[128,4096]{1,0:T(8,128)(2,1)} custom-call(s32[2]{0:T(128)S(1)} %pad_add_fusion.place, bf16[128,512]{1,0:T(8,128)(2,1)S(1)} %get-tuple-element.41.refs_0_, bf16[128,512]{1,0:T(8,128)(2,1)S(1)} %collective-permute-done.10.refs_1_, bf16[128,512]{1,0:T(8,128)(2,1)S(1)} %collective-permute-done.11.refs_2_, ...), custom_call_target="tpu_custom_call" | custom-call | tf_op jit(solution)/shard_map/pallas_call | solution.py:213
  (1 shorter events, 0.0 us)
Async XLA Ops:
  2.3 7.0 %collective-permute-start.3 = (bf16[528,128]{1,0:T(8,128)(2,1)S(1)}, bf16[528,128]{1,0:T(8,128)(2,1)S(1)}, u32[]{:S(2)}, u32[]{:S(2)}) collective-permute-start(bf16[528,128]{1,0:T(8,128)(2,1)S(1)} %get-tuple-element.34), channel_id=1, source_target_pairs={{0,2},{2,0},{4,6},{6,4},{8,10},{10,8},{12,14},{14,12},{16,18},{18,... | collective-permute-start | bytes 405512 | tf_op jit(solution)/shard_map/ppermute | solution.py:223
  5.3 7.9 %collective-permute-start.4 = (bf16[528,128]{1,0:T(8,128)(2,1)S(1)}, bf16[528,128]{1,0:T(8,128)(2,1)S(1)}, u32[]{:S(2)}, u32[]{:S(2)}) collective-permute-start(bf16[528,128]{1,0:T(8,128)(2,1)S(1)} %get-tuple-element.35), channel_id=1, source_target_pairs={{0,4},{2,6},{4,0},{6,2},{8,12},{10,14},{12,8},{14,10},{16,20},{18,... | collective-permute-start | bytes 405512 | tf_op jit(solution)/shard_map/ppermute | solution.py:223
  6.9 6.4 %collective-permute-start.5 = (bf16[528,128]{1,0:T(8,128)(2,1)S(1)}, bf16[528,128]{1,0:T(8,128)(2,1)S(1)}, u32[]{:S(2)}, u32[]{:S(2)}) collective-permute-start(bf16[528,128]{1,0:T(8,128)(2,1)S(1)} %get-tuple-element.36), channel_id=1, source_target_pairs={{0,6},{2,4},{4,2},{6,0},{8,14},{10,12},{12,10},{14,8},{16,22},{18,... | collective-permute-start | bytes 405512 | tf_op jit(solution)/shard_map/ppermute | solution.py:223
  13.3 14.1 %collective-permute-start.8 = (bf16[816,128]{1,0:T(8,128)(2,1)S(1)}, bf16[816,128]{1,0:T(8,128)(2,1)S(1)}, u32[]{:S(2)}, u32[]{:S(2)}) collective-permute-start(bf16[816,128]{1,0:T(8,128)(2,1)S(1)} %get-tuple-element.37), channel_id=1, source_target_pairs={{0,8},{2,10},{4,12},{6,14},{8,16},{10,18},{12,20},{14,22},{16,24},... | collective-permute-start | bytes 626696 | tf_op jit(solution)/shard_map/ppermute | solution.py:226
  16.8 9.2 %collective-permute-start.6 = (bf16[528,128]{1,0:T(8,128)(2,1)S(1)}, bf16[528,128]{1,0:T(8,128)(2,1)S(1)}, u32[]{:S(2)}, u32[]{:S(2)}) collective-permute-start(bf16[528,128]{1,0:T(8,128)(2,1)S(1)} %get-tuple-element.33.refs_4_), channel_id=1, source_target_pairs={{0,8},{2,10},{4,12},{6,14},{8,16},{10,18},{12,20},{14,22},{16,24},... | collective-permute-start | bytes 405512 | tf_op jit(solution)/shard_map/ppermute | solution.py:226
  20.3 8.6 %collective-permute-start = (bf16[128,1024]{1,0:T(8,128)(2,1)S(1)}, bf16[128,1024]{1,0:T(8,128)(2,1)S(1)}, u32[]{:S(2)}, u32[]{:S(2)}) collective-permute-start(bf16[128,1024]{1,0:T(8,128)(2,1)S(1)} %get-tuple-element.30), channel_id=1, source_target_pairs={{0,2},{2,0},{4,6},{6,4},{8,10},{10,8},{12,14},{14,12},{16,18},{18,... | collective-permute-start | bytes 786440 | tf_op jit(solution)/shard_map/ppermute | solution.py:223
  21.6 6.6 %collective-permute-start.13 = (bf16[768,128]{1,0:T(8,128)(2,1)S(1)}, bf16[768,128]{1,0:T(8,128)(2,1)S(1)}, u32[]{:S(2)}, u32[]{:S(2)}) collective-permute-start(bf16[768,128]{1,0:T(8,128)(2,1)S(1)} %get-tuple-element.45), channel_id=1, source_target_pairs={{0,8},{2,10},{4,12},{6,14},{8,16},{10,18},{12,20},{14,22},{16,24},... | collective-permute-start | bytes 589832 | tf_op jit(solution)/shard_map/ppermute | solution.py:226
  25.1 11.8 %collective-permute-start.1 = (bf16[128,1024]{1,0:T(8,128)(2,1)S(1)}, bf16[128,1024]{1,0:T(8,128)(2,1)S(1)}, u32[]{:S(2)}, u32[]{:S(2)}) collective-permute-start(bf16[128,1024]{1,0:T(8,128)(2,1)S(1)} %get-tuple-element.31), channel_id=1, source_target_pairs={{0,4},{2,6},{4,0},{6,2},{8,12},{10,14},{12,8},{14,10},{16,20},{18,... | collective-permute-start | bytes 786440 | tf_op jit(solution)/shard_map/ppermute | solution.py:223
  26.0 10.9 %collective-permute-start.2 = (bf16[128,1024]{1,0:T(8,128)(2,1)S(1)}, bf16[128,1024]{1,0:T(8,128)(2,1)S(1)}, u32[]{:S(2)}, u32[]{:S(2)}) collective-permute-start(bf16[128,1024]{1,0:T(8,128)(2,1)S(1)} %get-tuple-element.32), channel_id=1, source_target_pairs={{0,6},{2,4},{4,2},{6,0},{8,14},{10,12},{12,10},{14,8},{16,22},{18,... | collective-permute-start | bytes 786440 | tf_op jit(solution)/shard_map/ppermute | solution.py:223
  27.4 13.3 %collective-permute-start.9 = (bf16[816,128]{1,0:T(8,128)(2,1)S(1)}, bf16[816,128]{1,0:T(8,128)(2,1)S(1)}, u32[]{:S(2)}, u32[]{:S(2)}) collective-permute-start(bf16[816,128]{1,0:T(8,128)(2,1)S(1)} %collective-permute-done.8.refs_9_.refs_10_), channel_id=1, source_target_pairs={{8,16},{10,18},{12,20},{14,22},{16,24},{18,26},{20,28},{22,30},{9,... | collective-permute-start | bytes 626696 | tf_op jit(solution)/shard_map/ppermute | solution.py:226
  28.3 12.5 %collective-permute-start.14 = (bf16[768,128]{1,0:T(8,128)(2,1)S(1)}, bf16[768,128]{1,0:T(8,128)(2,1)S(1)}, u32[]{:S(2)}, u32[]{:S(2)}) collective-permute-start(bf16[768,128]{1,0:T(8,128)(2,1)S(1)} %collective-permute-done.13.refs_9_), channel_id=1, source_target_pairs={{8,16},{10,18},{12,20},{14,22},{16,24},{18,26},{20,28},{22,30},{9,... | collective-permute-start | bytes 589832 | tf_op jit(solution)/shard_map/ppermute | solution.py:226
  28.9 11.8 %collective-permute-start.7 = (bf16[528,128]{1,0:T(8,128)(2,1)S(1)}, bf16[528,128]{1,0:T(8,128)(2,1)S(1)}, u32[]{:S(2)}, u32[]{:S(2)}) collective-permute-start(bf16[528,128]{1,0:T(8,128)(2,1)S(1)} %collective-permute-done.6.refs_8_), channel_id=1, source_target_pairs={{8,16},{10,18},{12,20},{14,22},{16,24},{18,26},{20,28},{22,30},{9,... | collective-permute-start | bytes 405512 | tf_op jit(solution)/shard_map/ppermute | solution.py:226
  42.9 11.0 %collective-permute-start.15 = (bf16[128,512]{1,0:T(8,128)(2,1)S(1)}, bf16[128,512]{1,0:T(8,128)(2,1)S(1)}, u32[]{:S(2)}, u32[]{:S(2)}) collective-permute-start(bf16[128,512]{1,0:T(8,128)(2,1)S(1)} %get-tuple-element.50), channel_id=1, source_target_pairs={{0,2},{2,0},{4,6},{6,4},{8,10},{10,8},{12,14},{14,12},{16,18},{18,... | collective-permute-start | bytes 393224 | tf_op jit(solution)/shard_map/ppermute | solution.py:223
  47.4 8.8 %collective-permute-start.16 = (bf16[128,512]{1,0:T(8,128)(2,1)S(1)}, bf16[128,512]{1,0:T(8,128)(2,1)S(1)}, u32[]{:S(2)}, u32[]{:S(2)}) collective-permute-start(bf16[128,512]{1,0:T(8,128)(2,1)S(1)} %get-tuple-element.51), channel_id=1, source_target_pairs={{0,4},{2,6},{4,0},{6,2},{8,12},{10,14},{12,8},{14,10},{16,20},{18,... | collective-permute-start | bytes 393224 | tf_op jit(solution)/shard_map/ppermute | solution.py:223
  48.2 7.9 %collective-permute-start.17 = (bf16[128,512]{1,0:T(8,128)(2,1)S(1)}, bf16[128,512]{1,0:T(8,128)(2,1)S(1)}, u32[]{:S(2)}, u32[]{:S(2)}) collective-permute-start(bf16[128,512]{1,0:T(8,128)(2,1)S(1)} %get-tuple-element.52), channel_id=1, source_target_pairs={{0,6},{2,4},{4,2},{6,0},{8,14},{10,12},{12,10},{14,8},{16,22},{18,... | collective-permute-start | bytes 393224 | tf_op jit(solution)/shard_map/ppermute | solution.py:223
  52.6 5.4 %collective-permute-start.10 = (bf16[128,512]{1,0:T(8,128)(2,1)S(1)}, bf16[128,512]{1,0:T(8,128)(2,1)S(1)}, u32[]{:S(2)}, u32[]{:S(2)}) collective-permute-start(bf16[128,512]{1,0:T(8,128)(2,1)S(1)} %get-tuple-element.42), channel_id=1, source_target_pairs={{0,2},{2,0},{4,6},{6,4},{8,10},{10,8},{12,14},{14,12},{16,18},{18,... | collective-permute-start | bytes 393224 | tf_op jit(solution)/shard_map/ppermute | solution.py:223
  53.2 5.0 %collective-permute-start.11 = (bf16[128,512]{1,0:T(8,128)(2,1)S(1)}, bf16[128,512]{1,0:T(8,128)(2,1)S(1)}, u32[]{:S(2)}, u32[]{:S(2)}) collective-permute-start(bf16[128,512]{1,0:T(8,128)(2,1)S(1)} %get-tuple-element.43), channel_id=1, source_target_pairs={{0,4},{2,6},{4,0},{6,2},{8,12},{10,14},{12,8},{14,10},{16,20},{18,... | collective-permute-start | bytes 393224 | tf_op jit(solution)/shard_map/ppermute | solution.py:223
  53.9 5.9 %collective-permute-start.12 = (bf16[128,512]{1,0:T(8,128)(2,1)S(1)}, bf16[128,512]{1,0:T(8,128)(2,1)S(1)}, u32[]{:S(2)}, u32[]{:S(2)}) collective-permute-start(bf16[128,512]{1,0:T(8,128)(2,1)S(1)} %get-tuple-element.44), channel_id=1, source_target_pairs={{0,6},{2,4},{4,2},{6,0},{8,14},{10,12},{12,10},{14,8},{16,22},{18,... | collective-permute-start | bytes 393224 | tf_op jit(solution)/shard_map/ppermute | solution.py:223

commit v3 on v2

--- a/solution.py
+++ b/solution.py
@@ -82,7 +82,7 @@
     else:
         top_ref, sum_ref, acc_ref = refs[:3]
         refs = refs[3:]
-    q_buf, k_buf, v_buf, tag_buf, bias, s_buf, o_buf = refs
+    q_buf, k_buf, v_buf, tag_buf, col_buf, s_buf, w_buf, o_buf, stat_buf = refs
     wide = GROUP * rows
     member, block = place[0], place[1]
     tag_at = 2 * chunks * rows
@@ -96,94 +96,131 @@
             else:
                 ref, tag_ref = far[d][1], far[d][2]
                 start, tag_row = 2 * (k - 1) * rows, 2 * (size - 1) * rows + (k - 1) * ID_ROWS
-            at = pl.ds(pl.multiple_of((blocks.index(d) * size + spot) * rows, rows), rows)
-            if d in steps:
-                k_buf[at, :] = ref[start : start + rows, :]
-                v_buf[at, :] = ref[start + rows : start + 2 * rows, :]
+            place_in = blocks.index(d) * size + spot
             tag = tag_ref[tag_row : tag_row + 1, :].astype(jnp.float32)
             if d:
                 tag = jnp.where(block >= d, tag, -1.0)
-            at = pl.ds(pl.multiple_of((blocks.index(d) * size + spot) * 8, 8), 8)
-            tag_buf[at, :] = jnp.broadcast_to(tag, (8, rows))
+            if d in steps:
+                at = pl.ds(pl.multiple_of(place_in * rows, rows), rows)
+                k_buf[at, :] = ref[start : start + rows, :]
+                v_buf[:, at] = ref[start + rows : start + 2 * rows, :].T
+                col_buf[at, :] = jnp.broadcast_to(tag, (rows, rows)).T
+            if d == 0:
+                tag_buf[pl.ds(pl.multiple_of(spot * 8, 8), 8), :] = jnp.broadcast_to(tag, (8, rows))
         for h in range(GROUP):
             at = pl.ds(pl.multiple_of(spot * wide + h * rows, rows), rows)
             col = (chunk * GROUP + h) * DH
             q_buf[at, :] = q_refs[k][:, col : col + DH]
-    ahead = lax.broadcasted_iota(jnp.int32, (rows, rows), 0) - lax.broadcasted_iota(jnp.int32, (rows, rows), 1)
+    ahead = lax.broadcasted_iota(jnp.int32, (rows, rows), 1) - lax.broadcasted_iota(jnp.int32, (rows, rows), 0)
     scale = DH**-0.5 * LOG2E
-    for j in range(size):
-        seen = []
+
+    def reached(j):
+        seen = {}
         for d in steps:
             for n in range(size):
                 apart = d * size + j - n
                 if apart >= 0 and apart * rows - (rows - 1) < reach:
-                    seen.append((blocks.index(d) * size + n, apart))
-        seen.sort()
-        low, high = seen[0][0] * rows, (seen[-1][0] + 1) * rows
-        turn = j % 2
-        spot = blocks.index(0) * size + j
-        q_tag = jnp.broadcast_to(tag_buf[spot * 8 : spot * 8 + 1, :], (rows, rows)).T
-        for spot, apart in seen:
-            allowed = q_tag == jnp.broadcast_to(tag_buf[spot * 8 : spot * 8 + 1, :], (rows, rows))
+                    seen[blocks.index(d) * size + n] = apart
+        return min(seen) * rows, (max(seen) + 1) * rows, seen
+
+    def scores(j):
+        low, high, seen = reached(j)
+        q_tag = tag_buf[j * 8 : j * 8 + 1, :]
+        s = lax.dot_general(
+            k_buf[low:high, :],
+            q_buf[j * wide : (j + 1) * wide, :],
+            (((1,), (1,)), ((), ())),
+            preferred_element_type=jnp.float32,
+        )
+        top = None
+        for u in range(low, high, rows):
+            apart = seen[u // rows]
+            allowed = col_buf[u : u + rows, :] == q_tag
             if apart == 0:
                 allowed = allowed & (ahead >= 0)
             if apart * rows + rows > WINDOW:
                 allowed = allowed & (ahead + apart * rows < WINDOW)
-            bias[turn, :, spot * rows : (spot + 1) * rows] = jnp.where(allowed, 0.0, NEG_BIG)
-        q4 = q_buf[j * wide : (j + 1) * wide, :]
-        tiles = [(t, min(256, high - t)) for t in range(low, high, 256)]
-        top = None
-        for t, w in tiles:
-            s = lax.dot_general(
-                q4, k_buf[t : t + w, :], (((1,), (1,)), ((), ())), preferred_element_type=jnp.float32
-            )
-            s = s + jnp.concatenate([bias[turn, :, t : t + w]] * GROUP, axis=0)
-            s_buf[turn, :, t : t + w] = s
-            for u in range(0, w, DH):
-                part = s[:, u : u + DH]
-                top = part if top is None else jnp.maximum(top, part)
-        top = jnp.broadcast_to(jnp.max(top, axis=1, keepdims=True), (wide, DH))
+            bias = jnp.where(allowed, 0.0, NEG_BIG)
+            part = s[u - low : u - low + rows, :] + jnp.concatenate([bias] * GROUP, axis=1)
+            s_buf[j % 2, u : u + rows, :] = part
+            part = jnp.max(part.reshape(rows // 8, 8, wide), axis=0)
+            top = part if top is None else jnp.maximum(top, part)
+        stat_buf[j % 2] = top
+
+    def softmax(j):
+        low, high, _ = reached(j)
+        top = jnp.max(stat_buf[j % 2], axis=0, keepdims=True)
         if not first:
-            old_top = old_top_ref[j]
-            top = jnp.maximum(top, old_top)
-        total = acc = None
-        for t, w in tiles:
-            parts = []
-            for u in range(t, t + w, DH):
-                part = jnp.exp2((s_buf[turn, :, u : u + DH] - top) * scale)
-                total = part if total is None else total + part
-                parts.append(part.astype(jnp.bfloat16))
-            add = jnp.dot(jnp.concatenate(parts, axis=1), v_buf[t : t + w, :], preferred_element_type=jnp.float32)
-            acc = add if acc is None else acc + add
-        total = jnp.broadcast_to(jnp.sum(total, axis=1, keepdims=True), (wide, DH))
+            top = jnp.maximum(top, old_top_ref[j * 8 : j * 8 + 1, :])
+        total = None
+        for u in range(low, high, rows):
+            part = jnp.exp2((s_buf[j % 2, u : u + rows, :] - top) * scale)
+            w_buf[j % 2, u : u + rows, :] = part.astype(jnp.bfloat16)
+            part = jnp.sum(part.reshape(rows // 8, 8, wide), axis=0)
+            total = part if total is None else total + part
+        total = jnp.sum(total, axis=0, keepdims=True)
         if not first:
-            rescale = jnp.exp2((old_top - top) * scale)
-            total = total + old_sum_ref[j] * rescale
-            acc = acc + old_acc_ref[j] * rescale
+            rescale = jnp.exp2((old_top_ref[j * 8 : j * 8 + 1, :] - top) * scale)
+            total = total + old_sum_ref[j * 8 : j * 8 + 1, :] * rescale
+            stat_buf[2 + j % 2] = jnp.broadcast_to(rescale, (8, wide))
         if last:
-            result = (acc / total).astype(jnp.bfloat16)
+            stat_buf[4 + j % 2] = jnp.broadcast_to(1.0 / total, (8, wide))
+        else:
+            top_ref[j * 8 : (j + 1) * 8, :] = jnp.broadcast_to(top, (8, wide))
+            sum_ref[j * 8 : (j + 1) * 8, :] = jnp.broadcast_to(total, (8, wide))
+
+    def context(j):
+        low, high, _ = reached(j)
+        acc = jnp.dot(v_buf[:, low:high], w_buf[j % 2, low:high, :], preferred_element_type=jnp.float32)
+        if not first:
+            acc = acc + old_acc_ref[j] * stat_buf[2 + j % 2, 0:1, :]
+        if last:
+            acc = acc * stat_buf[4 + j % 2, 0:1, :]
             for h in range(GROUP):
-                o_buf[j * rows : (j + 1) * rows, h * DH : (h + 1) * DH] = result[h * rows : (h + 1) * rows, :]
+                o_buf[j * rows : (j + 1) * rows, h * DH : (h + 1) * DH] = acc[
+                    :, h * rows : (h + 1) * rows
+                ].T.astype(jnp.bfloat16)
         else:
-            top_ref[j] = top
-            sum_ref[j] = total
             acc_ref[j] = acc
+
+    for turn in range(size + 2):
+
+        @pl.when(block >= 0)
+        def _():
+            if turn < size:
+                scores(turn)
+            if 0 <= turn - 1 < size:
+                softmax(turn - 1)
+            if 0 <= turn - 2:
+                context(turn - 2)
+
     if last:
         for k in range(size):
             outs[k][...] = o_buf[pl.ds(pl.multiple_of((member ^ k) * rows, rows), rows), :]
 
 
 def scratch_of(size, rows, steps):
-    spots = len(set(steps) | {0}) * size
-    keys = spots * rows
+    keys = len(set(steps) | {0}) * size * rows
+    wide = GROUP * rows
     return [
-        pltpu.VMEM((size * GROUP * rows, DH), jnp.bfloat16),
+        pltpu.VMEM((size * wide, DH), jnp.bfloat16),
         pltpu.VMEM((keys, DH), jnp.bfloat16),
-        pltpu.VMEM((keys, DH), jnp.bfloat16),
-        pltpu.VMEM((spots * 8, rows), jnp.float32),
-        pltpu.VMEM((2, rows, keys), jnp.float32),
-        pltpu.VMEM((2, GROUP * rows, keys), jnp.float32),
+        pltpu.VMEM((DH, keys), jnp.bfloat16),
+        pltpu.VMEM((size * 8, rows), jnp.float32),
+        pltpu.VMEM((keys, rows), jnp.float32),
+        pltpu.VMEM((2, keys, wide), jnp.float32),
+        pltpu.VMEM((2, keys, wide), jnp.bfloat16),
         pltpu.VMEM((size * rows, GROUP * DH), jnp.bfloat16),
+        pltpu.VMEM((6, 8, wide), jnp.float32),
+    ]
+
+
+def state_of(size, rows):
+    wide = GROUP * rows
+    return [
+        jax.ShapeDtypeStruct((size * 8, wide), jnp.float32),
+        jax.ShapeDtypeStruct((size * 8, wide), jnp.float32),
+        jax.ShapeDtypeStruct((size, DH, wide), jnp.float32),
     ]
 
 
@@ -207,7 +244,6 @@
     hbm = pl.BlockSpec(memory_space=pltpu.HBM)
     params = pltpu.CompilerParams(vmem_limit_bytes=48 * 1024 * 1024)
     bf16 = functools.partial(jax.ShapeDtypeStruct, dtype=jnp.bfloat16)
-    f32 = functools.partial(jax.ShapeDtypeStruct, dtype=jnp.float32)
 
     def call(body, shapes, args, scratch=(), far_in=(), far_out=False):
         return pl.pallas_call(
@@ -250,7 +286,7 @@
             if d:
                 args += [far_own[d], far_rest[d][c]] + ([far_rest[d][0]] if c else [])
         args += list(state)
-        shapes = [bf16((rows, width))] * size if last else [f32((size, GROUP * rows, DH))] * 3
+        shapes = [bf16((rows, width))] * size if last else state_of(size, rows)
         scratch = scratch_of(size, rows, steps)
         body = functools.partial(
             attend, chunk=c, size=size, chunks=chunks, rows=rows, reach=reach, steps=steps, first=first, last=last

time: 61.6 us -> 60.8 us (0.987)
  Pallas kernels: 15.9 us -> 15 us
    pallas_call x7, Pallas kernels: 15.9 us -> 15 us  [call(): pl.pallas_call(body, in_specs=[smem if a is place else hbm if n in far_in...]
  transfers between devices with their start and end apart: 18 -> 18, of which waited for: 7 -> 7; matrix products, arithmetic and copies ran while one was open for 0% -> 0% of each run, Pallas kernels for 16% -> 15%
where the time goes in v3:
time: 60.8 us; the launch traced here: 60.5 us
  starting transfers between devices  27.8 us (46%)
  waiting for transfers between devices  17.5 us (29%)
  Pallas kernels  15 us (25%)
    ppermute x12, waiting for transfers between devices, swap(): lax.ppermute(x, 'seq', [(i, i ^ k) for i in range(shards)])  17.3 us
    ppermute x12, starting transfers between devices, swap(): lax.ppermute(x, 'seq', [(i, i ^ k) for i in range(shards)])  15.4 us
    pallas_call x7, Pallas kernels, call(): pl.pallas_call(body, in_specs=[smem if a is place else hbm if n in far_in...  15 us
    ppermute x6, starting transfers between devices, onward(): lax.ppermute(x, 'seq', [(i, i + size) for i in range((d - 1) * size, shar...  12.4 us
  transfers between devices with their start and end apart: 18, of which 7 were waited for; matrix products, arithmetic and copies ran while one was open for 0% of the time, Pallas kernels for 15%

profile of v3, /device:TPU:0, one launch (start us, length us, event | category | flops | bytes accessed | tf_op | source)
XLA Modules:
  0.0 60.5 jit_solution(11505920755962192313)
XLA Ops:
  0.0 0.1 pad_add_fusion.place
  0.1 2.2 %shard_map.37 = (bf16[528,128]{1,0:T(8,128)(2,1)S(1)}, bf16[528,128]{1,0:T(8,128)(2,1)S(1)}, bf16[528,128]{1,0:T(8,128)(2,1)S(1)}, bf16[528,128]{1,0:T(8,128)(2,...) custom-call(s32[2]{0:T(128)S(1)} %pad_add_fusion.place, ...), custom_call_target="tpu_custom_call" | custom-call | tf_op jit(solution)/shard_map/pallas_call | solution.py:249
  2.3 3.0 %collective-permute-start.3 = (bf16[528,128]{1,0:T(8,128)(2,1)S(1)}, bf16[528,128]{1,0:T(8,128)(2,1)S(1)}, u32[]{:S(2)}, u32[]{:S(2)}) collective-permute-start(bf16[528,128]{1,0:T(8,128)(2,1)S(1)} %get-tuple-element.34), channel_id=1, source_target_pairs={{0,2},{2,0},{4,6},{6,4},{8,10},{10,8},{12,14},{14,12},{16,18},{18,... | collective-permute-start | bytes 405512 | tf_op jit(solution)/shard_map/ppermute | solution.py:259
  5.3 1.5 %collective-permute-start.4 = (bf16[528,128]{1,0:T(8,128)(2,1)S(1)}, bf16[528,128]{1,0:T(8,128)(2,1)S(1)}, u32[]{:S(2)}, u32[]{:S(2)}) collective-permute-start(bf16[528,128]{1,0:T(8,128)(2,1)S(1)} %get-tuple-element.35), channel_id=1, source_target_pairs={{0,4},{2,6},{4,0},{6,2},{8,12},{10,14},{12,8},{14,10},{16,20},{18,... | collective-permute-start | bytes 405512 | tf_op jit(solution)/shard_map/ppermute | solution.py:259
  6.9 0.0 collective-permute-start.5
  6.9 2.4 %collective-permute-done.3.refs_0_.refs_5_ = bf16[528,128]{1,0:T(8,128)(2,1)S(1)} collective-permute-done((bf16[528,128]{1,0:T(8,128)(2,1)S(1)}, bf16[528,128]{1,0:T(8,128)(2,1)S(1)}, u32[]{:S(2)}, u32[]{:S(2)}) %collective-permute-start.3) | collective-permute-done | bytes 135200 | tf_op jit(solution)/shard_map/ppermute | solution.py:259
  9.3 4.0 %collective-permute-done.4.refs_1_.refs_6_ = bf16[528,128]{1,0:T(8,128)(2,1)S(1)} collective-permute-done((bf16[528,128]{1,0:T(8,128)(2,1)S(1)}, bf16[528,128]{1,0:T(8,128)(2,1)S(1)}, u32[]{:S(2)}, u32[]{:S(2)}) %collective-permute-start.4) | collective-permute-done | bytes 135200 | tf_op jit(solution)/shard_map/ppermute | solution.py:259
  13.3 0.0 collective-permute-done.5.refs_2_.refs_7_
  13.3 3.5 %collective-permute-start.8 = (bf16[816,128]{1,0:T(8,128)(2,1)S(1)}, bf16[816,128]{1,0:T(8,128)(2,1)S(1)}, u32[]{:S(2)}, u32[]{:S(2)}) collective-permute-start(bf16[816,128]{1,0:T(8,128)(2,1)S(1)} %get-tuple-element.37), channel_id=1, source_target_pairs={{0,8},{2,10},{4,12},{6,14},{8,16},{10,18},{12,20},{14,22},{16,24},... | collective-permute-start | bytes 626696 | tf_op jit(solution)/shard_map/ppermute | solution.py:262
  16.8 3.5 %collective-permute-start.6 = (bf16[528,128]{1,0:T(8,128)(2,1)S(1)}, bf16[528,128]{1,0:T(8,128)(2,1)S(1)}, u32[]{:S(2)}, u32[]{:S(2)}) collective-permute-start(bf16[528,128]{1,0:T(8,128)(2,1)S(1)} %get-tuple-element.33.refs_4_), channel_id=1, source_target_pairs={{0,8},{2,10},{4,12},{6,14},{8,16},{10,18},{12,20},{14,22},{16,24},... | collective-permute-start | bytes 405512 | tf_op jit(solution)/shard_map/ppermute | solution.py:262
  20.3 1.3 %collective-permute-start = (bf16[128,1024]{1,0:T(8,128)(2,1)S(1)}, bf16[128,1024]{1,0:T(8,128)(2,1)S(1)}, u32[]{:S(2)}, u32[]{:S(2)}) collective-permute-start(bf16[128,1024]{1,0:T(8,128)(2,1)S(1)} %get-tuple-element.30), channel_id=1, source_target_pairs={{0,2},{2,0},{4,6},{6,4},{8,10},{10,8},{12,14},{14,12},{16,18},{18,... | collective-permute-start | bytes 786440 | tf_op jit(solution)/shard_map/ppermute | solution.py:259
  21.6 3.5 %collective-permute-start.13 = (bf16[768,128]{1,0:T(8,128)(2,1)S(1)}, bf16[768,128]{1,0:T(8,128)(2,1)S(1)}, u32[]{:S(2)}, u32[]{:S(2)}) collective-permute-start(bf16[768,128]{1,0:T(8,128)(2,1)S(1)} %get-tuple-element.45), channel_id=1, source_target_pairs={{0,8},{2,10},{4,12},{6,14},{8,16},{10,18},{12,20},{14,22},{16,24},... | collective-permute-start | bytes 589832 | tf_op jit(solution)/shard_map/ppermute | solution.py:262
  25.1 0.9 %collective-permute-start.1 = (bf16[128,1024]{1,0:T(8,128)(2,1)S(1)}, bf16[128,1024]{1,0:T(8,128)(2,1)S(1)}, u32[]{:S(2)}, u32[]{:S(2)}) collective-permute-start(bf16[128,1024]{1,0:T(8,128)(2,1)S(1)} %get-tuple-element.31), channel_id=1, source_target_pairs={{0,4},{2,6},{4,0},{6,2},{8,12},{10,14},{12,8},{14,10},{16,20},{18,... | collective-permute-start | bytes 786440 | tf_op jit(solution)/shard_map/ppermute | solution.py:259
  26.0 0.0 collective-permute-done.6.refs_8_
  26.0 1.4 %collective-permute-start.2 = (bf16[128,1024]{1,0:T(8,128)(2,1)S(1)}, bf16[128,1024]{1,0:T(8,128)(2,1)S(1)}, u32[]{:S(2)}, u32[]{:S(2)}) collective-permute-start(bf16[128,1024]{1,0:T(8,128)(2,1)S(1)} %get-tuple-element.32), channel_id=1, source_target_pairs={{0,6},{2,4},{4,2},{6,0},{8,14},{10,12},{12,10},{14,8},{16,22},{18,... | collective-permute-start | bytes 786440 | tf_op jit(solution)/shard_map/ppermute | solution.py:259
  27.4 0.0 collective-permute-done.8.refs_9_.refs_10_
  27.4 0.7 %collective-permute-start.9 = (bf16[816,128]{1,0:T(8,128)(2,1)S(1)}, bf16[816,128]{1,0:T(8,128)(2,1)S(1)}, u32[]{:S(2)}, u32[]{:S(2)}) collective-permute-start(bf16[816,128]{1,0:T(8,128)(2,1)S(1)} %collective-permute-done.8.refs_9_.refs_10_), channel_id=1, source_target_pairs={{8,16},{10,18},{12,20},{14,22},{16,24},{18,26},{20,28},{22,30},{9,... | collective-permute-start | bytes 626696 | tf_op jit(solution)/shard_map/ppermute | solution.py:262
  28.1 0.2 collective-permute-done.13.refs_9_
  28.3 0.7 %collective-permute-start.14 = (bf16[768,128]{1,0:T(8,128)(2,1)S(1)}, bf16[768,128]{1,0:T(8,128)(2,1)S(1)}, u32[]{:S(2)}, u32[]{:S(2)}) collective-permute-start(bf16[768,128]{1,0:T(8,128)(2,1)S(1)} %collective-permute-done.13.refs_9_), channel_id=1, source_target_pairs={{8,16},{10,18},{12,20},{14,22},{16,24},{18,26},{20,28},{22,30},{9,... | collective-permute-start | bytes 589832 | tf_op jit(solution)/shard_map/ppermute | solution.py:262
  28.9 0.0 collective-permute-done.refs_1_
  28.9 0.7 %collective-permute-start.7 = (bf16[528,128]{1,0:T(8,128)(2,1)S(1)}, bf16[528,128]{1,0:T(8,128)(2,1)S(1)}, u32[]{:S(2)}, u32[]{:S(2)}) collective-permute-start(bf16[528,128]{1,0:T(8,128)(2,1)S(1)} %collective-permute-done.6.refs_8_), channel_id=1, source_target_pairs={{8,16},{10,18},{12,20},{14,22},{16,24},{18,26},{20,28},{22,30},{9,... | collective-permute-start | bytes 405512 | tf_op jit(solution)/shard_map/ppermute | solution.py:262
  29.6 7.2 %collective-permute-done.1.refs_2_ = bf16[128,1024]{1,0:T(8,128)(2,1)S(1)} collective-permute-done((bf16[128,1024]{1,0:T(8,128)(2,1)S(1)}, bf16[128,1024]{1,0:T(8,128)(2,1)S(1)}, u32[]{:S(2)}, u32[]{:S(2)}) %collective-permute-start.1) | collective-permute-done | bytes 262176 | tf_op jit(solution)/shard_map/ppermute | solution.py:259
  36.8 0.0 collective-permute-done.2.refs_3_
  36.8 3.5 %shard_map.41 = (f32[32,512]{1,0:T(8,128)S(1)}, f32[32,512]{1,0:T(8,128)S(1)}, f32[4,128,512]{2,1,0:T(8,128)S(1)}) custom-call(s32[2]{0:T(128)S(1)} %pad_add_fusion.place, bf16[128,1024]{1,0:T(8,128)(2,1)S(1)} %get-tuple-element.29.refs_0_, bf16[128,1024]{1,0:T(8,128)(2,1)S(1)} %collective-permute-done.refs_1_, ...), custom_call_target="tpu_custom_call" | custom-call | tf_op jit(solution)/shard_map/pallas_call | solution.py:249
  40.3 0.0 collective-permute-done.7.refs_8_
  40.3 0.0 collective-permute-done.14.refs_9_
  40.4 0.0 collective-permute-done.9.refs_9_.refs_10_
  40.4 2.1 %shard_map.42 = (bf16[128,512]{1,0:T(8,128)(2,1)S(1)}, bf16[128,512]{1,0:T(8,128)(2,1)S(1)}, bf16[128,512]{1,0:T(8,128)(2,1)S(1)}, bf16[128,512]{1,0:T(8,128)(2,1)S(1)}) custom-call(s32[2]{0:T(128)S(1)} %pad_add_fusion.place, bf16[128,1024]{1,0:T(8,128)(2,1)S(1)} %get-tuple-element.29.refs_0_, bf16[128,1024]{1,0:T(8,128)(2,1)S(1)} %collective-permute-done.refs_1_, ...), custom_call_target="tpu_custom_call" | custom-call | tf_op jit(solution)/shard_map/pallas_call | solution.py:249
  42.5 0.6 collective-permute-start.15
  43.1 3.5 %shard_map.39 = (f32[32,512]{1,0:T(8,128)S(1)}, f32[32,512]{1,0:T(8,128)S(1)}, f32[4,128,512]{2,1,0:T(8,128)S(1)}) custom-call(s32[2]{0:T(128)S(1)} %pad_add_fusion.place, bf16[128,1024]{1,0:T(8,128)(2,1)S(1)} %get-tuple-element.29.refs_0_, bf16[128,1024]{1,0:T(8,128)(2,1)S(1)} %collective-permute-done.refs_1_, ...), custom_call_target="tpu_custom_call" | custom-call | tf_op jit(solution)/shard_map/pallas_call | solution.py:249
  46.6 0.8 %collective-permute-start.16 = (bf16[128,512]{1,0:T(8,128)(2,1)S(1)}, bf16[128,512]{1,0:T(8,128)(2,1)S(1)}, u32[]{:S(2)}, u32[]{:S(2)}) collective-permute-start(bf16[128,512]{1,0:T(8,128)(2,1)S(1)} %get-tuple-element.51), channel_id=1, source_target_pairs={{0,4},{2,6},{4,0},{6,2},{8,12},{10,14},{12,8},{14,10},{16,20},{18,... | collective-permute-start | bytes 393224 | tf_op jit(solution)/shard_map/ppermute | solution.py:259
  47.4 2.2 %collective-permute-start.17 = (bf16[128,512]{1,0:T(8,128)(2,1)S(1)}, bf16[128,512]{1,0:T(8,128)(2,1)S(1)}, u32[]{:S(2)}, u32[]{:S(2)}) collective-permute-start(bf16[128,512]{1,0:T(8,128)(2,1)S(1)} %get-tuple-element.52), channel_id=1, source_target_pairs={{0,6},{2,4},{4,2},{6,0},{8,14},{10,12},{12,10},{14,8},{16,22},{18,... | collective-permute-start | bytes 393224 | tf_op jit(solution)/shard_map/ppermute | solution.py:259
  49.6 2.1 %shard_map.40 = (bf16[128,512]{1,0:T(8,128)(2,1)S(1)}, bf16[128,512]{1,0:T(8,128)(2,1)S(1)}, bf16[128,512]{1,0:T(8,128)(2,1)S(1)}, bf16[128,512]{1,0:T(8,128)(2,1)S(1)}) custom-call(s32[2]{0:T(128)S(1)} %pad_add_fusion.place, bf16[128,1024]{1,0:T(8,128)(2,1)S(1)} %get-tuple-element.29.refs_0_, bf16[128,1024]{1,0:T(8,128)(2,1)S(1)} %collective-permute-done.refs_1_, ...), custom_call_target="tpu_custom_call" | custom-call | tf_op jit(solution)/shard_map/pallas_call | solution.py:249
  51.8 0.6 collective-permute-start.10
  52.3 0.8 %collective-permute-start.11 = (bf16[128,512]{1,0:T(8,128)(2,1)S(1)}, bf16[128,512]{1,0:T(8,128)(2,1)S(1)}, u32[]{:S(2)}, u32[]{:S(2)}) collective-permute-start(bf16[128,512]{1,0:T(8,128)(2,1)S(1)} %get-tuple-element.43), channel_id=1, source_target_pairs={{0,4},{2,6},{4,0},{6,2},{8,12},{10,14},{12,8},{14,10},{16,20},{18,... | collective-permute-start | bytes 393224 | tf_op jit(solution)/shard_map/ppermute | solution.py:259
  53.1 0.0 collective-permute-done.15.refs_5_
  53.1 2.2 %collective-permute-start.12 = (bf16[128,512]{1,0:T(8,128)(2,1)S(1)}, bf16[128,512]{1,0:T(8,128)(2,1)S(1)}, u32[]{:S(2)}, u32[]{:S(2)}) collective-permute-start(bf16[128,512]{1,0:T(8,128)(2,1)S(1)} %get-tuple-element.44), channel_id=1, source_target_pairs={{0,6},{2,4},{4,2},{6,0},{8,14},{10,12},{12,10},{14,8},{16,22},{18,... | collective-permute-start | bytes 393224 | tf_op jit(solution)/shard_map/ppermute | solution.py:259
  55.3 0.0 collective-permute-done.16.refs_6_
  55.3 0.0 collective-permute-done.17.refs_7_
  55.3 1.8 %collective-permute-done.10.refs_1_ = bf16[128,512]{1,0:T(8,128)(2,1)S(1)} collective-permute-done((bf16[128,512]{1,0:T(8,128)(2,1)S(1)}, bf16[128,512]{1,0:T(8,128)(2,1)S(1)}, u32[]{:S(2)}, u32[]{:S(2)}) %collective-permute-start.10) | collective-permute-done | bytes 131104 | tf_op jit(solution)/shard_map/ppermute | solution.py:259
  57.2 0.2 collective-permute-done.11.refs_2_
  57.3 1.6 %collective-permute-done.12.refs_3_ = bf16[128,512]{1,0:T(8,128)(2,1)S(1)} collective-permute-done((bf16[128,512]{1,0:T(8,128)(2,1)S(1)}, bf16[128,512]{1,0:T(8,128)(2,1)S(1)}, u32[]{:S(2)}, u32[]{:S(2)}) %collective-permute-start.12) | collective-permute-done | bytes 131104 | tf_op jit(solution)/shard_map/ppermute | solution.py:259
  59.0 1.6 %shard_map.43 = bf16[128,4096]{1,0:T(8,128)(2,1)} custom-call(s32[2]{0:T(128)S(1)} %pad_add_fusion.place, bf16[128,512]{1,0:T(8,128)(2,1)S(1)} %get-tuple-element.41.refs_0_, bf16[128,512]{1,0:T(8,128)(2,1)S(1)} %collective-permute-done.10.refs_1_, bf16[128,512]{1,0:T(8,128)(2,1)S(1)} %collective-permute-done.11.refs_2_, ...), custom_call_target="tpu_custom_call" | custom-call | tf_op jit(solution)/shard_map/pallas_call | solution.py:249
  (1 shorter events, 0.0 us)
Async XLA Ops:
  2.3 7.0 %collective-permute-start.3 = (bf16[528,128]{1,0:T(8,128)(2,1)S(1)}, bf16[528,128]{1,0:T(8,128)(2,1)S(1)}, u32[]{:S(2)}, u32[]{:S(2)}) collective-permute-start(bf16[528,128]{1,0:T(8,128)(2,1)S(1)} %get-tuple-element.34), channel_id=1, source_target_pairs={{0,2},{2,0},{4,6},{6,4},{8,10},{10,8},{12,14},{14,12},{16,18},{18,... | collective-permute-start | bytes 405512 | tf_op jit(solution)/shard_map/ppermute | solution.py:259
  5.3 7.9 %collective-permute-start.4 = (bf16[528,128]{1,0:T(8,128)(2,1)S(1)}, bf16[528,128]{1,0:T(8,128)(2,1)S(1)}, u32[]{:S(2)}, u32[]{:S(2)}) collective-permute-start(bf16[528,128]{1,0:T(8,128)(2,1)S(1)} %get-tuple-element.35), channel_id=1, source_target_pairs={{0,4},{2,6},{4,0},{6,2},{8,12},{10,14},{12,8},{14,10},{16,20},{18,... | collective-permute-start | bytes 405512 | tf_op jit(solution)/shard_map/ppermute | solution.py:259
  6.9 6.4 %collective-permute-start.5 = (bf16[528,128]{1,0:T(8,128)(2,1)S(1)}, bf16[528,128]{1,0:T(8,128)(2,1)S(1)}, u32[]{:S(2)}, u32[]{:S(2)}) collective-permute-start(bf16[528,128]{1,0:T(8,128)(2,1)S(1)} %get-tuple-element.36), channel_id=1, source_target_pairs={{0,6},{2,4},{4,2},{6,0},{8,14},{10,12},{12,10},{14,8},{16,22},{18,... | collective-permute-start | bytes 405512 | tf_op jit(solution)/shard_map/ppermute | solution.py:259
  13.3 14.1 %collective-permute-start.8 = (bf16[816,128]{1,0:T(8,128)(2,1)S(1)}, bf16[816,128]{1,0:T(8,128)(2,1)S(1)}, u32[]{:S(2)}, u32[]{:S(2)}) collective-permute-start(bf16[816,128]{1,0:T(8,128)(2,1)S(1)} %get-tuple-element.37), channel_id=1, source_target_pairs={{0,8},{2,10},{4,12},{6,14},{8,16},{10,18},{12,20},{14,22},{16,24},... | collective-permute-start | bytes 626696 | tf_op jit(solution)/shard_map/ppermute | solution.py:262
  16.8 9.2 %collective-permute-start.6 = (bf16[528,128]{1,0:T(8,128)(2,1)S(1)}, bf16[528,128]{1,0:T(8,128)(2,1)S(1)}, u32[]{:S(2)}, u32[]{:S(2)}) collective-permute-start(bf16[528,128]{1,0:T(8,128)(2,1)S(1)} %get-tuple-element.33.refs_4_), channel_id=1, source_target_pairs={{0,8},{2,10},{4,12},{6,14},{8,16},{10,18},{12,20},{14,22},{16,24},... | collective-permute-start | bytes 405512 | tf_op jit(solution)/shard_map/ppermute | solution.py:262
  20.3 8.6 %collective-permute-start = (bf16[128,1024]{1,0:T(8,128)(2,1)S(1)}, bf16[128,1024]{1,0:T(8,128)(2,1)S(1)}, u32[]{:S(2)}, u32[]{:S(2)}) collective-permute-start(bf16[128,1024]{1,0:T(8,128)(2,1)S(1)} %get-tuple-element.30), channel_id=1, source_target_pairs={{0,2},{2,0},{4,6},{6,4},{8,10},{10,8},{12,14},{14,12},{16,18},{18,... | collective-permute-start | bytes 786440 | tf_op jit(solution)/shard_map/ppermute | solution.py:259
  21.6 6.6 %collective-permute-start.13 = (bf16[768,128]{1,0:T(8,128)(2,1)S(1)}, bf16[768,128]{1,0:T(8,128)(2,1)S(1)}, u32[]{:S(2)}, u32[]{:S(2)}) collective-permute-start(bf16[768,128]{1,0:T(8,128)(2,1)S(1)} %get-tuple-element.45), channel_id=1, source_target_pairs={{0,8},{2,10},{4,12},{6,14},{8,16},{10,18},{12,20},{14,22},{16,24},... | collective-permute-start | bytes 589832 | tf_op jit(solution)/shard_map/ppermute | solution.py:262
  25.1 11.8 %collective-permute-start.1 = (bf16[128,1024]{1,0:T(8,128)(2,1)S(1)}, bf16[128,1024]{1,0:T(8,128)(2,1)S(1)}, u32[]{:S(2)}, u32[]{:S(2)}) collective-permute-start(bf16[128,1024]{1,0:T(8,128)(2,1)S(1)} %get-tuple-element.31), channel_id=1, source_target_pairs={{0,4},{2,6},{4,0},{6,2},{8,12},{10,14},{12,8},{14,10},{16,20},{18,... | collective-permute-start | bytes 786440 | tf_op jit(solution)/shard_map/ppermute | solution.py:259
  26.0 10.9 %collective-permute-start.2 = (bf16[128,1024]{1,0:T(8,128)(2,1)S(1)}, bf16[128,1024]{1,0:T(8,128)(2,1)S(1)}, u32[]{:S(2)}, u32[]{:S(2)}) collective-permute-start(bf16[128,1024]{1,0:T(8,128)(2,1)S(1)} %get-tuple-element.32), channel_id=1, source_target_pairs={{0,6},{2,4},{4,2},{6,0},{8,14},{10,12},{12,10},{14,8},{16,22},{18,... | collective-permute-start | bytes 786440 | tf_op jit(solution)/shard_map/ppermute | solution.py:259
  27.4 12.9 %collective-permute-start.9 = (bf16[816,128]{1,0:T(8,128)(2,1)S(1)}, bf16[816,128]{1,0:T(8,128)(2,1)S(1)}, u32[]{:S(2)}, u32[]{:S(2)}) collective-permute-start(bf16[816,128]{1,0:T(8,128)(2,1)S(1)} %collective-permute-done.8.refs_9_.refs_10_), channel_id=1, source_target_pairs={{8,16},{10,18},{12,20},{14,22},{16,24},{18,26},{20,28},{22,30},{9,... | collective-permute-start | bytes 626696 | tf_op jit(solution)/shard_map/ppermute | solution.py:262
  28.3 12.1 %collective-permute-start.14 = (bf16[768,128]{1,0:T(8,128)(2,1)S(1)}, bf16[768,128]{1,0:T(8,128)(2,1)S(1)}, u32[]{:S(2)}, u32[]{:S(2)}) collective-permute-start(bf16[768,128]{1,0:T(8,128)(2,1)S(1)} %collective-permute-done.13.refs_9_), channel_id=1, source_target_pairs={{8,16},{10,18},{12,20},{14,22},{16,24},{18,26},{20,28},{22,30},{9,... | collective-permute-start | bytes 589832 | tf_op jit(solution)/shard_map/ppermute | solution.py:262
  28.9 11.4 %collective-permute-start.7 = (bf16[528,128]{1,0:T(8,128)(2,1)S(1)}, bf16[528,128]{1,0:T(8,128)(2,1)S(1)}, u32[]{:S(2)}, u32[]{:S(2)}) collective-permute-start(bf16[528,128]{1,0:T(8,128)(2,1)S(1)} %collective-permute-done.6.refs_8_), channel_id=1, source_target_pairs={{8,16},{10,18},{12,20},{14,22},{16,24},{18,26},{20,28},{22,30},{9,... | collective-permute-start | bytes 405512 | tf_op jit(solution)/shard_map/ppermute | solution.py:262
  42.5 10.6 %collective-permute-start.15 = (bf16[128,512]{1,0:T(8,128)(2,1)S(1)}, bf16[128,512]{1,0:T(8,128)(2,1)S(1)}, u32[]{:S(2)}, u32[]{:S(2)}) collective-permute-start(bf16[128,512]{1,0:T(8,128)(2,1)S(1)} %get-tuple-element.50), channel_id=1, source_target_pairs={{0,2},{2,0},{4,6},{6,4},{8,10},{10,8},{12,14},{14,12},{16,18},{18,... | collective-permute-start | bytes 393224 | tf_op jit(solution)/shard_map/ppermute | solution.py:259
  46.6 8.7 %collective-permute-start.16 = (bf16[128,512]{1,0:T(8,128)(2,1)S(1)}, bf16[128,512]{1,0:T(8,128)(2,1)S(1)}, u32[]{:S(2)}, u32[]{:S(2)}) collective-permute-start(bf16[128,512]{1,0:T(8,128)(2,1)S(1)} %get-tuple-element.51), channel_id=1, source_target_pairs={{0,4},{2,6},{4,0},{6,2},{8,12},{10,14},{12,8},{14,10},{16,20},{18,... | collective-permute-start | bytes 393224 | tf_op jit(solution)/shard_map/ppermute | solution.py:259
  47.4 7.9 %collective-permute-start.17 = (bf16[128,512]{1,0:T(8,128)(2,1)S(1)}, bf16[128,512]{1,0:T(8,128)(2,1)S(1)}, u32[]{:S(2)}, u32[]{:S(2)}) collective-permute-start(bf16[128,512]{1,0:T(8,128)(2,1)S(1)} %get-tuple-element.52), channel_id=1, source_target_pairs={{0,6},{2,4},{4,2},{6,0},{8,14},{10,12},{12,10},{14,8},{16,22},{18,... | collective-permute-start | bytes 393224 | tf_op jit(solution)/shard_map/ppermute | solution.py:259
  51.8 5.4 %collective-permute-start.10 = (bf16[128,512]{1,0:T(8,128)(2,1)S(1)}, bf16[128,512]{1,0:T(8,128)(2,1)S(1)}, u32[]{:S(2)}, u32[]{:S(2)}) collective-permute-start(bf16[128,512]{1,0:T(8,128)(2,1)S(1)} %get-tuple-element.42), channel_id=1, source_target_pairs={{0,2},{2,0},{4,6},{6,4},{8,10},{10,8},{12,14},{14,12},{16,18},{18,... | collective-permute-start | bytes 393224 | tf_op jit(solution)/shard_map/ppermute | solution.py:259
  52.3 5.0 %collective-permute-start.11 = (bf16[128,512]{1,0:T(8,128)(2,1)S(1)}, bf16[128,512]{1,0:T(8,128)(2,1)S(1)}, u32[]{:S(2)}, u32[]{:S(2)}) collective-permute-start(bf16[128,512]{1,0:T(8,128)(2,1)S(1)} %get-tuple-element.43), channel_id=1, source_target_pairs={{0,4},{2,6},{4,0},{6,2},{8,12},{10,14},{12,8},{14,10},{16,20},{18,... | collective-permute-start | bytes 393224 | tf_op jit(solution)/shard_map/ppermute | solution.py:259
  53.1 5.9 %collective-permute-start.12 = (bf16[128,512]{1,0:T(8,128)(2,1)S(1)}, bf16[128,512]{1,0:T(8,128)(2,1)S(1)}, u32[]{:S(2)}, u32[]{:S(2)}) collective-permute-start(bf16[128,512]{1,0:T(8,128)(2,1)S(1)} %get-tuple-element.44), channel_id=1, source_target_pairs={{0,6},{2,4},{4,2},{6,0},{8,14},{10,12},{12,10},{14,8},{16,22},{18,... | collective-permute-start | bytes 393224 | tf_op jit(solution)/shard_map/ppermute | solution.py:259

commit v4 on v3

--- a/solution.py
+++ b/solution.py
@@ -15,6 +15,10 @@
 NEG_BIG = -1e30
 LOG2E = 1.4426950408889634
 ID_ROWS = 16
+
+
+def early_steps(c, back):
+    return 0 if c else back
 
 
 def pack(place, kv, ids, q, *refs, size, chunks):
@@ -51,15 +55,23 @@
         ]
 
 
-def unpack(place, *refs, size, chunks):
+def join_own(*refs, count, chunk, rows):
+    own, rest, out = refs
+    out[0 : 2 * rows, :] = own[2 * chunk * rows : 2 * (chunk + 1) * rows, :]
+    out[2 * rows : 2 * (count + 1) * rows, :] = rest[0 : 2 * count * rows, :]
+    if not chunk:
+        tag_at = 2 * (count + 1) * rows
+        out[tag_at : tag_at + ID_ROWS, :] = own[own.shape[0] - ID_ROWS :, :]
+        out[tag_at + ID_ROWS :, :] = rest[2 * count * rows :, :]
+
+
+def unpack(place, *refs, chunk, size, chunks):
     out, sems = refs[-2:]
     width = refs[0].shape[1]
     copies = []
-    for c in range(chunks):
-        for k in range(size):
-            start = pl.multiple_of(((place[0] ^ k) * chunks + c) * width, width)
-            n = c * size + k
-            copies.append(pltpu.make_async_copy(refs[n], out.at[:, pl.ds(start, width)], sems.at[n]))
+    for k in range(size):
+        start = pl.multiple_of(((place[0] ^ k) * chunks + chunk) * width, width)
+        copies.append(pltpu.make_async_copy(refs[k], out.at[:, pl.ds(start, width)], sems.at[k]))
     for copy in copies:
         copy.start()
     for copy in copies:
@@ -71,8 +83,8 @@
     far = {}
     for d in steps:
         if d:
-            count = 3 if chunk else 2
-            far[d] = (refs[0], refs[1], refs[count - 1])
+            count = (3 if d == 1 else 2) - (0 if chunk else 1)
+            far[d] = (refs[0], refs[1 if d == 1 else 0], refs[count - 1])
             refs = refs[count:]
     if not first:
         old_top_ref, old_sum_ref, old_acc_ref = refs[:3]
@@ -90,12 +102,13 @@
     for k in range(size):
         spot = member ^ k
         for d in blocks:
-            if d == 0 or k == 0:
+            if d == 0 or (d == 1 and k == 0):
                 ref = near[k] if d == 0 else far[d][0]
                 start, tag_ref, tag_row = 2 * chunk * rows, ref, tag_at
             else:
+                n, count = (k - 1, size - 1) if d == 1 else (k, size)
                 ref, tag_ref = far[d][1], far[d][2]
-                start, tag_row = 2 * (k - 1) * rows, 2 * (size - 1) * rows + (k - 1) * ID_ROWS
+                start, tag_row = 2 * n * rows, 2 * count * rows + n * ID_ROWS
             place_in = blocks.index(d) * size + spot
             tag = tag_ref[tag_row : tag_row + 1, :].astype(jnp.float32)
             if d:
@@ -245,13 +258,14 @@
     params = pltpu.CompilerParams(vmem_limit_bytes=48 * 1024 * 1024)
     bf16 = functools.partial(jax.ShapeDtypeStruct, dtype=jnp.bfloat16)
 
-    def call(body, shapes, args, scratch=(), far_in=(), far_out=False):
+    def call(body, shapes, args, scratch=(), far_in=(), far_out=False, aliases={}):
         return pl.pallas_call(
             body,
             in_specs=[smem if a is place else hbm if n in far_in else vmem for n, a in enumerate(args)],
             out_specs=[hbm if far_out else vmem] * len(shapes),
             out_shape=shapes,
             scratch_shapes=scratch,
+            input_output_aliases=aliases,
             compiler_params=params,
         )(*[pltpu.with_memory_space_constraint(a, pltpu.HBM) if n in far_in else a for n, a in enumerate(args)])
 
@@ -273,18 +287,28 @@
     q_parts = [swap(q_sent[k], k) for k in range(size)]
     count = size - 1
     rest_shapes = [bf16((count * (2 * rows + (0 if c else ID_ROWS)), DH)) for c in range(chunks)]
-    far_own, far_rest = [sent[0]], []
+    far = {}
     if back:
-        far_rest.append(call(functools.partial(join, count=count, chunks=chunks, rows=rows), rest_shapes, near[1:]))
-    for d in range(1, back + 1):
-        far_own.append(onward(far_own[d - 1], d))
-        far_rest.append([onward(far_rest[d - 1][c], d) for c in range(chunks)])
+        joined = call(functools.partial(join, count=count, chunks=chunks, rows=rows), rest_shapes, near[1:])
+        own = onward(sent[0], 1)
+        rest = [onward(joined[c], 1) for c in range(chunks)]
+        far[1] = [[own, rest[c]] for c in range(chunks)]
+    for d in range(2, back + 1):
+        far[d] = []
+        for c in range(chunks):
+            if d == 2:
+                shape = bf16((size * (2 * rows + (0 if c else ID_ROWS)), DH))
+                body = functools.partial(join_own, count=count, chunk=c, rows=rows)
+                last = call(body, [shape], [own, rest[c]])[0]
+            else:
+                last = far[d - 1][c][0]
+            far[d].append([onward(last, d)])
 
     def stage(c, steps, state, first, last):
         args = [place] + q_parts + near
         for d in steps:
             if d:
-                args += [far_own[d], far_rest[d][c]] + ([far_rest[d][0]] if c else [])
+                args += far[d][c] + (far[d][0][-1:] if c else [])
         args += list(state)
         shapes = [bf16((rows, width))] * size if last else state_of(size, rows)
         scratch = scratch_of(size, rows, steps)
@@ -293,20 +317,26 @@
         )
         return call(body, shapes, args, scratch)
 
-    states = [()] * chunks
-    if back:
-        states = [stage(c, tuple(range(back)), (), True, False) for c in range(chunks)]
-    done = []
+    out = None
     for c in range(chunks):
-        result = stage(c, (back,), states[c], not back, True)
-        done += [swap(result[k], k) for k in range(size)]
-    return call(
-        functools.partial(unpack, size=size, chunks=chunks),
-        [bf16(queries.shape)],
-        [place] + done,
-        [pltpu.SemaphoreType.DMA((len(done),))],
-        far_out=True,
-    )[0]
+        state, steps = (), tuple(range(back + 1))
+        early = early_steps(c, back)
+        if early:
+            state = stage(c, steps[:early], (), True, False)
+            steps = steps[early:]
+        result = stage(c, steps, state, not state, True)
+        done = [swap(result[k], k) for k in range(size)]
+        args = [place] + done + ([out] if c else [])
+        out = call(
+            functools.partial(unpack, chunk=c, size=size, chunks=chunks),
+            [bf16(queries.shape)],
+            args,
+            [pltpu.SemaphoreType.DMA((size,))],
+            far_in=(1 + size,) if c else (),
+            far_out=True,
+            aliases={1 + size: 0} if c else {},
+        )[0]
+    return out
 
 
 def solution(mesh):

time: 60.8 us -> 63.3 us (1.041)
  the two profiles are of different devices: /device:TPU:0 before, /device:TPU:8 now
where the time goes in v4:
time: 63.3 us; the launch traced here: 63.1 us
  starting transfers between devices  31.2 us (49%)
  waiting for transfers between devices  16.5 us (26%)
  Pallas kernels  15.1 us (24%)
    ppermute x5, starting transfers between devices, onward(): lax.ppermute(x, 'seq', [(i, i + size) for i in range((d - 1) * size, shar...  16.7 us
    pallas_call x9, Pallas kernels, call(): pl.pallas_call(body, in_specs=[smem if a is place else hbm if n in far_in...  15.1 us
    ppermute x12, starting transfers between devices, swap(): lax.ppermute(x, 'seq', [(i, i ^ k) for i in range(shards)])  14.5 us
    ppermute x12, waiting for transfers between devices, swap(): lax.ppermute(x, 'seq', [(i, i ^ k) for i in range(shards)])  13.9 us
    ppermute x5, waiting for transfers between devices, onward(): lax.ppermute(x, 'seq', [(i, i + size) for i in range((d - 1) * size, shar...  2.66 us
  transfers between devices with their start and end apart: 17, of which 8 were waited for; matrix products, arithmetic and copies ran while one was open for 0% of the time, Pallas kernels for 18%

profile of v4, /device:TPU:8, one launch (start us, length us, event | category | flops | bytes accessed | tf_op | source)
XLA Modules:
  0.0 63.1 jit_solution(7224614931019230884)
XLA Ops:
  0.0 0.1 pad_add_fusion.place
  0.1 2.2 %shard_map.37 = (bf16[528,128]{1,0:T(8,128)(2,1)S(1)}, bf16[528,128]{1,0:T(8,128)(2,1)S(1)}, bf16[528,128]{1,0:T(8,128)(2,1)S(1)}, bf16[528,128]{1,0:T(8,128)(2,...) custom-call(s32[2]{0:T(128)S(1)} %pad_add_fusion.place, ...), custom_call_target="tpu_custom_call" | custom-call | tf_op jit(solution)/shard_map/pallas_call | solution.py:262
  2.3 1.6 %collective-permute-start.3 = (bf16[528,128]{1,0:T(8,128)(2,1)S(1)}, bf16[528,128]{1,0:T(8,128)(2,1)S(1)}, u32[]{:S(2)}, u32[]{:S(2)}) collective-permute-start(bf16[528,128]{1,0:T(8,128)(2,1)S(1)} %get-tuple-element.31), channel_id=1, source_target_pairs={{0,2},{2,0},{4,6},{6,4},{8,10},{10,8},{12,14},{14,12},{16,18},{18,... | collective-permute-start | bytes 405512 | tf_op jit(solution)/shard_map/ppermute | solution.py:273
  3.9 1.5 %collective-permute-start.4 = (bf16[528,128]{1,0:T(8,128)(2,1)S(1)}, bf16[528,128]{1,0:T(8,128)(2,1)S(1)}, u32[]{:S(2)}, u32[]{:S(2)}) collective-permute-start(bf16[528,128]{1,0:T(8,128)(2,1)S(1)} %get-tuple-element.32), channel_id=1, source_target_pairs={{0,4},{2,6},{4,0},{6,2},{8,12},{10,14},{12,8},{14,10},{16,20},{18,... | collective-permute-start | bytes 405512 | tf_op jit(solution)/shard_map/ppermute | solution.py:273
  5.4 0.5 collective-permute-start.5
  5.9 2.3 %collective-permute-done.3.refs_0_.refs_5_ = bf16[528,128]{1,0:T(8,128)(2,1)S(1)} collective-permute-done((bf16[528,128]{1,0:T(8,128)(2,1)S(1)}, bf16[528,128]{1,0:T(8,128)(2,1)S(1)}, u32[]{:S(2)}, u32[]{:S(2)}) %collective-permute-start.3) | collective-permute-done | bytes 135200 | tf_op jit(solution)/shard_map/ppermute | solution.py:273
  8.2 3.6 %collective-permute-done.4.refs_1_.refs_6_ = bf16[528,128]{1,0:T(8,128)(2,1)S(1)} collective-permute-done((bf16[528,128]{1,0:T(8,128)(2,1)S(1)}, bf16[528,128]{1,0:T(8,128)(2,1)S(1)}, u32[]{:S(2)}, u32[]{:S(2)}) %collective-permute-start.4) | collective-permute-done | bytes 135200 | tf_op jit(solution)/shard_map/ppermute | solution.py:273
  11.8 0.0 collective-permute-done.5.refs_2_.refs_7_
  11.8 3.5 %collective-permute-start.8 = (bf16[816,128]{1,0:T(8,128)(2,1)S(1)}, bf16[816,128]{1,0:T(8,128)(2,1)S(1)}, u32[]{:S(2)}, u32[]{:S(2)}) collective-permute-start(bf16[816,128]{1,0:T(8,128)(2,1)S(1)} %get-tuple-element.35), channel_id=1, source_target_pairs={{0,8},{2,10},{4,12},{6,14},{8,16},{10,18},{12,20},{14,22},{16,24},... | collective-permute-start | bytes 626696 | tf_op jit(solution)/shard_map/ppermute | solution.py:276
  15.3 3.5 %collective-permute-start.6 = (bf16[528,128]{1,0:T(8,128)(2,1)S(1)}, bf16[528,128]{1,0:T(8,128)(2,1)S(1)}, u32[]{:S(2)}, u32[]{:S(2)}) collective-permute-start(bf16[528,128]{1,0:T(8,128)(2,1)S(1)} %get-tuple-element.30.refs_4_), channel_id=1, source_target_pairs={{0,8},{2,10},{4,12},{6,14},{8,16},{10,18},{12,20},{14,22},{16,24},... | collective-permute-start | bytes 405512 | tf_op jit(solution)/shard_map/ppermute | solution.py:276
  18.8 1.9 %collective-permute-start.7 = (bf16[768,128]{1,0:T(8,128)(2,1)S(1)}, bf16[768,128]{1,0:T(8,128)(2,1)S(1)}, u32[]{:S(2)}, u32[]{:S(2)}) collective-permute-start(bf16[768,128]{1,0:T(8,128)(2,1)S(1)} %get-tuple-element.34), channel_id=1, source_target_pairs={{0,8},{2,10},{4,12},{6,14},{8,16},{10,18},{12,20},{14,22},{16,24},... | collective-permute-start | bytes 589832 | tf_op jit(solution)/shard_map/ppermute | solution.py:276
  20.8 2.6 %collective-permute-done.6.refs_0_.refs_8_ = bf16[528,128]{1,0:T(8,128)(2,1)S(1)} collective-permute-done((bf16[528,128]{1,0:T(8,128)(2,1)S(1)}, bf16[528,128]{1,0:T(8,128)(2,1)S(1)}, u32[]{:S(2)}, u32[]{:S(2)}) %collective-permute-start.6) | collective-permute-done | bytes 135200 | tf_op jit(solution)/shard_map/ppermute | solution.py:276
  23.4 0.0 collective-permute-done.8.refs_1_.refs_10_.refs_9_
  23.4 3.8 %collective-permute-start.10 = (bf16[1088,128]{1,0:T(8,128)(2,1)S(1)}, bf16[1088,128]{1,0:T(8,128)(2,1)S(1)}, u32[]{:S(2)}, u32[]{:S(2)}) collective-permute-start(bf16[1088,128]{1,0:T(8,128)(2,1)S(1)} %shard_map.40), channel_id=1, source_target_pairs={{8,16},{10,18},{12,20},{14,22},{16,24},{18,26},{20,28},{22,30},{9,... | collective-permute-start | bytes 835592 | tf_op jit(solution)/shard_map/ppermute | solution.py:276
  27.3 1.5 %collective-permute-start = (bf16[128,1024]{1,0:T(8,128)(2,1)S(1)}, bf16[128,1024]{1,0:T(8,128)(2,1)S(1)}, u32[]{:S(2)}, u32[]{:S(2)}) collective-permute-start(bf16[128,1024]{1,0:T(8,128)(2,1)S(1)} %get-tuple-element.27), channel_id=1, source_target_pairs={{0,2},{2,0},{4,6},{6,4},{8,10},{10,8},{12,14},{14,12},{16,18},{18,... | collective-permute-start | bytes 786440 | tf_op jit(solution)/shard_map/ppermute | solution.py:273
  28.8 0.9 %collective-permute-start.1 = (bf16[128,1024]{1,0:T(8,128)(2,1)S(1)}, bf16[128,1024]{1,0:T(8,128)(2,1)S(1)}, u32[]{:S(2)}, u32[]{:S(2)}) collective-permute-start(bf16[128,1024]{1,0:T(8,128)(2,1)S(1)} %get-tuple-element.28), channel_id=1, source_target_pairs={{0,4},{2,6},{4,0},{6,2},{8,12},{10,14},{12,8},{14,10},{16,20},{18,... | collective-permute-start | bytes 786440 | tf_op jit(solution)/shard_map/ppermute | solution.py:273
  29.7 1.4 %collective-permute-start.2 = (bf16[128,1024]{1,0:T(8,128)(2,1)S(1)}, bf16[128,1024]{1,0:T(8,128)(2,1)S(1)}, u32[]{:S(2)}, u32[]{:S(2)}) collective-permute-start(bf16[128,1024]{1,0:T(8,128)(2,1)S(1)} %get-tuple-element.29), channel_id=1, source_target_pairs={{0,6},{2,4},{4,2},{6,0},{8,14},{10,12},{12,10},{14,8},{16,22},{18,... | collective-permute-start | bytes 786440 | tf_op jit(solution)/shard_map/ppermute | solution.py:273
  31.1 0.0 collective-permute-done.7.refs_1_.refs_9_
  31.1 4.0 %collective-permute-start.9 = (bf16[1024,128]{1,0:T(8,128)(2,1)S(1)}, bf16[1024,128]{1,0:T(8,128)(2,1)S(1)}, u32[]{:S(2)}, u32[]{:S(2)}) collective-permute-start(bf16[1024,128]{1,0:T(8,128)(2,1)S(1)} %shard_map.39), channel_id=1, source_target_pairs={{8,16},{10,18},{12,20},{14,22},{16,24},{18,26},{20,28},{22,30},{9,... | collective-permute-start | bytes 786440 | tf_op jit(solution)/shard_map/ppermute | solution.py:276
  35.1 0.5 collective-permute-done.refs_1_
  35.6 4.0 %collective-permute-done.1.refs_2_ = bf16[128,1024]{1,0:T(8,128)(2,1)S(1)} collective-permute-done((bf16[128,1024]{1,0:T(8,128)(2,1)S(1)}, bf16[128,1024]{1,0:T(8,128)(2,1)S(1)}, u32[]{:S(2)}, u32[]{:S(2)}) %collective-permute-start.1) | collective-permute-done | bytes 262176 | tf_op jit(solution)/shard_map/ppermute | solution.py:273
  39.6 0.0 collective-permute-done.2.refs_3_
  39.6 3.5 %shard_map.42 = (f32[32,512]{1,0:T(8,128)S(1)}, f32[32,512]{1,0:T(8,128)S(1)}, f32[4,128,512]{2,1,0:T(8,128)S(1)}) custom-call(s32[2]{0:T(128)S(1)} %pad_add_fusion.place, bf16[128,1024]{1,0:T(8,128)(2,1)S(1)} %get-tuple-element.26.refs_0_, bf16[128,1024]{1,0:T(8,128)(2,1)S(1)} %collective-permute-done.refs_1_, ...), custom_call_target="tpu_custom_call" | custom-call | tf_op jit(solution)/shard_map/pallas_call | solution.py:262
  43.1 0.0 collective-permute-done.10.refs_12_.refs_8_
  43.1 2.2 %shard_map.43 = (bf16[128,512]{1,0:T(8,128)(2,1)S(1)}, bf16[128,512]{1,0:T(8,128)(2,1)S(1)}, bf16[128,512]{1,0:T(8,128)(2,1)S(1)}, bf16[128,512]{1,0:T(8,128)(2,1)S(1)}) custom-call(s32[2]{0:T(128)S(1)} %pad_add_fusion.place, bf16[128,1024]{1,0:T(8,128)(2,1)S(1)} %get-tuple-element.26.refs_0_, bf16[128,1024]{1,0:T(8,128)(2,1)S(1)} %collective-permute-done.refs_1_, ...), custom_call_target="tpu_custom_call" | custom-call | tf_op jit(solution)/shard_map/pallas_call | solution.py:262
  45.3 0.6 collective-permute-start.14
  45.9 0.0 collective-permute-done.9.refs_11_
  45.9 4.5 %shard_map.41 = (bf16[128,512]{1,0:T(8,128)(2,1)S(1)}, bf16[128,512]{1,0:T(8,128)(2,1)S(1)}, bf16[128,512]{1,0:T(8,128)(2,1)S(1)}, bf16[128,512]{1,0:T(8,128)(2,1)S(1)}) custom-call(s32[2]{0:T(128)S(1)} %pad_add_fusion.place, bf16[128,1024]{1,0:T(8,128)(2,1)S(1)} %get-tuple-element.26.refs_0_, bf16[128,1024]{1,0:T(8,128)(2,1)S(1)} %collective-permute-done.refs_1_, ...), custom_call_target="tpu_custom_call" | custom-call | tf_op jit(solution)/shard_map/pallas_call | solution.py:262
  50.4 1.6 %collective-permute-start.11 = (bf16[128,512]{1,0:T(8,128)(2,1)S(1)}, bf16[128,512]{1,0:T(8,128)(2,1)S(1)}, u32[]{:S(2)}, u32[]{:S(2)}) collective-permute-start(bf16[128,512]{1,0:T(8,128)(2,1)S(1)} %get-tuple-element.37), channel_id=1, source_target_pairs={{0,2},{2,0},{4,6},{6,4},{8,10},{10,8},{12,14},{14,12},{16,18},{18,... | collective-permute-start | bytes 393224 | tf_op jit(solution)/shard_map/ppermute | solution.py:273
  52.0 0.7 %collective-permute-start.15 = (bf16[128,512]{1,0:T(8,128)(2,1)S(1)}, bf16[128,512]{1,0:T(8,128)(2,1)S(1)}, u32[]{:S(2)}, u32[]{:S(2)}) collective-permute-start(bf16[128,512]{1,0:T(8,128)(2,1)S(1)} %get-tuple-element.45), channel_id=1, source_target_pairs={{0,4},{2,6},{4,0},{6,2},{8,12},{10,14},{12,8},{14,10},{16,20},{18,... | collective-permute-start | bytes 393224 | tf_op jit(solution)/shard_map/ppermute | solution.py:273
  52.6 1.3 %collective-permute-start.16 = (bf16[128,512]{1,0:T(8,128)(2,1)S(1)}, bf16[128,512]{1,0:T(8,128)(2,1)S(1)}, u32[]{:S(2)}, u32[]{:S(2)}) collective-permute-start(bf16[128,512]{1,0:T(8,128)(2,1)S(1)} %get-tuple-element.46), channel_id=1, source_target_pairs={{0,6},{2,4},{4,2},{6,0},{8,14},{10,12},{12,10},{14,8},{16,22},{18,... | collective-permute-start | bytes 393224 | tf_op jit(solution)/shard_map/ppermute | solution.py:273
  53.9 1.9 %collective-permute-start.12 = (bf16[128,512]{1,0:T(8,128)(2,1)S(1)}, bf16[128,512]{1,0:T(8,128)(2,1)S(1)}, u32[]{:S(2)}, u32[]{:S(2)}) collective-permute-start(bf16[128,512]{1,0:T(8,128)(2,1)S(1)} %get-tuple-element.38), channel_id=1, source_target_pairs={{0,4},{2,6},{4,0},{6,2},{8,12},{10,14},{12,8},{14,10},{16,20},{18,... | collective-permute-start | bytes 393224 | tf_op jit(solution)/shard_map/ppermute | solution.py:273
  55.8 0.0 collective-permute-done.14.refs_1_
  55.8 1.1 %collective-permute-start.13 = (bf16[128,512]{1,0:T(8,128)(2,1)S(1)}, bf16[128,512]{1,0:T(8,128)(2,1)S(1)}, u32[]{:S(2)}, u32[]{:S(2)}) collective-permute-start(bf16[128,512]{1,0:T(8,128)(2,1)S(1)} %get-tuple-element.39), channel_id=1, source_target_pairs={{0,6},{2,4},{4,2},{6,0},{8,14},{10,12},{12,10},{14,8},{16,22},{18,... | collective-permute-start | bytes 393224 | tf_op jit(solution)/shard_map/ppermute | solution.py:273
  56.9 0.0 collective-permute-done.15.refs_2_
  56.9 1.7 %collective-permute-done.16.refs_3_ = bf16[128,512]{1,0:T(8,128)(2,1)S(1)} collective-permute-done((bf16[128,512]{1,0:T(8,128)(2,1)S(1)}, bf16[128,512]{1,0:T(8,128)(2,1)S(1)}, u32[]{:S(2)}, u32[]{:S(2)}) %collective-permute-start.16) | collective-permute-done | bytes 131104 | tf_op jit(solution)/shard_map/ppermute | solution.py:273
  58.6 1.4 %shard_map.44.refs_4_ = bf16[128,4096]{1,0:T(8,128)(2,1)} custom-call(s32[2]{0:T(128)S(1)} %pad_add_fusion.place, bf16[128,512]{1,0:T(8,128)(2,1)S(1)} %get-tuple-element.43.refs_0_, bf16[128,512]{1,0:T(8,128)(2,1)S(1)} %collective-permute-done.14.refs_1_, bf16[128,512]{1,0:T(8,128)(2,1)S(1)} %collective-permute-done.15.refs_2_, ...), custom_call_target="tpu_custom_call" | custom-call | tf_op jit(solution)/shard_map/pallas_call | solution.py:262
  60.0 0.0 collective-permute-done.11.refs_1_
  60.0 0.2 collective-permute-done.12.refs_2_
  60.2 1.5 %collective-permute-done.13.refs_3_ = bf16[128,512]{1,0:T(8,128)(2,1)S(1)} collective-permute-done((bf16[128,512]{1,0:T(8,128)(2,1)S(1)}, bf16[128,512]{1,0:T(8,128)(2,1)S(1)}, u32[]{:S(2)}, u32[]{:S(2)}) %collective-permute-start.13) | collective-permute-done | bytes 131104 | tf_op jit(solution)/shard_map/ppermute | solution.py:273
  61.7 1.4 %shard_map.45 = bf16[128,4096]{1,0:T(8,128)(2,1)} custom-call(s32[2]{0:T(128)S(1)} %pad_add_fusion.place, bf16[128,512]{1,0:T(8,128)(2,1)S(1)} %get-tuple-element.36.refs_0_, bf16[128,512]{1,0:T(8,128)(2,1)S(1)} %collective-permute-done.11.refs_1_, bf16[128,512]{1,0:T(8,128)(2,1)S(1)} %collective-permute-done.12.refs_2_, ...), custom_call_target="tpu_custom_call", output_to_operand_aliasing={{}: (5, {})} | custom-call | tf_op jit(solution)/shard_map/pallas_call | solution.py:262
  (3 shorter events, 0.1 us)
Async XLA Ops:
  2.3 5.9 %collective-permute-start.3 = (bf16[528,128]{1,0:T(8,128)(2,1)S(1)}, bf16[528,128]{1,0:T(8,128)(2,1)S(1)}, u32[]{:S(2)}, u32[]{:S(2)}) collective-permute-start(bf16[528,128]{1,0:T(8,128)(2,1)S(1)} %get-tuple-element.31), channel_id=1, source_target_pairs={{0,2},{2,0},{4,6},{6,4},{8,10},{10,8},{12,14},{14,12},{16,18},{18,... | collective-permute-start | bytes 405512 | tf_op jit(solution)/shard_map/ppermute | solution.py:273
  3.9 7.9 %collective-permute-start.4 = (bf16[528,128]{1,0:T(8,128)(2,1)S(1)}, bf16[528,128]{1,0:T(8,128)(2,1)S(1)}, u32[]{:S(2)}, u32[]{:S(2)}) collective-permute-start(bf16[528,128]{1,0:T(8,128)(2,1)S(1)} %get-tuple-element.32), channel_id=1, source_target_pairs={{0,4},{2,6},{4,0},{6,2},{8,12},{10,14},{12,8},{14,10},{16,20},{18,... | collective-permute-start | bytes 405512 | tf_op jit(solution)/shard_map/ppermute | solution.py:273
  5.4 6.4 %collective-permute-start.5 = (bf16[528,128]{1,0:T(8,128)(2,1)S(1)}, bf16[528,128]{1,0:T(8,128)(2,1)S(1)}, u32[]{:S(2)}, u32[]{:S(2)}) collective-permute-start(bf16[528,128]{1,0:T(8,128)(2,1)S(1)} %get-tuple-element.33), channel_id=1, source_target_pairs={{0,6},{2,4},{4,2},{6,0},{8,14},{10,12},{12,10},{14,8},{16,22},{18,... | collective-permute-start | bytes 405512 | tf_op jit(solution)/shard_map/ppermute | solution.py:273
  11.8 11.6 %collective-permute-start.8 = (bf16[816,128]{1,0:T(8,128)(2,1)S(1)}, bf16[816,128]{1,0:T(8,128)(2,1)S(1)}, u32[]{:S(2)}, u32[]{:S(2)}) collective-permute-start(bf16[816,128]{1,0:T(8,128)(2,1)S(1)} %get-tuple-element.35), channel_id=1, source_target_pairs={{0,8},{2,10},{4,12},{6,14},{8,16},{10,18},{12,20},{14,22},{16,24},... | collective-permute-start | bytes 626696 | tf_op jit(solution)/shard_map/ppermute | solution.py:276
  15.3 8.1 %collective-permute-start.6 = (bf16[528,128]{1,0:T(8,128)(2,1)S(1)}, bf16[528,128]{1,0:T(8,128)(2,1)S(1)}, u32[]{:S(2)}, u32[]{:S(2)}) collective-permute-start(bf16[528,128]{1,0:T(8,128)(2,1)S(1)} %get-tuple-element.30.refs_4_), channel_id=1, source_target_pairs={{0,8},{2,10},{4,12},{6,14},{8,16},{10,18},{12,20},{14,22},{16,24},... | collective-permute-start | bytes 405512 | tf_op jit(solution)/shard_map/ppermute | solution.py:276
  18.8 12.2 %collective-permute-start.7 = (bf16[768,128]{1,0:T(8,128)(2,1)S(1)}, bf16[768,128]{1,0:T(8,128)(2,1)S(1)}, u32[]{:S(2)}, u32[]{:S(2)}) collective-permute-start(bf16[768,128]{1,0:T(8,128)(2,1)S(1)} %get-tuple-element.34), channel_id=1, source_target_pairs={{0,8},{2,10},{4,12},{6,14},{8,16},{10,18},{12,20},{14,22},{16,24},... | collective-permute-start | bytes 589832 | tf_op jit(solution)/shard_map/ppermute | solution.py:276
  23.4 19.7 %collective-permute-start.10 = (bf16[1088,128]{1,0:T(8,128)(2,1)S(1)}, bf16[1088,128]{1,0:T(8,128)(2,1)S(1)}, u32[]{:S(2)}, u32[]{:S(2)}) collective-permute-start(bf16[1088,128]{1,0:T(8,128)(2,1)S(1)} %shard_map.40), channel_id=1, source_target_pairs={{8,16},{10,18},{12,20},{14,22},{16,24},{18,26},{20,28},{22,30},{9,... | collective-permute-start | bytes 835592 | tf_op jit(solution)/shard_map/ppermute | solution.py:276
  27.3 8.3 %collective-permute-start = (bf16[128,1024]{1,0:T(8,128)(2,1)S(1)}, bf16[128,1024]{1,0:T(8,128)(2,1)S(1)}, u32[]{:S(2)}, u32[]{:S(2)}) collective-permute-start(bf16[128,1024]{1,0:T(8,128)(2,1)S(1)} %get-tuple-element.27), channel_id=1, source_target_pairs={{0,2},{2,0},{4,6},{6,4},{8,10},{10,8},{12,14},{14,12},{16,18},{18,... | collective-permute-start | bytes 786440 | tf_op jit(solution)/shard_map/ppermute | solution.py:273
  28.8 10.9 %collective-permute-start.1 = (bf16[128,1024]{1,0:T(8,128)(2,1)S(1)}, bf16[128,1024]{1,0:T(8,128)(2,1)S(1)}, u32[]{:S(2)}, u32[]{:S(2)}) collective-permute-start(bf16[128,1024]{1,0:T(8,128)(2,1)S(1)} %get-tuple-element.28), channel_id=1, source_target_pairs={{0,4},{2,6},{4,0},{6,2},{8,12},{10,14},{12,8},{14,10},{16,20},{18,... | collective-permute-start | bytes 786440 | tf_op jit(solution)/shard_map/ppermute | solution.py:273
  29.7 10.0 %collective-permute-start.2 = (bf16[128,1024]{1,0:T(8,128)(2,1)S(1)}, bf16[128,1024]{1,0:T(8,128)(2,1)S(1)}, u32[]{:S(2)}, u32[]{:S(2)}) collective-permute-start(bf16[128,1024]{1,0:T(8,128)(2,1)S(1)} %get-tuple-element.29), channel_id=1, source_target_pairs={{0,6},{2,4},{4,2},{6,0},{8,14},{10,12},{12,10},{14,8},{16,22},{18,... | collective-permute-start | bytes 786440 | tf_op jit(solution)/shard_map/ppermute | solution.py:273
  31.1 14.8 %collective-permute-start.9 = (bf16[1024,128]{1,0:T(8,128)(2,1)S(1)}, bf16[1024,128]{1,0:T(8,128)(2,1)S(1)}, u32[]{:S(2)}, u32[]{:S(2)}) collective-permute-start(bf16[1024,128]{1,0:T(8,128)(2,1)S(1)} %shard_map.39), channel_id=1, source_target_pairs={{8,16},{10,18},{12,20},{14,22},{16,24},{18,26},{20,28},{22,30},{9,... | collective-permute-start | bytes 786440 | tf_op jit(solution)/shard_map/ppermute | solution.py:276
  45.3 10.5 %collective-permute-start.14 = (bf16[128,512]{1,0:T(8,128)(2,1)S(1)}, bf16[128,512]{1,0:T(8,128)(2,1)S(1)}, u32[]{:S(2)}, u32[]{:S(2)}) collective-permute-start(bf16[128,512]{1,0:T(8,128)(2,1)S(1)} %get-tuple-element.44), channel_id=1, source_target_pairs={{0,2},{2,0},{4,6},{6,4},{8,10},{10,8},{12,14},{14,12},{16,18},{18,... | collective-permute-start | bytes 393224 | tf_op jit(solution)/shard_map/ppermute | solution.py:273
  50.4 9.6 %collective-permute-start.11 = (bf16[128,512]{1,0:T(8,128)(2,1)S(1)}, bf16[128,512]{1,0:T(8,128)(2,1)S(1)}, u32[]{:S(2)}, u32[]{:S(2)}) collective-permute-start(bf16[128,512]{1,0:T(8,128)(2,1)S(1)} %get-tuple-element.37), channel_id=1, source_target_pairs={{0,2},{2,0},{4,6},{6,4},{8,10},{10,8},{12,14},{14,12},{16,18},{18,... | collective-permute-start | bytes 393224 | tf_op jit(solution)/shard_map/ppermute | solution.py:273
  52.0 5.0 %collective-permute-start.15 = (bf16[128,512]{1,0:T(8,128)(2,1)S(1)}, bf16[128,512]{1,0:T(8,128)(2,1)S(1)}, u32[]{:S(2)}, u32[]{:S(2)}) collective-permute-start(bf16[128,512]{1,0:T(8,128)(2,1)S(1)} %get-tuple-element.45), channel_id=1, source_target_pairs={{0,4},{2,6},{4,0},{6,2},{8,12},{10,14},{12,8},{14,10},{16,20},{18,... | collective-permute-start | bytes 393224 | tf_op jit(solution)/shard_map/ppermute | solution.py:273
  52.6 6.0 %collective-permute-start.16 = (bf16[128,512]{1,0:T(8,128)(2,1)S(1)}, bf16[128,512]{1,0:T(8,128)(2,1)S(1)}, u32[]{:S(2)}, u32[]{:S(2)}) collective-permute-start(bf16[128,512]{1,0:T(8,128)(2,1)S(1)} %get-tuple-element.46), channel_id=1, source_target_pairs={{0,6},{2,4},{4,2},{6,0},{8,14},{10,12},{12,10},{14,8},{16,22},{18,... | collective-permute-start | bytes 393224 | tf_op jit(solution)/shard_map/ppermute | solution.py:273
  53.9 6.2 %collective-permute-start.12 = (bf16[128,512]{1,0:T(8,128)(2,1)S(1)}, bf16[128,512]{1,0:T(8,128)(2,1)S(1)}, u32[]{:S(2)}, u32[]{:S(2)}) collective-permute-start(bf16[128,512]{1,0:T(8,128)(2,1)S(1)} %get-tuple-element.38), channel_id=1, source_target_pairs={{0,4},{2,6},{4,0},{6,2},{8,12},{10,14},{12,8},{14,10},{16,20},{18,... | collective-permute-start | bytes 393224 | tf_op jit(solution)/shard_map/ppermute | solution.py:273
  55.8 5.9 %collective-permute-start.13 = (bf16[128,512]{1,0:T(8,128)(2,1)S(1)}, bf16[128,512]{1,0:T(8,128)(2,1)S(1)}, u32[]{:S(2)}, u32[]{:S(2)}) collective-permute-start(bf16[128,512]{1,0:T(8,128)(2,1)S(1)} %get-tuple-element.39), channel_id=1, source_target_pairs={{0,6},{2,4},{4,2},{6,0},{8,14},{10,12},{12,10},{14,8},{16,22},{18,... | collective-permute-start | bytes 393224 | tf_op jit(solution)/shard_map/ppermute | solution.py:273

commit v5 on v4

--- a/solution.py
+++ b/solution.py
@@ -273,7 +273,10 @@
         return lax.ppermute(x, "seq", [(i, i ^ k) for i in range(shards)]) if k else x
 
     def onward(x, d):
-        return lax.ppermute(x, "seq", [(i, i + size) for i in range((d - 1) * size, shards - size)])
+        pairs = [(i, (i + size) % shards) for i in range(shards)]
+        if d > 1:
+            pairs = pairs[(d - 1) * size : shards - size]
+        return lax.ppermute(x, "seq", pairs)
 
     packed = call(
         functools.partial(pack, size=size, chunks=chunks),

time: 63.3 us -> 61.3 us (0.968)
  the two profiles are of different devices: /device:TPU:8 before, /device:TPU:0 now
where the time goes in v5:
time: 61.3 us; the launch traced here: 61.1 us
  waiting for transfers between devices  24.5 us (40%)
  starting transfers between devices  21.4 us (35%)
  Pallas kernels  15.1 us (25%)
    ppermute x12, waiting for transfers between devices, swap(): lax.ppermute(x, 'seq', [(i, i ^ k) for i in range(shards)])  16.5 us
    ppermute x12, starting transfers between devices, swap(): lax.ppermute(x, 'seq', [(i, i ^ k) for i in range(shards)])  15.2 us
    pallas_call x9, Pallas kernels, call(): pl.pallas_call(body, in_specs=[smem if a is place else hbm if n in far_in...  15.1 us
    ppermute x5, waiting for transfers between devices, onward(): return lax.ppermute(x, 'seq', pairs)  7.92 us
    ppermute x5, starting transfers between devices, onward(): return lax.ppermute(x, 'seq', pairs)  6.14 us
  transfers between devices with their start and end apart: 17, of which 8 were waited for; matrix products, arithmetic and copies ran while one was open for 0% of the time, Pallas kernels for 19%

profile of v5, /device:TPU:0, one launch (start us, length us, event | category | flops | bytes accessed | tf_op | source)
XLA Modules:
  0.0 61.1 jit_solution(12992362019653384485)
XLA Ops:
  0.0 0.1 pad_add_fusion.place
  0.1 2.2 %shard_map.37 = (bf16[528,128]{1,0:T(8,128)(2,1)S(1)}, bf16[528,128]{1,0:T(8,128)(2,1)S(1)}, bf16[528,128]{1,0:T(8,128)(2,1)S(1)}, bf16[528,128]{1,0:T(8,128)(2,...) custom-call(s32[2]{0:T(128)S(1)} %pad_add_fusion.place, ...), custom_call_target="tpu_custom_call" | custom-call | tf_op jit(solution)/shard_map/pallas_call | solution.py:262
  2.3 3.0 %collective-permute-start.3 = (bf16[528,128]{1,0:T(8,128)(2,1)S(1)}, bf16[528,128]{1,0:T(8,128)(2,1)S(1)}, u32[]{:S(2)}, u32[]{:S(2)}) collective-permute-start(bf16[528,128]{1,0:T(8,128)(2,1)S(1)} %get-tuple-element.31), channel_id=1, source_target_pairs={{0,2},{2,0},{4,6},{6,4},{8,10},{10,8},{12,14},{14,12},{16,18},{18,... | collective-permute-start | bytes 405512 | tf_op jit(solution)/shard_map/ppermute | solution.py:273
  5.3 1.5 %collective-permute-start.4 = (bf16[528,128]{1,0:T(8,128)(2,1)S(1)}, bf16[528,128]{1,0:T(8,128)(2,1)S(1)}, u32[]{:S(2)}, u32[]{:S(2)}) collective-permute-start(bf16[528,128]{1,0:T(8,128)(2,1)S(1)} %get-tuple-element.32), channel_id=1, source_target_pairs={{0,4},{2,6},{4,0},{6,2},{8,12},{10,14},{12,8},{14,10},{16,20},{18,... | collective-permute-start | bytes 405512 | tf_op jit(solution)/shard_map/ppermute | solution.py:273
  6.9 0.0 collective-permute-start.5
  6.9 2.4 %collective-permute-done.3.refs_0_.refs_5_ = bf16[528,128]{1,0:T(8,128)(2,1)S(1)} collective-permute-done((bf16[528,128]{1,0:T(8,128)(2,1)S(1)}, bf16[528,128]{1,0:T(8,128)(2,1)S(1)}, u32[]{:S(2)}, u32[]{:S(2)}) %collective-permute-start.3) | collective-permute-done | bytes 135200 | tf_op jit(solution)/shard_map/ppermute | solution.py:273
  9.3 4.0 %collective-permute-done.4.refs_1_.refs_6_ = bf16[528,128]{1,0:T(8,128)(2,1)S(1)} collective-permute-done((bf16[528,128]{1,0:T(8,128)(2,1)S(1)}, bf16[528,128]{1,0:T(8,128)(2,1)S(1)}, u32[]{:S(2)}, u32[]{:S(2)}) %collective-permute-start.4) | collective-permute-done | bytes 135200 | tf_op jit(solution)/shard_map/ppermute | solution.py:273
  13.3 0.0 collective-permute-done.5.refs_2_.refs_7_
  13.3 1.6 %collective-permute-start.8 = (bf16[816,128]{1,0:T(8,128)(2,1)S(1)}, bf16[816,128]{1,0:T(8,128)(2,1)S(1)}, u32[]{:S(2)}, u32[]{:S(2)}) collective-permute-start(bf16[816,128]{1,0:T(8,128)(2,1)S(1)} %get-tuple-element.35), channel_id=1, source_target_pairs={{0,8},{2,10},{4,12},{6,14},{8,16},{10,18},{12,20},{14,22},{16,24},... | collective-permute-start | bytes 626696 | tf_op jit(solution)/shard_map/ppermute | solution.py:279
  14.9 1.6 %collective-permute-start.6 = (bf16[528,128]{1,0:T(8,128)(2,1)S(1)}, bf16[528,128]{1,0:T(8,128)(2,1)S(1)}, u32[]{:S(2)}, u32[]{:S(2)}) collective-permute-start(bf16[528,128]{1,0:T(8,128)(2,1)S(1)} %get-tuple-element.30.refs_4_), channel_id=1, source_target_pairs={{0,8},{2,10},{4,12},{6,14},{8,16},{10,18},{12,20},{14,22},{16,24},... | collective-permute-start | bytes 405512 | tf_op jit(solution)/shard_map/ppermute | solution.py:279
  16.5 1.6 %collective-permute-start.7 = (bf16[768,128]{1,0:T(8,128)(2,1)S(1)}, bf16[768,128]{1,0:T(8,128)(2,1)S(1)}, u32[]{:S(2)}, u32[]{:S(2)}) collective-permute-start(bf16[768,128]{1,0:T(8,128)(2,1)S(1)} %get-tuple-element.34), channel_id=1, source_target_pairs={{0,8},{2,10},{4,12},{6,14},{8,16},{10,18},{12,20},{14,22},{16,24},... | collective-permute-start | bytes 589832 | tf_op jit(solution)/shard_map/ppermute | solution.py:279
  18.1 7.9 %collective-permute-done.6.refs_0_.refs_8_ = bf16[528,128]{1,0:T(8,128)(2,1)S(1)} collective-permute-done((bf16[528,128]{1,0:T(8,128)(2,1)S(1)}, bf16[528,128]{1,0:T(8,128)(2,1)S(1)}, u32[]{:S(2)}, u32[]{:S(2)}) %collective-permute-start.6) | collective-permute-done | bytes 135200 | tf_op jit(solution)/shard_map/ppermute | solution.py:279
  26.0 0.0 collective-permute-done.8.refs_1_.refs_10_.refs_9_
  26.0 0.7 %collective-permute-start.10 = (bf16[1088,128]{1,0:T(8,128)(2,1)S(1)}, bf16[1088,128]{1,0:T(8,128)(2,1)S(1)}, u32[]{:S(2)}, u32[]{:S(2)}) collective-permute-start(bf16[1088,128]{1,0:T(8,128)(2,1)S(1)} %shard_map.40), channel_id=1, source_target_pairs={{8,16},{10,18},{12,20},{14,22},{16,24},{18,26},{20,28},{22,30},{9,... | collective-permute-start | bytes 835592 | tf_op jit(solution)/shard_map/ppermute | solution.py:279
  26.7 1.4 %collective-permute-start = (bf16[128,1024]{1,0:T(8,128)(2,1)S(1)}, bf16[128,1024]{1,0:T(8,128)(2,1)S(1)}, u32[]{:S(2)}, u32[]{:S(2)}) collective-permute-start(bf16[128,1024]{1,0:T(8,128)(2,1)S(1)} %get-tuple-element.27), channel_id=1, source_target_pairs={{0,2},{2,0},{4,6},{6,4},{8,10},{10,8},{12,14},{14,12},{16,18},{18,... | collective-permute-start | bytes 786440 | tf_op jit(solution)/shard_map/ppermute | solution.py:273
  28.1 0.7 %collective-permute-start.1 = (bf16[128,1024]{1,0:T(8,128)(2,1)S(1)}, bf16[128,1024]{1,0:T(8,128)(2,1)S(1)}, u32[]{:S(2)}, u32[]{:S(2)}) collective-permute-start(bf16[128,1024]{1,0:T(8,128)(2,1)S(1)} %get-tuple-element.28), channel_id=1, source_target_pairs={{0,4},{2,6},{4,0},{6,2},{8,12},{10,14},{12,8},{14,10},{16,20},{18,... | collective-permute-start | bytes 786440 | tf_op jit(solution)/shard_map/ppermute | solution.py:273
  28.8 1.5 %collective-permute-start.2 = (bf16[128,1024]{1,0:T(8,128)(2,1)S(1)}, bf16[128,1024]{1,0:T(8,128)(2,1)S(1)}, u32[]{:S(2)}, u32[]{:S(2)}) collective-permute-start(bf16[128,1024]{1,0:T(8,128)(2,1)S(1)} %get-tuple-element.29), channel_id=1, source_target_pairs={{0,6},{2,4},{4,2},{6,0},{8,14},{10,12},{12,10},{14,8},{16,22},{18,... | collective-permute-start | bytes 786440 | tf_op jit(solution)/shard_map/ppermute | solution.py:273
  30.3 0.0 collective-permute-done.7.refs_1_.refs_9_
  30.3 0.7 %collective-permute-start.9 = (bf16[1024,128]{1,0:T(8,128)(2,1)S(1)}, bf16[1024,128]{1,0:T(8,128)(2,1)S(1)}, u32[]{:S(2)}, u32[]{:S(2)}) collective-permute-start(bf16[1024,128]{1,0:T(8,128)(2,1)S(1)} %shard_map.39), channel_id=1, source_target_pairs={{8,16},{10,18},{12,20},{14,22},{16,24},{18,26},{20,28},{22,30},{9,... | collective-permute-start | bytes 786440 | tf_op jit(solution)/shard_map/ppermute | solution.py:279
  31.0 2.7 %collective-permute-done.refs_1_ = bf16[128,1024]{1,0:T(8,128)(2,1)S(1)} collective-permute-done((bf16[128,1024]{1,0:T(8,128)(2,1)S(1)}, bf16[128,1024]{1,0:T(8,128)(2,1)S(1)}, u32[]{:S(2)}, u32[]{:S(2)}) %collective-permute-start) | collective-permute-done | bytes 262176 | tf_op jit(solution)/shard_map/ppermute | solution.py:273
  33.7 4.2 %collective-permute-done.1.refs_2_ = bf16[128,1024]{1,0:T(8,128)(2,1)S(1)} collective-permute-done((bf16[128,1024]{1,0:T(8,128)(2,1)S(1)}, bf16[128,1024]{1,0:T(8,128)(2,1)S(1)}, u32[]{:S(2)}, u32[]{:S(2)}) %collective-permute-start.1) | collective-permute-done | bytes 262176 | tf_op jit(solution)/shard_map/ppermute | solution.py:273
  37.9 0.0 collective-permute-done.2.refs_3_
  37.9 3.5 %shard_map.42 = (f32[32,512]{1,0:T(8,128)S(1)}, f32[32,512]{1,0:T(8,128)S(1)}, f32[4,128,512]{2,1,0:T(8,128)S(1)}) custom-call(s32[2]{0:T(128)S(1)} %pad_add_fusion.place, bf16[128,1024]{1,0:T(8,128)(2,1)S(1)} %get-tuple-element.26.refs_0_, bf16[128,1024]{1,0:T(8,128)(2,1)S(1)} %collective-permute-done.refs_1_, ...), custom_call_target="tpu_custom_call" | custom-call | tf_op jit(solution)/shard_map/pallas_call | solution.py:262
  41.4 0.0 collective-permute-done.10.refs_12_.refs_8_
  41.4 2.2 %shard_map.43 = (bf16[128,512]{1,0:T(8,128)(2,1)S(1)}, bf16[128,512]{1,0:T(8,128)(2,1)S(1)}, bf16[128,512]{1,0:T(8,128)(2,1)S(1)}, bf16[128,512]{1,0:T(8,128)(2,1)S(1)}) custom-call(s32[2]{0:T(128)S(1)} %pad_add_fusion.place, bf16[128,1024]{1,0:T(8,128)(2,1)S(1)} %get-tuple-element.26.refs_0_, bf16[128,1024]{1,0:T(8,128)(2,1)S(1)} %collective-permute-done.refs_1_, ...), custom_call_target="tpu_custom_call" | custom-call | tf_op jit(solution)/shard_map/pallas_call | solution.py:262
  43.6 0.4 collective-permute-start.14
  44.0 0.0 collective-permute-done.9.refs_11_
  44.0 4.5 %shard_map.41 = (bf16[128,512]{1,0:T(8,128)(2,1)S(1)}, bf16[128,512]{1,0:T(8,128)(2,1)S(1)}, bf16[128,512]{1,0:T(8,128)(2,1)S(1)}, bf16[128,512]{1,0:T(8,128)(2,1)S(1)}) custom-call(s32[2]{0:T(128)S(1)} %pad_add_fusion.place, bf16[128,1024]{1,0:T(8,128)(2,1)S(1)} %get-tuple-element.26.refs_0_, bf16[128,1024]{1,0:T(8,128)(2,1)S(1)} %collective-permute-done.refs_1_, ...), custom_call_target="tpu_custom_call" | custom-call | tf_op jit(solution)/shard_map/pallas_call | solution.py:262
  48.5 1.7 %collective-permute-start.11 = (bf16[128,512]{1,0:T(8,128)(2,1)S(1)}, bf16[128,512]{1,0:T(8,128)(2,1)S(1)}, u32[]{:S(2)}, u32[]{:S(2)}) collective-permute-start(bf16[128,512]{1,0:T(8,128)(2,1)S(1)} %get-tuple-element.37), channel_id=1, source_target_pairs={{0,2},{2,0},{4,6},{6,4},{8,10},{10,8},{12,14},{14,12},{16,18},{18,... | collective-permute-start | bytes 393224 | tf_op jit(solution)/shard_map/ppermute | solution.py:273
  50.2 0.3 collective-permute-start.15
  50.6 1.5 %collective-permute-start.16 = (bf16[128,512]{1,0:T(8,128)(2,1)S(1)}, bf16[128,512]{1,0:T(8,128)(2,1)S(1)}, u32[]{:S(2)}, u32[]{:S(2)}) collective-permute-start(bf16[128,512]{1,0:T(8,128)(2,1)S(1)} %get-tuple-element.46), channel_id=1, source_target_pairs={{0,6},{2,4},{4,2},{6,0},{8,14},{10,12},{12,10},{14,8},{16,22},{18,... | collective-permute-start | bytes 393224 | tf_op jit(solution)/shard_map/ppermute | solution.py:273
  52.0 1.9 %collective-permute-start.12 = (bf16[128,512]{1,0:T(8,128)(2,1)S(1)}, bf16[128,512]{1,0:T(8,128)(2,1)S(1)}, u32[]{:S(2)}, u32[]{:S(2)}) collective-permute-start(bf16[128,512]{1,0:T(8,128)(2,1)S(1)} %get-tuple-element.38), channel_id=1, source_target_pairs={{0,4},{2,6},{4,0},{6,2},{8,12},{10,14},{12,8},{14,10},{16,20},{18,... | collective-permute-start | bytes 393224 | tf_op jit(solution)/shard_map/ppermute | solution.py:273
  53.9 0.0 collective-permute-done.14.refs_1_
  53.9 1.3 %collective-permute-start.13 = (bf16[128,512]{1,0:T(8,128)(2,1)S(1)}, bf16[128,512]{1,0:T(8,128)(2,1)S(1)}, u32[]{:S(2)}, u32[]{:S(2)}) collective-permute-start(bf16[128,512]{1,0:T(8,128)(2,1)S(1)} %get-tuple-element.39), channel_id=1, source_target_pairs={{0,6},{2,4},{4,2},{6,0},{8,14},{10,12},{12,10},{14,8},{16,22},{18,... | collective-permute-start | bytes 393224 | tf_op jit(solution)/shard_map/ppermute | solution.py:273
  55.2 1.4 %collective-permute-done.15.refs_2_ = bf16[128,512]{1,0:T(8,128)(2,1)S(1)} collective-permute-done((bf16[128,512]{1,0:T(8,128)(2,1)S(1)}, bf16[128,512]{1,0:T(8,128)(2,1)S(1)}, u32[]{:S(2)}, u32[]{:S(2)}) %collective-permute-start.15) | collective-permute-done | bytes 131104 | tf_op jit(solution)/shard_map/ppermute | solution.py:273
  56.6 0.0 collective-permute-done.16.refs_3_
  56.6 1.4 %shard_map.44.refs_4_ = bf16[128,4096]{1,0:T(8,128)(2,1)} custom-call(s32[2]{0:T(128)S(1)} %pad_add_fusion.place, bf16[128,512]{1,0:T(8,128)(2,1)S(1)} %get-tuple-element.43.refs_0_, bf16[128,512]{1,0:T(8,128)(2,1)S(1)} %collective-permute-done.14.refs_1_, bf16[128,512]{1,0:T(8,128)(2,1)S(1)} %collective-permute-done.15.refs_2_, ...), custom_call_target="tpu_custom_call" | custom-call | tf_op jit(solution)/shard_map/pallas_call | solution.py:262
  58.0 0.0 collective-permute-done.11.refs_1_
  58.0 0.5 collective-permute-done.12.refs_2_
  58.5 1.3 %collective-permute-done.13.refs_3_ = bf16[128,512]{1,0:T(8,128)(2,1)S(1)} collective-permute-done((bf16[128,512]{1,0:T(8,128)(2,1)S(1)}, bf16[128,512]{1,0:T(8,128)(2,1)S(1)}, u32[]{:S(2)}, u32[]{:S(2)}) %collective-permute-start.13) | collective-permute-done | bytes 131104 | tf_op jit(solution)/shard_map/ppermute | solution.py:273
  59.8 1.4 %shard_map.45 = bf16[128,4096]{1,0:T(8,128)(2,1)} custom-call(s32[2]{0:T(128)S(1)} %pad_add_fusion.place, bf16[128,512]{1,0:T(8,128)(2,1)S(1)} %get-tuple-element.36.refs_0_, bf16[128,512]{1,0:T(8,128)(2,1)S(1)} %collective-permute-done.11.refs_1_, bf16[128,512]{1,0:T(8,128)(2,1)S(1)} %collective-permute-done.12.refs_2_, ...), custom_call_target="tpu_custom_call", output_to_operand_aliasing={{}: (5, {})} | custom-call | tf_op jit(solution)/shard_map/pallas_call | solution.py:262
  (3 shorter events, 0.1 us)
Async XLA Ops:
  2.3 7.0 %collective-permute-start.3 = (bf16[528,128]{1,0:T(8,128)(2,1)S(1)}, bf16[528,128]{1,0:T(8,128)(2,1)S(1)}, u32[]{:S(2)}, u32[]{:S(2)}) collective-permute-start(bf16[528,128]{1,0:T(8,128)(2,1)S(1)} %get-tuple-element.31), channel_id=1, source_target_pairs={{0,2},{2,0},{4,6},{6,4},{8,10},{10,8},{12,14},{14,12},{16,18},{18,... | collective-permute-start | bytes 405512 | tf_op jit(solution)/shard_map/ppermute | solution.py:273
  5.3 7.9 %collective-permute-start.4 = (bf16[528,128]{1,0:T(8,128)(2,1)S(1)}, bf16[528,128]{1,0:T(8,128)(2,1)S(1)}, u32[]{:S(2)}, u32[]{:S(2)}) collective-permute-start(bf16[528,128]{1,0:T(8,128)(2,1)S(1)} %get-tuple-element.32), channel_id=1, source_target_pairs={{0,4},{2,6},{4,0},{6,2},{8,12},{10,14},{12,8},{14,10},{16,20},{18,... | collective-permute-start | bytes 405512 | tf_op jit(solution)/shard_map/ppermute | solution.py:273
  6.9 6.4 %collective-permute-start.5 = (bf16[528,128]{1,0:T(8,128)(2,1)S(1)}, bf16[528,128]{1,0:T(8,128)(2,1)S(1)}, u32[]{:S(2)}, u32[]{:S(2)}) collective-permute-start(bf16[528,128]{1,0:T(8,128)(2,1)S(1)} %get-tuple-element.33), channel_id=1, source_target_pairs={{0,6},{2,4},{4,2},{6,0},{8,14},{10,12},{12,10},{14,8},{16,22},{18,... | collective-permute-start | bytes 405512 | tf_op jit(solution)/shard_map/ppermute | solution.py:273
  13.3 12.7 %collective-permute-start.8 = (bf16[816,128]{1,0:T(8,128)(2,1)S(1)}, bf16[816,128]{1,0:T(8,128)(2,1)S(1)}, u32[]{:S(2)}, u32[]{:S(2)}) collective-permute-start(bf16[816,128]{1,0:T(8,128)(2,1)S(1)} %get-tuple-element.35), channel_id=1, source_target_pairs={{0,8},{2,10},{4,12},{6,14},{8,16},{10,18},{12,20},{14,22},{16,24},... | collective-permute-start | bytes 626696 | tf_op jit(solution)/shard_map/ppermute | solution.py:279
  14.9 11.1 %collective-permute-start.6 = (bf16[528,128]{1,0:T(8,128)(2,1)S(1)}, bf16[528,128]{1,0:T(8,128)(2,1)S(1)}, u32[]{:S(2)}, u32[]{:S(2)}) collective-permute-start(bf16[528,128]{1,0:T(8,128)(2,1)S(1)} %get-tuple-element.30.refs_4_), channel_id=1, source_target_pairs={{0,8},{2,10},{4,12},{6,14},{8,16},{10,18},{12,20},{14,22},{16,24},... | collective-permute-start | bytes 405512 | tf_op jit(solution)/shard_map/ppermute | solution.py:279
  16.5 13.8 %collective-permute-start.7 = (bf16[768,128]{1,0:T(8,128)(2,1)S(1)}, bf16[768,128]{1,0:T(8,128)(2,1)S(1)}, u32[]{:S(2)}, u32[]{:S(2)}) collective-permute-start(bf16[768,128]{1,0:T(8,128)(2,1)S(1)} %get-tuple-element.34), channel_id=1, source_target_pairs={{0,8},{2,10},{4,12},{6,14},{8,16},{10,18},{12,20},{14,22},{16,24},... | collective-permute-start | bytes 589832 | tf_op jit(solution)/shard_map/ppermute | solution.py:279
  26.0 15.4 %collective-permute-start.10 = (bf16[1088,128]{1,0:T(8,128)(2,1)S(1)}, bf16[1088,128]{1,0:T(8,128)(2,1)S(1)}, u32[]{:S(2)}, u32[]{:S(2)}) collective-permute-start(bf16[1088,128]{1,0:T(8,128)(2,1)S(1)} %shard_map.40), channel_id=1, source_target_pairs={{8,16},{10,18},{12,20},{14,22},{16,24},{18,26},{20,28},{22,30},{9,... | collective-permute-start | bytes 835592 | tf_op jit(solution)/shard_map/ppermute | solution.py:279
  26.7 7.0 %collective-permute-start = (bf16[128,1024]{1,0:T(8,128)(2,1)S(1)}, bf16[128,1024]{1,0:T(8,128)(2,1)S(1)}, u32[]{:S(2)}, u32[]{:S(2)}) collective-permute-start(bf16[128,1024]{1,0:T(8,128)(2,1)S(1)} %get-tuple-element.27), channel_id=1, source_target_pairs={{0,2},{2,0},{4,6},{6,4},{8,10},{10,8},{12,14},{14,12},{16,18},{18,... | collective-permute-start | bytes 786440 | tf_op jit(solution)/shard_map/ppermute | solution.py:273
  28.1 9.8 %collective-permute-start.1 = (bf16[128,1024]{1,0:T(8,128)(2,1)S(1)}, bf16[128,1024]{1,0:T(8,128)(2,1)S(1)}, u32[]{:S(2)}, u32[]{:S(2)}) collective-permute-start(bf16[128,1024]{1,0:T(8,128)(2,1)S(1)} %get-tuple-element.28), channel_id=1, source_target_pairs={{0,4},{2,6},{4,0},{6,2},{8,12},{10,14},{12,8},{14,10},{16,20},{18,... | collective-permute-start | bytes 786440 | tf_op jit(solution)/shard_map/ppermute | solution.py:273
  28.8 9.1 %collective-permute-start.2 = (bf16[128,1024]{1,0:T(8,128)(2,1)S(1)}, bf16[128,1024]{1,0:T(8,128)(2,1)S(1)}, u32[]{:S(2)}, u32[]{:S(2)}) collective-permute-start(bf16[128,1024]{1,0:T(8,128)(2,1)S(1)} %get-tuple-element.29), channel_id=1, source_target_pairs={{0,6},{2,4},{4,2},{6,0},{8,14},{10,12},{12,10},{14,8},{16,22},{18,... | collective-permute-start | bytes 786440 | tf_op jit(solution)/shard_map/ppermute | solution.py:273
  30.3 13.7 %collective-permute-start.9 = (bf16[1024,128]{1,0:T(8,128)(2,1)S(1)}, bf16[1024,128]{1,0:T(8,128)(2,1)S(1)}, u32[]{:S(2)}, u32[]{:S(2)}) collective-permute-start(bf16[1024,128]{1,0:T(8,128)(2,1)S(1)} %shard_map.39), channel_id=1, source_target_pairs={{8,16},{10,18},{12,20},{14,22},{16,24},{18,26},{20,28},{22,30},{9,... | collective-permute-start | bytes 786440 | tf_op jit(solution)/shard_map/ppermute | solution.py:279
  43.6 10.3 %collective-permute-start.14 = (bf16[128,512]{1,0:T(8,128)(2,1)S(1)}, bf16[128,512]{1,0:T(8,128)(2,1)S(1)}, u32[]{:S(2)}, u32[]{:S(2)}) collective-permute-start(bf16[128,512]{1,0:T(8,128)(2,1)S(1)} %get-tuple-element.44), channel_id=1, source_target_pairs={{0,2},{2,0},{4,6},{6,4},{8,10},{10,8},{12,14},{14,12},{16,18},{18,... | collective-permute-start | bytes 393224 | tf_op jit(solution)/shard_map/ppermute | solution.py:273
  48.5 9.5 %collective-permute-start.11 = (bf16[128,512]{1,0:T(8,128)(2,1)S(1)}, bf16[128,512]{1,0:T(8,128)(2,1)S(1)}, u32[]{:S(2)}, u32[]{:S(2)}) collective-permute-start(bf16[128,512]{1,0:T(8,128)(2,1)S(1)} %get-tuple-element.37), channel_id=1, source_target_pairs={{0,2},{2,0},{4,6},{6,4},{8,10},{10,8},{12,14},{14,12},{16,18},{18,... | collective-permute-start | bytes 393224 | tf_op jit(solution)/shard_map/ppermute | solution.py:273
  50.2 6.4 %collective-permute-start.15 = (bf16[128,512]{1,0:T(8,128)(2,1)S(1)}, bf16[128,512]{1,0:T(8,128)(2,1)S(1)}, u32[]{:S(2)}, u32[]{:S(2)}) collective-permute-start(bf16[128,512]{1,0:T(8,128)(2,1)S(1)} %get-tuple-element.45), channel_id=1, source_target_pairs={{0,4},{2,6},{4,0},{6,2},{8,12},{10,14},{12,8},{14,10},{16,20},{18,... | collective-permute-start | bytes 393224 | tf_op jit(solution)/shard_map/ppermute | solution.py:273
  50.6 6.0 %collective-permute-start.16 = (bf16[128,512]{1,0:T(8,128)(2,1)S(1)}, bf16[128,512]{1,0:T(8,128)(2,1)S(1)}, u32[]{:S(2)}, u32[]{:S(2)}) collective-permute-start(bf16[128,512]{1,0:T(8,128)(2,1)S(1)} %get-tuple-element.46), channel_id=1, source_target_pairs={{0,6},{2,4},{4,2},{6,0},{8,14},{10,12},{12,10},{14,8},{16,22},{18,... | collective-permute-start | bytes 393224 | tf_op jit(solution)/shard_map/ppermute | solution.py:273
  52.0 6.4 %collective-permute-start.12 = (bf16[128,512]{1,0:T(8,128)(2,1)S(1)}, bf16[128,512]{1,0:T(8,128)(2,1)S(1)}, u32[]{:S(2)}, u32[]{:S(2)}) collective-permute-start(bf16[128,512]{1,0:T(8,128)(2,1)S(1)} %get-tuple-element.38), channel_id=1, source_target_pairs={{0,4},{2,6},{4,0},{6,2},{8,12},{10,14},{12,8},{14,10},{16,20},{18,... | collective-permute-start | bytes 393224 | tf_op jit(solution)/shard_map/ppermute | solution.py:273
  53.9 5.9 %collective-permute-start.13 = (bf16[128,512]{1,0:T(8,128)(2,1)S(1)}, bf16[128,512]{1,0:T(8,128)(2,1)S(1)}, u32[]{:S(2)}, u32[]{:S(2)}) collective-permute-start(bf16[128,512]{1,0:T(8,128)(2,1)S(1)} %get-tuple-element.39), channel_id=1, source_target_pairs={{0,6},{2,4},{4,2},{6,0},{8,14},{10,12},{12,10},{14,8},{16,22},{18,... | collective-permute-start | bytes 393224 | tf_op jit(solution)/shard_map/ppermute | solution.py:273

commit v6 on v5

--- a/solution.py
+++ b/solution.py
@@ -21,27 +21,37 @@
     return 0 if c else back
 
 
-def pack(place, kv, ids, q, *refs, size, chunks):
-    kv_outs, q_outs, (ids_buf, sems) = refs[:size], refs[size : 2 * size], refs[2 * size :]
+def pack_kv(place, kv, ids, *refs, size, chunks):
+    outs, (ids_buf, sems) = refs[:size], refs[size:]
     rows = kv.shape[1]
-    width = q_outs[0].shape[1]
     moves = [(ids, ids_buf)]
     for k in range(size):
         for c in range(chunks):
             start = pl.multiple_of(((place[0] ^ k) * chunks + c) * DH, DH)
             for part in range(2):
                 first = (2 * c + part) * rows
-                moves.append((kv.at[part, :, pl.ds(start, DH)], kv_outs[k].at[pl.ds(first, rows), :]))
-    for k in range(size):
-        moves.append((q.at[:, pl.ds(pl.multiple_of((place[0] ^ k) * width, width), width)], q_outs[k]))
+                moves.append((kv.at[part, :, pl.ds(start, DH)], outs[k].at[pl.ds(first, rows), :]))
     copies = [pltpu.make_async_copy(a, b, sems.at[n]) for n, (a, b) in enumerate(moves)]
     for copy in copies:
         copy.start()
     copies[0].wait()
     tag = jnp.broadcast_to(ids_buf[...].astype(jnp.float32), (ID_ROWS, rows)).astype(jnp.bfloat16)
     for k in range(size):
-        kv_outs[k][2 * chunks * rows :, :] = tag
+        outs[k][2 * chunks * rows :, :] = tag
     for copy in copies[1:]:
+        copy.wait()
+
+
+def pack_q(place, q, *refs, size):
+    outs, sems = refs[:size], refs[size]
+    width = outs[0].shape[1]
+    copies = []
+    for k in range(size):
+        start = pl.multiple_of((place[0] ^ k) * width, width)
+        copies.append(pltpu.make_async_copy(q.at[:, pl.ds(start, width)], outs[k], sems.at[k]))
+    for copy in copies:
+        copy.start()
+    for copy in copies:
         copy.wait()
 
 
@@ -278,14 +288,20 @@
             pairs = pairs[(d - 1) * size : shards - size]
         return lax.ppermute(x, "seq", pairs)
 
-    packed = call(
-        functools.partial(pack, size=size, chunks=chunks),
-        [bf16((2 * chunks * rows + ID_ROWS, DH))] * size + [bf16((rows, chunks * width))] * size,
-        [place, keys_values, segment_ids.reshape(1, rows), queries],
-        [pltpu.VMEM((1, rows), jnp.int32), pltpu.SemaphoreType.DMA((1 + 2 * HK + size,))],
-        far_in=(1, 2, 3),
+    sent = call(
+        functools.partial(pack_kv, size=size, chunks=chunks),
+        [bf16((2 * chunks * rows + ID_ROWS, DH))] * size,
+        [place, keys_values, segment_ids.reshape(1, rows)],
+        [pltpu.VMEM((1, rows), jnp.int32), pltpu.SemaphoreType.DMA((1 + 2 * HK,))],
+        far_in=(1, 2),
     )
-    sent, q_sent = packed[:size], packed[size:]
+    q_sent = call(
+        functools.partial(pack_q, size=size),
+        [bf16((rows, chunks * width))] * size,
+        [place, queries],
+        [pltpu.SemaphoreType.DMA((size,))],
+        far_in=(1,),
+    )
     near = [swap(sent[k], k) for k in range(size)]
     q_parts = [swap(q_sent[k], k) for k in range(size)]
     count = size - 1

time: 61.3 us -> 62.6 us (1.021)
  Pallas kernels: 15.1 us -> 16.4 us
    pallas_call x9 -> x10, Pallas kernels: 15.1 us -> 16.4 us  [call(): pl.pallas_call(body, in_specs=[smem if a is place else hbm if n in far_in...]
  transfers between devices with their start and end apart: 17 -> 17, of which waited for: 8 -> 8; matrix products, arithmetic and copies ran while one was open for 0% -> 0% of each run, Pallas kernels for 19% -> 21%
where the time goes in v6:
time: 62.6 us; the launch traced here: 62.4 us
  waiting for transfers between devices  24.5 us (39%)
  starting transfers between devices  21.4 us (34%)
  Pallas kernels  16.4 us (26%)
    ppermute x12, waiting for transfers between devices, swap(): lax.ppermute(x, 'seq', [(i, i ^ k) for i in range(shards)])  16.5 us
    pallas_call x10, Pallas kernels, call(): pl.pallas_call(body, in_specs=[smem if a is place else hbm if n in far_in...  16.4 us
    ppermute x12, starting transfers between devices, swap(): lax.ppermute(x, 'seq', [(i, i ^ k) for i in range(shards)])  15.2 us
    ppermute x5, waiting for transfers between devices, onward(): return lax.ppermute(x, 'seq', pairs)  7.92 us
    ppermute x5, starting transfers between devices, onward(): return lax.ppermute(x, 'seq', pairs)  6.14 us
  transfers between devices with their start and end apart: 17, of which 8 were waited for; matrix products, arithmetic and copies ran while one was open for 0% of the time, Pallas kernels for 21%

profile of v6, /device:TPU:0, one launch (start us, length us, event | category | flops | bytes accessed | tf_op | source)
XLA Modules:
  0.0 62.4 jit_solution(7636016806101927447)
XLA Ops:
  0.0 0.1 pad_add_fusion.place
  0.1 1.7 %shard_map.38 = (bf16[528,128]{1,0:T(8,128)(2,1)S(1)}, bf16[528,128]{1,0:T(8,128)(2,1)S(1)}, bf16[528,128]{1,0:T(8,128)(2,1)S(1)}, bf16[528,128]{1,0:T(8,128)(2,1)S(1)}) custom-call(s32[2]{0:T(128)S(1)} %pad_add_fusion.place, bf16[2,128,1024]{2,1,0:T(8,128)(2,1)} %kv.1, s32[1,128]{1,0:T(1,128)} %bitcast.3), custom_call_target="tpu_custom_call" | custom-call | tf_op jit(solution)/shard_map/pallas_call | solution.py:272
  1.8 3.0 %collective-permute-start.3 = (bf16[528,128]{1,0:T(8,128)(2,1)S(1)}, bf16[528,128]{1,0:T(8,128)(2,1)S(1)}, u32[]{:S(2)}, u32[]{:S(2)}) collective-permute-start(bf16[528,128]{1,0:T(8,128)(2,1)S(1)} %get-tuple-element.31), channel_id=1, source_target_pairs={{0,2},{2,0},{4,6},{6,4},{8,10},{10,8},{12,14},{14,12},{16,18},{18,... | collective-permute-start | bytes 405512 | tf_op jit(solution)/shard_map/ppermute | solution.py:283
  4.8 1.5 %collective-permute-start.4 = (bf16[528,128]{1,0:T(8,128)(2,1)S(1)}, bf16[528,128]{1,0:T(8,128)(2,1)S(1)}, u32[]{:S(2)}, u32[]{:S(2)}) collective-permute-start(bf16[528,128]{1,0:T(8,128)(2,1)S(1)} %get-tuple-element.32), channel_id=1, source_target_pairs={{0,4},{2,6},{4,0},{6,2},{8,12},{10,14},{12,8},{14,10},{16,20},{18,... | collective-permute-start | bytes 405512 | tf_op jit(solution)/shard_map/ppermute | solution.py:283
  6.3 0.0 collective-permute-start.5
  6.4 2.4 %collective-permute-done.3.refs_0_.refs_5_ = bf16[528,128]{1,0:T(8,128)(2,1)S(1)} collective-permute-done((bf16[528,128]{1,0:T(8,128)(2,1)S(1)}, bf16[528,128]{1,0:T(8,128)(2,1)S(1)}, u32[]{:S(2)}, u32[]{:S(2)}) %collective-permute-start.3) | collective-permute-done | bytes 135200 | tf_op jit(solution)/shard_map/ppermute | solution.py:283
  8.8 4.0 %collective-permute-done.4.refs_1_.refs_6_ = bf16[528,128]{1,0:T(8,128)(2,1)S(1)} collective-permute-done((bf16[528,128]{1,0:T(8,128)(2,1)S(1)}, bf16[528,128]{1,0:T(8,128)(2,1)S(1)}, u32[]{:S(2)}, u32[]{:S(2)}) %collective-permute-start.4) | collective-permute-done | bytes 135200 | tf_op jit(solution)/shard_map/ppermute | solution.py:283
  12.8 0.0 collective-permute-done.5.refs_2_.refs_7_
  12.8 1.6 %collective-permute-start.8 = (bf16[816,128]{1,0:T(8,128)(2,1)S(1)}, bf16[816,128]{1,0:T(8,128)(2,1)S(1)}, u32[]{:S(2)}, u32[]{:S(2)}) collective-permute-start(bf16[816,128]{1,0:T(8,128)(2,1)S(1)} %get-tuple-element.35), channel_id=1, source_target_pairs={{0,8},{2,10},{4,12},{6,14},{8,16},{10,18},{12,20},{14,22},{16,24},... | collective-permute-start | bytes 626696 | tf_op jit(solution)/shard_map/ppermute | solution.py:289
  14.4 1.6 %collective-permute-start.6 = (bf16[528,128]{1,0:T(8,128)(2,1)S(1)}, bf16[528,128]{1,0:T(8,128)(2,1)S(1)}, u32[]{:S(2)}, u32[]{:S(2)}) collective-permute-start(bf16[528,128]{1,0:T(8,128)(2,1)S(1)} %get-tuple-element.30.refs_4_), channel_id=1, source_target_pairs={{0,8},{2,10},{4,12},{6,14},{8,16},{10,18},{12,20},{14,22},{16,24},... | collective-permute-start | bytes 405512 | tf_op jit(solution)/shard_map/ppermute | solution.py:289
  16.0 1.6 %collective-permute-start.7 = (bf16[768,128]{1,0:T(8,128)(2,1)S(1)}, bf16[768,128]{1,0:T(8,128)(2,1)S(1)}, u32[]{:S(2)}, u32[]{:S(2)}) collective-permute-start(bf16[768,128]{1,0:T(8,128)(2,1)S(1)} %get-tuple-element.34), channel_id=1, source_target_pairs={{0,8},{2,10},{4,12},{6,14},{8,16},{10,18},{12,20},{14,22},{16,24},... | collective-permute-start | bytes 589832 | tf_op jit(solution)/shard_map/ppermute | solution.py:289
  17.6 7.9 %collective-permute-done.6.refs_0_.refs_8_ = bf16[528,128]{1,0:T(8,128)(2,1)S(1)} collective-permute-done((bf16[528,128]{1,0:T(8,128)(2,1)S(1)}, bf16[528,128]{1,0:T(8,128)(2,1)S(1)}, u32[]{:S(2)}, u32[]{:S(2)}) %collective-permute-start.6) | collective-permute-done | bytes 135200 | tf_op jit(solution)/shard_map/ppermute | solution.py:289
  25.5 0.0 collective-permute-done.8.refs_1_.refs_10_.refs_9_
  25.5 0.7 %collective-permute-start.10 = (bf16[1088,128]{1,0:T(8,128)(2,1)S(1)}, bf16[1088,128]{1,0:T(8,128)(2,1)S(1)}, u32[]{:S(2)}, u32[]{:S(2)}) collective-permute-start(bf16[1088,128]{1,0:T(8,128)(2,1)S(1)} %shard_map.41), channel_id=1, source_target_pairs={{8,16},{10,18},{12,20},{14,22},{16,24},{18,26},{20,28},{22,30},{9,... | collective-permute-start | bytes 835592 | tf_op jit(solution)/shard_map/ppermute | solution.py:289
  26.2 1.8 %shard_map.37 = (bf16[128,1024]{1,0:T(8,128)(2,1)S(1)}, bf16[128,1024]{1,0:T(8,128)(2,1)S(1)}, bf16[128,1024]{1,0:T(8,128)(2,1)S(1)}, bf16[128,1024]{1,0:T(8,128)(2,1)S(1)}) custom-call(s32[2]{0:T(128)S(1)} %pad_add_fusion.place, bf16[128,4096]{1,0:T(8,128)(2,1)} %q.1), custom_call_target="tpu_custom_call" | custom-call | tf_op jit(solution)/shard_map/pallas_call | solution.py:272
  28.0 1.4 %collective-permute-start = (bf16[128,1024]{1,0:T(8,128)(2,1)S(1)}, bf16[128,1024]{1,0:T(8,128)(2,1)S(1)}, u32[]{:S(2)}, u32[]{:S(2)}) collective-permute-start(bf16[128,1024]{1,0:T(8,128)(2,1)S(1)} %get-tuple-element.27), channel_id=1, source_target_pairs={{0,2},{2,0},{4,6},{6,4},{8,10},{10,8},{12,14},{14,12},{16,18},{18,... | collective-permute-start | bytes 786440 | tf_op jit(solution)/shard_map/ppermute | solution.py:283
  29.4 0.7 %collective-permute-start.1 = (bf16[128,1024]{1,0:T(8,128)(2,1)S(1)}, bf16[128,1024]{1,0:T(8,128)(2,1)S(1)}, u32[]{:S(2)}, u32[]{:S(2)}) collective-permute-start(bf16[128,1024]{1,0:T(8,128)(2,1)S(1)} %get-tuple-element.28), channel_id=1, source_target_pairs={{0,4},{2,6},{4,0},{6,2},{8,12},{10,14},{12,8},{14,10},{16,20},{18,... | collective-permute-start | bytes 786440 | tf_op jit(solution)/shard_map/ppermute | solution.py:283
  30.1 1.5 %collective-permute-start.2 = (bf16[128,1024]{1,0:T(8,128)(2,1)S(1)}, bf16[128,1024]{1,0:T(8,128)(2,1)S(1)}, u32[]{:S(2)}, u32[]{:S(2)}) collective-permute-start(bf16[128,1024]{1,0:T(8,128)(2,1)S(1)} %get-tuple-element.29), channel_id=1, source_target_pairs={{0,6},{2,4},{4,2},{6,0},{8,14},{10,12},{12,10},{14,8},{16,22},{18,... | collective-permute-start | bytes 786440 | tf_op jit(solution)/shard_map/ppermute | solution.py:283
  31.5 0.0 collective-permute-done.7.refs_1_.refs_9_
  31.6 0.7 %collective-permute-start.9 = (bf16[1024,128]{1,0:T(8,128)(2,1)S(1)}, bf16[1024,128]{1,0:T(8,128)(2,1)S(1)}, u32[]{:S(2)}, u32[]{:S(2)}) collective-permute-start(bf16[1024,128]{1,0:T(8,128)(2,1)S(1)} %shard_map.40), channel_id=1, source_target_pairs={{8,16},{10,18},{12,20},{14,22},{16,24},{18,26},{20,28},{22,30},{9,... | collective-permute-start | bytes 786440 | tf_op jit(solution)/shard_map/ppermute | solution.py:289
  32.3 2.7 %collective-permute-done.refs_1_ = bf16[128,1024]{1,0:T(8,128)(2,1)S(1)} collective-permute-done((bf16[128,1024]{1,0:T(8,128)(2,1)S(1)}, bf16[128,1024]{1,0:T(8,128)(2,1)S(1)}, u32[]{:S(2)}, u32[]{:S(2)}) %collective-permute-start) | collective-permute-done | bytes 262176 | tf_op jit(solution)/shard_map/ppermute | solution.py:283
  35.0 4.2 %collective-permute-done.1.refs_2_ = bf16[128,1024]{1,0:T(8,128)(2,1)S(1)} collective-permute-done((bf16[128,1024]{1,0:T(8,128)(2,1)S(1)}, bf16[128,1024]{1,0:T(8,128)(2,1)S(1)}, u32[]{:S(2)}, u32[]{:S(2)}) %collective-permute-start.1) | collective-permute-done | bytes 262176 | tf_op jit(solution)/shard_map/ppermute | solution.py:283
  39.2 0.0 collective-permute-done.2.refs_3_
  39.2 3.5 %shard_map.43 = (f32[32,512]{1,0:T(8,128)S(1)}, f32[32,512]{1,0:T(8,128)S(1)}, f32[4,128,512]{2,1,0:T(8,128)S(1)}) custom-call(s32[2]{0:T(128)S(1)} %pad_add_fusion.place, bf16[128,1024]{1,0:T(8,128)(2,1)S(1)} %get-tuple-element.26.refs_0_, bf16[128,1024]{1,0:T(8,128)(2,1)S(1)} %collective-permute-done.refs_1_, ...), custom_call_target="tpu_custom_call" | custom-call | tf_op jit(solution)/shard_map/pallas_call | solution.py:272
  42.7 0.0 collective-permute-done.10.refs_12_.refs_8_
  42.7 2.1 %shard_map.44 = (bf16[128,512]{1,0:T(8,128)(2,1)S(1)}, bf16[128,512]{1,0:T(8,128)(2,1)S(1)}, bf16[128,512]{1,0:T(8,128)(2,1)S(1)}, bf16[128,512]{1,0:T(8,128)(2,1)S(1)}) custom-call(s32[2]{0:T(128)S(1)} %pad_add_fusion.place, bf16[128,1024]{1,0:T(8,128)(2,1)S(1)} %get-tuple-element.26.refs_0_, bf16[128,1024]{1,0:T(8,128)(2,1)S(1)} %collective-permute-done.refs_1_, ...), custom_call_target="tpu_custom_call" | custom-call | tf_op jit(solution)/shard_map/pallas_call | solution.py:272
  44.8 0.4 collective-permute-start.14
  45.3 0.0 collective-permute-done.9.refs_11_
  45.3 4.5 %shard_map.42 = (bf16[128,512]{1,0:T(8,128)(2,1)S(1)}, bf16[128,512]{1,0:T(8,128)(2,1)S(1)}, bf16[128,512]{1,0:T(8,128)(2,1)S(1)}, bf16[128,512]{1,0:T(8,128)(2,1)S(1)}) custom-call(s32[2]{0:T(128)S(1)} %pad_add_fusion.place, bf16[128,1024]{1,0:T(8,128)(2,1)S(1)} %get-tuple-element.26.refs_0_, bf16[128,1024]{1,0:T(8,128)(2,1)S(1)} %collective-permute-done.refs_1_, ...), custom_call_target="tpu_custom_call" | custom-call | tf_op jit(solution)/shard_map/pallas_call | solution.py:272
  49.8 1.7 %collective-permute-start.11 = (bf16[128,512]{1,0:T(8,128)(2,1)S(1)}, bf16[128,512]{1,0:T(8,128)(2,1)S(1)}, u32[]{:S(2)}, u32[]{:S(2)}) collective-permute-start(bf16[128,512]{1,0:T(8,128)(2,1)S(1)} %get-tuple-element.37), channel_id=1, source_target_pairs={{0,2},{2,0},{4,6},{6,4},{8,10},{10,8},{12,14},{14,12},{16,18},{18,... | collective-permute-start | bytes 393224 | tf_op jit(solution)/shard_map/ppermute | solution.py:283
  51.5 0.3 collective-permute-start.15
  51.8 1.5 %collective-permute-start.16 = (bf16[128,512]{1,0:T(8,128)(2,1)S(1)}, bf16[128,512]{1,0:T(8,128)(2,1)S(1)}, u32[]{:S(2)}, u32[]{:S(2)}) collective-permute-start(bf16[128,512]{1,0:T(8,128)(2,1)S(1)} %get-tuple-element.46), channel_id=1, source_target_pairs={{0,6},{2,4},{4,2},{6,0},{8,14},{10,12},{12,10},{14,8},{16,22},{18,... | collective-permute-start | bytes 393224 | tf_op jit(solution)/shard_map/ppermute | solution.py:283
  53.3 1.8 %collective-permute-start.12 = (bf16[128,512]{1,0:T(8,128)(2,1)S(1)}, bf16[128,512]{1,0:T(8,128)(2,1)S(1)}, u32[]{:S(2)}, u32[]{:S(2)}) collective-permute-start(bf16[128,512]{1,0:T(8,128)(2,1)S(1)} %get-tuple-element.38), channel_id=1, source_target_pairs={{0,4},{2,6},{4,0},{6,2},{8,12},{10,14},{12,8},{14,10},{16,20},{18,... | collective-permute-start | bytes 393224 | tf_op jit(solution)/shard_map/ppermute | solution.py:283
  55.2 0.0 collective-permute-done.14.refs_1_
  55.2 1.3 %collective-permute-start.13 = (bf16[128,512]{1,0:T(8,128)(2,1)S(1)}, bf16[128,512]{1,0:T(8,128)(2,1)S(1)}, u32[]{:S(2)}, u32[]{:S(2)}) collective-permute-start(bf16[128,512]{1,0:T(8,128)(2,1)S(1)} %get-tuple-element.39), channel_id=1, source_target_pairs={{0,6},{2,4},{4,2},{6,0},{8,14},{10,12},{12,10},{14,8},{16,22},{18,... | collective-permute-start | bytes 393224 | tf_op jit(solution)/shard_map/ppermute | solution.py:283
  56.4 1.4 %collective-permute-done.15.refs_2_ = bf16[128,512]{1,0:T(8,128)(2,1)S(1)} collective-permute-done((bf16[128,512]{1,0:T(8,128)(2,1)S(1)}, bf16[128,512]{1,0:T(8,128)(2,1)S(1)}, u32[]{:S(2)}, u32[]{:S(2)}) %collective-permute-start.15) | collective-permute-done | bytes 131104 | tf_op jit(solution)/shard_map/ppermute | solution.py:283
  57.9 0.0 collective-permute-done.16.refs_3_
  57.9 1.4 %shard_map.45.refs_4_ = bf16[128,4096]{1,0:T(8,128)(2,1)} custom-call(s32[2]{0:T(128)S(1)} %pad_add_fusion.place, bf16[128,512]{1,0:T(8,128)(2,1)S(1)} %get-tuple-element.43.refs_0_, bf16[128,512]{1,0:T(8,128)(2,1)S(1)} %collective-permute-done.14.refs_1_, bf16[128,512]{1,0:T(8,128)(2,1)S(1)} %collective-permute-done.15.refs_2_, ...), custom_call_target="tpu_custom_call" | custom-call | tf_op jit(solution)/shard_map/pallas_call | solution.py:272
  59.2 0.0 collective-permute-done.11.refs_1_
  59.2 0.5 collective-permute-done.12.refs_2_
  59.7 1.3 %collective-permute-done.13.refs_3_ = bf16[128,512]{1,0:T(8,128)(2,1)S(1)} collective-permute-done((bf16[128,512]{1,0:T(8,128)(2,1)S(1)}, bf16[128,512]{1,0:T(8,128)(2,1)S(1)}, u32[]{:S(2)}, u32[]{:S(2)}) %collective-permute-start.13) | collective-permute-done | bytes 131104 | tf_op jit(solution)/shard_map/ppermute | solution.py:283
  61.0 1.4 %shard_map.46 = bf16[128,4096]{1,0:T(8,128)(2,1)} custom-call(s32[2]{0:T(128)S(1)} %pad_add_fusion.place, bf16[128,512]{1,0:T(8,128)(2,1)S(1)} %get-tuple-element.36.refs_0_, bf16[128,512]{1,0:T(8,128)(2,1)S(1)} %collective-permute-done.11.refs_1_, bf16[128,512]{1,0:T(8,128)(2,1)S(1)} %collective-permute-done.12.refs_2_, ...), custom_call_target="tpu_custom_call", output_to_operand_aliasing={{}: (5, {})} | custom-call | tf_op jit(solution)/shard_map/pallas_call | solution.py:272
  (3 shorter events, 0.1 us)
Async XLA Ops:
  1.8 7.0 %collective-permute-start.3 = (bf16[528,128]{1,0:T(8,128)(2,1)S(1)}, bf16[528,128]{1,0:T(8,128)(2,1)S(1)}, u32[]{:S(2)}, u32[]{:S(2)}) collective-permute-start(bf16[528,128]{1,0:T(8,128)(2,1)S(1)} %get-tuple-element.31), channel_id=1, source_target_pairs={{0,2},{2,0},{4,6},{6,4},{8,10},{10,8},{12,14},{14,12},{16,18},{18,... | collective-permute-start | bytes 405512 | tf_op jit(solution)/shard_map/ppermute | solution.py:283
  4.8 7.9 %collective-permute-start.4 = (bf16[528,128]{1,0:T(8,128)(2,1)S(1)}, bf16[528,128]{1,0:T(8,128)(2,1)S(1)}, u32[]{:S(2)}, u32[]{:S(2)}) collective-permute-start(bf16[528,128]{1,0:T(8,128)(2,1)S(1)} %get-tuple-element.32), channel_id=1, source_target_pairs={{0,4},{2,6},{4,0},{6,2},{8,12},{10,14},{12,8},{14,10},{16,20},{18,... | collective-permute-start | bytes 405512 | tf_op jit(solution)/shard_map/ppermute | solution.py:283
  6.3 6.4 %collective-permute-start.5 = (bf16[528,128]{1,0:T(8,128)(2,1)S(1)}, bf16[528,128]{1,0:T(8,128)(2,1)S(1)}, u32[]{:S(2)}, u32[]{:S(2)}) collective-permute-start(bf16[528,128]{1,0:T(8,128)(2,1)S(1)} %get-tuple-element.33), channel_id=1, source_target_pairs={{0,6},{2,4},{4,2},{6,0},{8,14},{10,12},{12,10},{14,8},{16,22},{18,... | collective-permute-start | bytes 405512 | tf_op jit(solution)/shard_map/ppermute | solution.py:283
  12.8 12.7 %collective-permute-start.8 = (bf16[816,128]{1,0:T(8,128)(2,1)S(1)}, bf16[816,128]{1,0:T(8,128)(2,1)S(1)}, u32[]{:S(2)}, u32[]{:S(2)}) collective-permute-start(bf16[816,128]{1,0:T(8,128)(2,1)S(1)} %get-tuple-element.35), channel_id=1, source_target_pairs={{0,8},{2,10},{4,12},{6,14},{8,16},{10,18},{12,20},{14,22},{16,24},... | collective-permute-start | bytes 626696 | tf_op jit(solution)/shard_map/ppermute | solution.py:289
  14.4 11.1 %collective-permute-start.6 = (bf16[528,128]{1,0:T(8,128)(2,1)S(1)}, bf16[528,128]{1,0:T(8,128)(2,1)S(1)}, u32[]{:S(2)}, u32[]{:S(2)}) collective-permute-start(bf16[528,128]{1,0:T(8,128)(2,1)S(1)} %get-tuple-element.30.refs_4_), channel_id=1, source_target_pairs={{0,8},{2,10},{4,12},{6,14},{8,16},{10,18},{12,20},{14,22},{16,24},... | collective-permute-start | bytes 405512 | tf_op jit(solution)/shard_map/ppermute | solution.py:289
  16.0 15.5 %collective-permute-start.7 = (bf16[768,128]{1,0:T(8,128)(2,1)S(1)}, bf16[768,128]{1,0:T(8,128)(2,1)S(1)}, u32[]{:S(2)}, u32[]{:S(2)}) collective-permute-start(bf16[768,128]{1,0:T(8,128)(2,1)S(1)} %get-tuple-element.34), channel_id=1, source_target_pairs={{0,8},{2,10},{4,12},{6,14},{8,16},{10,18},{12,20},{14,22},{16,24},... | collective-permute-start | bytes 589832 | tf_op jit(solution)/shard_map/ppermute | solution.py:289
  25.5 17.2 %collective-permute-start.10 = (bf16[1088,128]{1,0:T(8,128)(2,1)S(1)}, bf16[1088,128]{1,0:T(8,128)(2,1)S(1)}, u32[]{:S(2)}, u32[]{:S(2)}) collective-permute-start(bf16[1088,128]{1,0:T(8,128)(2,1)S(1)} %shard_map.41), channel_id=1, source_target_pairs={{8,16},{10,18},{12,20},{14,22},{16,24},{18,26},{20,28},{22,30},{9,... | collective-permute-start | bytes 835592 | tf_op jit(solution)/shard_map/ppermute | solution.py:289
  28.0 7.0 %collective-permute-start = (bf16[128,1024]{1,0:T(8,128)(2,1)S(1)}, bf16[128,1024]{1,0:T(8,128)(2,1)S(1)}, u32[]{:S(2)}, u32[]{:S(2)}) collective-permute-start(bf16[128,1024]{1,0:T(8,128)(2,1)S(1)} %get-tuple-element.27), channel_id=1, source_target_pairs={{0,2},{2,0},{4,6},{6,4},{8,10},{10,8},{12,14},{14,12},{16,18},{18,... | collective-permute-start | bytes 786440 | tf_op jit(solution)/shard_map/ppermute | solution.py:283
  29.4 9.8 %collective-permute-start.1 = (bf16[128,1024]{1,0:T(8,128)(2,1)S(1)}, bf16[128,1024]{1,0:T(8,128)(2,1)S(1)}, u32[]{:S(2)}, u32[]{:S(2)}) collective-permute-start(bf16[128,1024]{1,0:T(8,128)(2,1)S(1)} %get-tuple-element.28), channel_id=1, source_target_pairs={{0,4},{2,6},{4,0},{6,2},{8,12},{10,14},{12,8},{14,10},{16,20},{18,... | collective-permute-start | bytes 786440 | tf_op jit(solution)/shard_map/ppermute | solution.py:283
  30.1 9.1 %collective-permute-start.2 = (bf16[128,1024]{1,0:T(8,128)(2,1)S(1)}, bf16[128,1024]{1,0:T(8,128)(2,1)S(1)}, u32[]{:S(2)}, u32[]{:S(2)}) collective-permute-start(bf16[128,1024]{1,0:T(8,128)(2,1)S(1)} %get-tuple-element.29), channel_id=1, source_target_pairs={{0,6},{2,4},{4,2},{6,0},{8,14},{10,12},{12,10},{14,8},{16,22},{18,... | collective-permute-start | bytes 786440 | tf_op jit(solution)/shard_map/ppermute | solution.py:283
  31.6 13.7 %collective-permute-start.9 = (bf16[1024,128]{1,0:T(8,128)(2,1)S(1)}, bf16[1024,128]{1,0:T(8,128)(2,1)S(1)}, u32[]{:S(2)}, u32[]{:S(2)}) collective-permute-start(bf16[1024,128]{1,0:T(8,128)(2,1)S(1)} %shard_map.40), channel_id=1, source_target_pairs={{8,16},{10,18},{12,20},{14,22},{16,24},{18,26},{20,28},{22,30},{9,... | collective-permute-start | bytes 786440 | tf_op jit(solution)/shard_map/ppermute | solution.py:289
  44.8 10.3 %collective-permute-start.14 = (bf16[128,512]{1,0:T(8,128)(2,1)S(1)}, bf16[128,512]{1,0:T(8,128)(2,1)S(1)}, u32[]{:S(2)}, u32[]{:S(2)}) collective-permute-start(bf16[128,512]{1,0:T(8,128)(2,1)S(1)} %get-tuple-element.44), channel_id=1, source_target_pairs={{0,2},{2,0},{4,6},{6,4},{8,10},{10,8},{12,14},{14,12},{16,18},{18,... | collective-permute-start | bytes 393224 | tf_op jit(solution)/shard_map/ppermute | solution.py:283
  49.8 9.5 %collective-permute-start.11 = (bf16[128,512]{1,0:T(8,128)(2,1)S(1)}, bf16[128,512]{1,0:T(8,128)(2,1)S(1)}, u32[]{:S(2)}, u32[]{:S(2)}) collective-permute-start(bf16[128,512]{1,0:T(8,128)(2,1)S(1)} %get-tuple-element.37), channel_id=1, source_target_pairs={{0,2},{2,0},{4,6},{6,4},{8,10},{10,8},{12,14},{14,12},{16,18},{18,... | collective-permute-start | bytes 393224 | tf_op jit(solution)/shard_map/ppermute | solution.py:283
  51.5 6.4 %collective-permute-start.15 = (bf16[128,512]{1,0:T(8,128)(2,1)S(1)}, bf16[128,512]{1,0:T(8,128)(2,1)S(1)}, u32[]{:S(2)}, u32[]{:S(2)}) collective-permute-start(bf16[128,512]{1,0:T(8,128)(2,1)S(1)} %get-tuple-element.45), channel_id=1, source_target_pairs={{0,4},{2,6},{4,0},{6,2},{8,12},{10,14},{12,8},{14,10},{16,20},{18,... | collective-permute-start | bytes 393224 | tf_op jit(solution)/shard_map/ppermute | solution.py:283
  51.8 6.1 %collective-permute-start.16 = (bf16[128,512]{1,0:T(8,128)(2,1)S(1)}, bf16[128,512]{1,0:T(8,128)(2,1)S(1)}, u32[]{:S(2)}, u32[]{:S(2)}) collective-permute-start(bf16[128,512]{1,0:T(8,128)(2,1)S(1)} %get-tuple-element.46), channel_id=1, source_target_pairs={{0,6},{2,4},{4,2},{6,0},{8,14},{10,12},{12,10},{14,8},{16,22},{18,... | collective-permute-start | bytes 393224 | tf_op jit(solution)/shard_map/ppermute | solution.py:283
  53.3 6.4 %collective-permute-start.12 = (bf16[128,512]{1,0:T(8,128)(2,1)S(1)}, bf16[128,512]{1,0:T(8,128)(2,1)S(1)}, u32[]{:S(2)}, u32[]{:S(2)}) collective-permute-start(bf16[128,512]{1,0:T(8,128)(2,1)S(1)} %get-tuple-element.38), channel_id=1, source_target_pairs={{0,4},{2,6},{4,0},{6,2},{8,12},{10,14},{12,8},{14,10},{16,20},{18,... | collective-permute-start | bytes 393224 | tf_op jit(solution)/shard_map/ppermute | solution.py:283
  55.2 5.9 %collective-permute-start.13 = (bf16[128,512]{1,0:T(8,128)(2,1)S(1)}, bf16[128,512]{1,0:T(8,128)(2,1)S(1)}, u32[]{:S(2)}, u32[]{:S(2)}) collective-permute-start(bf16[128,512]{1,0:T(8,128)(2,1)S(1)} %get-tuple-element.39), channel_id=1, source_target_pairs={{0,6},{2,4},{4,2},{6,0},{8,14},{10,12},{12,10},{14,8},{16,22},{18,... | collective-permute-start | bytes 393224 | tf_op jit(solution)/shard_map/ppermute | solution.py:283
